TPU v7x, 128 devices: a whole 4x4x4 slice. The times are simulated.
128 devices in a mesh: graph: 128 (over z, y, x, core).
Axes of the slice: x: 4, y: 4, z: 4, core: 2. Of those that a mesh axis runs over, the one named last changes fastest.
Arguments:
- feats: bfloat16 [524288, 768], P('graph')
- w_one: float32 [768, 1024], replicated
- w_two: float32 [1024, 153], replicated
- send_idx: int32 [16384, 4], P('graph')
- send_count: int32 [16384], P('graph')
- edge_src: int32 [524288, 8], P('graph')
- edge_wt: float32 [524288, 8], P('graph')
- labels: int32 [524288], P('graph')
- label_mask: int32 [524288], P('graph')
Outputs:
- output 1: float32 [], replicated
- output 2: float32 [768, 1024], replicated
- output 3: float32 [1024, 153], replicated
All inputs are finite; a program needn't handle non-finite values.
Results may differ from a plain program's by a relative error of at most 0.001.
Values are sent between devices in bfloat16 or wider.
A program may use at most 1 GiB of HBM per device.

v0:
```python
import jax
import jax.numpy as jnp
from jax import lax
from jax.sharding import PartitionSpec as P


def solution(mesh):
    dev_count = mesh.shape["graph"]

    def device_step(feats, w_one, w_two, send_idx, send_count, edge_src, edge_wt, labels, label_mask):
        row_count = feats.shape[0]
        halo_rows = send_idx.shape[1]
        in_deg = edge_src.shape[1]
        list_ids = send_idx.reshape(dev_count * halo_rows)
        list_ok = (jnp.arange(halo_rows)[None, :] < send_count[:, None]).reshape(dev_count * halo_rows, 1)
        flat_src = edge_src.reshape(row_count * in_deg)
        w_one_b = w_one.astype(jnp.bfloat16)
        w_two_b = w_two.astype(jnp.bfloat16)

        def aggregate(h_rows):
            outgoing = jnp.where(list_ok, h_rows[list_ids], 0)
            incoming = lax.all_to_all(outgoing, "graph", 0, 0, tiled=True)
            ext_rows = jnp.concatenate([h_rows, incoming], axis=0)
            return jnp.sum(ext_rows[edge_src].astype(jnp.float32) * edge_wt[:, :, None], axis=1)

        z_one = aggregate(feats).astype(jnp.bfloat16)
        h_one = jnp.maximum(jnp.dot(z_one, w_one_b, preferred_element_type=jnp.float32), 0.0).astype(jnp.bfloat16)
        z_two = aggregate(h_one).astype(jnp.bfloat16)
        logits = jnp.dot(z_two, w_two_b, preferred_element_type=jnp.float32)
        mask_f = label_mask.astype(jnp.float32)
        label_total = lax.psum(jnp.sum(mask_f), "graph")
        log_prob = jax.nn.log_softmax(logits, axis=-1)
        onehot = (labels[:, None] == jnp.arange(logits.shape[1])[None, :]).astype(jnp.float32)
        loss_val = -lax.psum(jnp.sum(mask_f[:, None] * onehot * log_prob), "graph") / label_total
        d_logits = ((jnp.exp(log_prob) - onehot) * (mask_f / label_total)[:, None]).astype(jnp.bfloat16)
        grad_two = lax.psum(jnp.einsum("nf,nc->fc", z_two, d_logits, preferred_element_type=jnp.float32), "graph")
        d_z2 = jnp.einsum("nc,fc->nf", d_logits, w_two_b, preferred_element_type=jnp.float32)
        contrib = (edge_wt[:, :, None] * d_z2[:, None, :]).reshape(row_count * in_deg, d_z2.shape[1])
        ext_grad = jax.ops.segment_sum(contrib, flat_src, num_segments=row_count + dev_count * halo_rows)
        returned = lax.all_to_all(ext_grad[row_count:], "graph", 0, 0, tiled=True)
        d_h1 = ext_grad[:row_count] + jax.ops.segment_sum(jnp.where(list_ok, returned, 0.0), list_ids, num_segments=row_count)
        d_y1 = jnp.where(h_one > 0, d_h1, 0.0).astype(jnp.bfloat16)
        grad_one = lax.psum(jnp.einsum("nf,nh->fh", z_one, d_y1, preferred_element_type=jnp.float32), "graph")
        return loss_val, grad_one, grad_two

    row_spec = P("graph", None)
    vec_spec = P("graph")
    return jax.shard_map(device_step, mesh=mesh, in_specs=(row_spec, P(), P(), row_spec, vec_spec, row_spec, row_spec, vec_spec, vec_spec), out_specs=(P(), P(), P()), check_vma=False)
```

profile of v0, /device:TPU:1, one launch (start us, length us, event | category | flops | bytes accessed | tf_op | source)
XLA Modules:
  0.0 1119.9 jit_solution(2202340999457523535)
XLA Ops:
  9.2 6.0 gather_fusion
  16.9 12.3 %all-to-all-start = ((bf16[128,4,768]{2,1,0:T(4,128)(2,1)}), bf16[128,4,768]{2,1,0:T(4,128)(2,1)}, u32[]{:S(2)}, u32[]{:S(2)}) async-start(bf16[128,4,768]{2,1,0:T(4,128)(2,1)} %broadcast_select_fusion.1), calls=%async_computation | async-start | bytes 1572864 | tf_op jit(solution)/shard_map/all_to_all | solution.py:22
  31.5 13.4 %all-to-all-done = bf16[128,4,768]{2,1,0:T(4,128)(2,1)} async-done(((bf16[128,4,768]{2,1,0:T(4,128)(2,1)}), bf16[128,4,768]{2,1,0:T(4,128)(2,1)}, u32[]{:S(2)}, u32[]{:S(2)}) %all-to-all-start) | async-done | bytes 786464 | tf_op jit(solution)/shard_map/all_to_all | solution.py:22
  46.5 6.1 pad_maximum_fusion.1
  52.6 149.6 %gather_fusion.1 = bf16[32768,768]{1,0:T(8,128)(2,1)} fusion(bf16[4608,768]{1,0:T(8,128)(2,1)} %pad_maximum_fusion.1, s32[32768]{0:T(1024)S(1)} %broadcast_clamp_fusion), kind=kCustom, calls=%fused_computation.1 | custom fusion | bytes 100794368 | tf_op jit(solution)/shard_map/gather | solution.py:24
  202.2 37.8 %fusion.2 = bf16[4096,768]{1,0:T(8,128)(2,1)} fusion(bf16[32768,768]{1,0:T(8,128)(2,1)} %gather_fusion.1, f32[4096,8]{1,0:T(8,128)S(1)} %copy.16), kind=kLoop, calls=%fused_computation.11 | loop fusion | flops 72351744 | bytes 56754176 | tf_op jit(solution)/shard_map/reduce_sum | solution.py:24
  240.1 12.3 %maximum_convert_fusion = bf16[4096,1024]{1,0:T(8,128)(2,1)} fusion(bf16[4096,768]{1,0:T(8,128)(2,1)} %fusion.2, f32[768,1024]{1,0:T(8,128)} %param.10), kind=kOutput, calls=%fused_computation.15 | convolution fusion | flops 6451625984 | bytes 17825792 | tf_op jit(solution)/shard_map/dot_general | solution.py:27
  252.3 7.2 gather_fusion.2
  263.5 4.9 all-to-all-start.1
  273.2 14.1 %all-to-all-done.1 = bf16[128,4,1024]{2,1,0:T(4,128)(2,1)S(1)} async-done(((bf16[128,4,1024]{2,1,0:T(4,128)(2,1)}), bf16[128,4,1024]{2,1,0:T(4,128)(2,1)S(1)}, u32[]{:S(2)}, u32[]{:S(2)}) %all-to-all-start.1) | async-done | bytes 1048608 | tf_op jit(solution)/shard_map/all_to_all | solution.py:22
  287.6 12.2 %pad_maximum_fusion = bf16[4608,1024]{1,0:T(8,128)(2,1)} fusion(bf16[512,1024]{1,0:T(8,128)(2,1)S(1)} %all_to_all.23, bf16[4096,1024]{1,0:T(8,128)(2,1)} %maximum_convert_fusion), kind=kLoop, calls=%fused_computation.16 | loop fusion | flops 18874368 | bytes 18874368 | tf_op jit(solution)/shard_map/concatenate | solution.py:23
  299.8 164.4 %gather_fusion.3 = bf16[32768,1024]{1,0:T(8,128)(2,1)} fusion(bf16[4608,1024]{1,0:T(8,128)(2,1)} %pad_maximum_fusion, s32[32768]{0:T(1024)S(1)} %broadcast_clamp_fusion), kind=kCustom, calls=%fused_computation.3 | custom fusion | bytes 134348800 | tf_op jit(solution)/shard_map/gather | solution.py:24
  464.2 49.9 %fusion = bf16[4096,1024]{1,0:T(8,128)(2,1)S(1)} fusion(bf16[32768,1024]{1,0:T(8,128)(2,1)} %gather_fusion.3, f32[4096,8]{1,0:T(8,128)S(1)} %copy-done.2), kind=kLoop, calls=%fused_computation.7 | loop fusion | flops 96468992 | bytes 75628544 | tf_op jit(solution)/shard_map/reduce_sum | solution.py:24
  522.8 62.5 %all-reduce = (f32[]{:T(128)}, f32[]{:T(128)}) all-reduce(f32[]{:T(128)} %multiply_reduce_fusion, f32[]{:T(128)} %convert_reduce_fusion), channel_id=1, replica_groups=mesh['graph'=128] {'graph'}, use_global_device_ids=true, to_apply=%region_5.6 | all-reduce | flops 2 | bytes 16 | tf_op jit(solution)/shard_map/psum | solution.py:34
  585.9 8.2 fusion.20
  594.1 287.0 %scatter_custom_fusion = f32[4608,1024]{1,0:T(8,128)} fusion(s32[32768]{0:T(1024)} %reshape.119, f32[4096,1024]{1,0:T(8,128)} %fusion.20, f32[32768]{0:T(1024)S(1)} %copy-done.7, f32[]{:T(128)} %constant.6.clone.1), kind=kCustom, calls=%fused_computation.9 | custom fusion | flops 67108864 | bytes 35783168 | tf_op jit(solution)/shard_map/scatter-add | solution.py:39
  887.2 5.6 all-to-all-start.2
  893.1 12.0 %slice.16 = f32[4096,1024]{1,0:T(8,128)} slice(f32[4608,1024]{1,0:T(8,128)} %scatter_custom_fusion), slice={[0:4096], [0:1024]} | slice | bytes 33554432 | tf_op jit(solution)/shard_map/slice | solution.py:41
  905.1 5.8 fusion.9
  910.9 12.5 %all-to-all-done.2 = f32[128,4,1024]{2,1,0:T(4,128)} async-done(((f32[128,4,1024]{2,1,0:T(4,128)}), f32[128,4,1024]{2,1,0:T(4,128)}, u32[]{:S(2)}, u32[]{:S(2)}) %all-to-all-start.2) | async-done | bytes 2097184 | tf_op jit(solution)/shard_map/all_to_all | solution.py:40
  925.4 16.3 %scatter_custom_fusion.1 = f32[4096,1024]{1,0:T(8,128)} fusion(f32[4096,1024]{1,0:T(8,128)} %slice.16, s32[512]{0:T(512)S(1)} %reshape.127, f32[512,1024]{1,0:T(8,128)S(1)} %all_to_all.26, f32[]{:T(128)} %constant.6.clone.1, pred[512]{0:T(512)(128)(4,1)S(1)} %lt.41), kind=kCustom, calls=%fused_computation.32 | custom fusion | flops 1048576 | bytes 18875392 | tf_op jit(solution)/shard_map/scatter-add | solution.py:41
  941.8 14.5 %fusion.6 = f32[768,1024]{1,0:T(8,128)} fusion(f32[4096,1024]{1,0:T(8,128)} %scatter_custom_fusion.1, bf16[4096,1024]{1,0:T(8,128)(2,1)} %maximum_convert_fusion, bf16[4096,768]{1,0:T(8,128)(2,1)} %fusion.2), kind=kOutput, calls=%fused_computation.18 | convolution fusion | flops 6459228160 | bytes 34603008 | tf_op jit(solution)/shard_map/nf,nh->fh/dot_general | solution.py:43
  957.6 149.2 %all-reduce.4.cloned.1.call-done = (f32[768,1024]{1,0:T(8,128)}, f32[1024,153]{0,1:T(8,128)}) async-done(((f32[768,1024]{1,0:T(8,128)}, f32[1024,153]{0,1:T(8,128)}), (f32[768,1024]{1,0:T(8,128)}, f32[1024,153]{0,1:T(8,128)})) %all-reduce.4.cloned.1.call-update) | async-done | bytes 3772432 | tf_op jit(solution)/shard_map/psum | solution.py:43
  1106.8 4.0 copy.24
  (76 shorter events, 35.0 us)
Async XLA Ops:
  7.2 8.3 copy-start.20
  7.2 22.0 %copy-start.8 = (s32[4096,8]{0,1:T(8,128)S(1)}, s32[4096,8]{0,1:T(8,128)}, u32[]{:S(2)}) copy-start(s32[4096,8]{0,1:T(8,128)} %param.14) | copy-start | bytes 393220
  8.0 0.6 copy-start.5
  15.2 15.6 %copy-start.16 = (f32[4096,8]{0,1:T(8,128)S(1)}, f32[4096,8]{0,1:T(8,128)}, u32[]{:S(2)}) copy-start(f32[4096,8]{0,1:T(8,128)} %param.15) | copy-start | bytes 393220
  15.5 13.6 %copy-start.10 = (pred[128,4]{1,0:T(8,128)(4,1)}, pred[128,4]{1,0:T(8,128)(4,1)S(1)}, u32[]{:S(2)}) copy-start(pred[128,4]{1,0:T(8,128)(4,1)S(1)} %iota_compare_fusion.1) | copy-start | bytes 1540
  16.9 28.0 %all-to-all-start = ((bf16[128,4,768]{2,1,0:T(4,128)(2,1)}), bf16[128,4,768]{2,1,0:T(4,128)(2,1)}, u32[]{:S(2)}, u32[]{:S(2)}) async-start(bf16[128,4,768]{2,1,0:T(4,128)(2,1)} %broadcast_select_fusion.1), calls=%async_computation | async-start | bytes 1572864 | tf_op jit(solution)/shard_map/all_to_all | solution.py:22
  31.5 236.9 %copy-start.1 = (f32[4096,8]{1,0:T(8,128)}, f32[4096,8]{1,0:T(8,128)S(1)}, u32[]{:S(2)}) copy-start(f32[4096,8]{1,0:T(8,128)S(1)} %copy.16) | copy-start | bytes 393220
  240.1 12.3 %copy-start.19 = (s32[1024]{0:T(1024)S(1)}, s32[1024]{0:T(1024)}, u32[]{:S(2)}) copy-start(s32[1024]{0:T(1024)} %copy-done.18) | copy-start | bytes 12292
  252.3 8.5 copy-start.11
  259.5 10.5 copy-start.9
  259.5 12.5 %copy-start.14 = (s32[4096]{0:T(1024)S(1)}, s32[4096]{0:T(1024)}, u32[]{:S(2)}) copy-start(s32[4096]{0:T(1024)} %param.17) | copy-start | bytes 49156
  263.5 23.8 %all-to-all-start.1 = ((bf16[128,4,1024]{2,1,0:T(4,128)(2,1)}), bf16[128,4,1024]{2,1,0:T(4,128)(2,1)S(1)}, u32[]{:S(2)}, u32[]{:S(2)}) async-start(bf16[128,4,1024]{2,1,0:T(4,128)(2,1)} %broadcast_select_fusion), calls=%async_computation.1 | async-start | bytes 2097152 | tf_op jit(solution)/shard_map/all_to_all | solution.py:22
  299.8 164.4 %copy-start.2 = (f32[4096,8]{1,0:T(8,128)S(1)}, f32[4096,8]{1,0:T(8,128)}, u32[]{:S(2)}) copy-start(f32[4096,8]{1,0:T(8,128)} %copy-done.1) | copy-start | bytes 393220
  464.2 49.9 %copy-start.3 = (f32[1024,153]{0,1:T(8,128)S(1)}, f32[1024,153]{0,1:T(8,128)}, u32[]{:S(2)}) copy-start(f32[1024,153]{0,1:T(8,128)} %param.11) | copy-start | bytes 1880068
  514.1 3.3 copy-start
  514.1 3.7 copy-start.13
  514.2 3.7 copy-start.17
  517.4 67.8 %copy-start.15 = (s32[4096]{0:T(1024)S(1)}, s32[4096]{0:T(1024)}, u32[]{:S(2)}) copy-start(s32[4096]{0:T(1024)} %param.17) | copy-start | bytes 49156
  585.9 8.2 copy-start.7
  881.1 11.7 %copy-start.12 = (pred[128,4]{1,0:T(8,128)(4,1)S(1)}, pred[128,4]{1,0:T(8,128)(4,1)}, u32[]{:S(2)}) copy-start(pred[128,4]{1,0:T(8,128)(4,1)} %copy-done.10) | copy-start | bytes 1540
  881.1 11.9 %copy-start.6 = (s32[128,4]{1,0:T(8,128)S(1)}, s32[128,4]{1,0:T(8,128)}, u32[]{:S(2)}) copy-start(s32[128,4]{1,0:T(8,128)} %copy-done.5) | copy-start | bytes 6148
  887.2 36.3 %all-to-all-start.2 = ((f32[128,4,1024]{2,1,0:T(4,128)}), f32[128,4,1024]{2,1,0:T(4,128)}, u32[]{:S(2)}, u32[]{:S(2)}) async-start(f32[128,4,1024]{2,1,0:T(4,128)} %all_to_all.24), calls=%async_computation.2 | async-start | bytes 4194304 | tf_op jit(solution)/shard_map/all_to_all | solution.py:40
  892.8 214.1 %all-reduce.4.cloned.1.call-start = ((), (), s32[]{:S(2)}) async-start(), calls=%async_computation.3 | async-start | bytes 7602176 | tf_op jit(solution)/shard_map/psum | solution.py:43
  1106.8 4.0 copy-start.4
  (1 other events, 0.6 us)
Sparse Core Ops, SparseCore 0:
  956.4 150.3 all-reduce.3
where the time goes:
time: 1120 us
  other arithmetic  417 us (37%)
  local copies, waits for them, and re-layouts  367 us (33%)
  waiting for transfers between devices  189 us (17%)
  blocking collectives  62.5 us (6%)
  matrix products  43.7 us (4%)
  starting transfers between devices  22.8 us (2%)
  between operations  17.1 us (2%)
    gather x2, local copies, waits for them, and re-layouts, aggregate(): ext_rows[edge_src].astype(jnp.float32) * edge_wt[:, :, None]  314 us
    scatter-add x1, other arithmetic, device_step(): jax.ops.segment_sum(contrib, flat_src, num_segments=row_count + dev_count...  287 us
    psum x1, waiting for transfers between devices, device_step(): lax.psum(jnp.einsum('nf,nh->fh', z_one, d_y1, preferred_element_type=jnp....  149 us
    reduce_sum x2, other arithmetic, aggregate(): jnp.sum(ext_rows[edge_src].astype(jnp.float32) * edge_wt[:, :, None], axi...  87.7 us
    psum x1, blocking collectives, device_step(): lax.psum(jnp.sum(mask_f[:, None] * onehot * log_prob), 'graph')  62.5 us
    all_to_all x2, waiting for transfers between devices, aggregate(): incoming = lax.all_to_all(outgoing, 'graph', 0, 0, tiled=True)  27.5 us
  transfers between devices with their start and end apart: 4, of which 4 were waited for; matrix products, arithmetic and copies ran while one was open for 2% of the time, Pallas kernels for 0%

commit v1 on v0

v1 whole, which is shorter than its diff:
```python
import functools

import jax
import jax.numpy as jnp
from jax import lax
from jax.experimental import pallas as pl
from jax.experimental.pallas import tpu as pltpu
from jax.sharding import PartitionSpec as P

LANES = 128
STEP = 16
BLOCK = 256
F32, BF16 = jnp.float32, jnp.bfloat16


def once(shape):
    return pl.BlockSpec(shape, lambda g: (0,) * len(shape), pipeline_mode=pl.Buffered(1))


def fill_rows(dst, src, offset, blocks):
    def step(i, carry):
        r = pl.multiple_of(i * 64, 64)
        x = src[pl.ds(r, 64), :].astype(F32)
        for c in range(blocks):
            dst[pl.ds((r + offset) * 8 + c, 64, stride=8), :] = x[:, c * LANES : (c + 1) * LANES]
        return carry

    lax.fori_loop(0, src.shape[0] // 64, step, 0)


def spread_weights(w, deg):
    return tuple(jnp.broadcast_to(w[h * 8 : h * 8 + 8, k : k + 1], (8, LANES)) for h in range(STEP // 8) for k in range(deg))


def gather_rows(first_step, steps, src, wt, table, out, wbuf):
    deg = wt.shape[1]

    def weights_at(i):
        return spread_weights(wt[pl.ds(pl.multiple_of(i * STEP, STEP), STEP), :], deg)

    def step(i, tiles):
        for t, tile in enumerate(tiles):
            wbuf[pl.ds(t * 8, 8), :] = tile
        ahead = weights_at(jnp.minimum(i + 1, steps - 1))
        dst = out.at[pl.ds(pl.multiple_of(i * STEP * 8, STEP * 8), STEP * 8)]
        for u in range(STEP):
            acc = None
            for k in range(deg):
                row = table[pl.ds(pl.multiple_of(src[u * deg + k, first_step + i], 8), 8), :]
                term = row * wbuf[pl.ds((u // 8 * deg + k) * 8 + u % 8, 8, stride=0), :]
                acc = term if acc is None else acc + term
            dst[pl.ds(u * 8, 8), :] = acc
        return ahead

    lax.fori_loop(0, steps, step, weights_at(0))


def layer_one_kernel(src, wt, own, halo, w, z_out, h_out, table, zbuf, wbuf):
    g = pl.program_id(0)
    rows, blocks = z_out.shape[0], own.shape[1] // LANES

    @pl.when(g == 0)
    def _():
        fill_rows(table, own, 0, blocks)
        fill_rows(table, halo, own.shape[0], blocks)

    steps = rows // STEP
    gather_rows(g * steps, steps, src, wt, table, zbuf, wbuf)
    z = jnp.concatenate([zbuf[pl.ds(c, rows, stride=8), :] for c in range(blocks)], axis=1).astype(BF16)
    z_out[...] = z
    y = jnp.dot(z, w[...], preferred_element_type=F32)
    h_out[...] = jnp.maximum(y, 0.0).astype(BF16)


def layer_two_kernel(classes, src, inv_total, wt, own, halo, w, label, g_out, gw_out, loss_out, table, zbuf, wbuf):
    g = pl.program_id(0)
    rows, blocks = g_out.shape[0], own.shape[1] // LANES

    @pl.when(g == 0)
    def _():
        fill_rows(table, own, 0, blocks)
        fill_rows(table, halo, own.shape[0], blocks)
        gw_out[...] = jnp.zeros_like(gw_out)
        loss_out[...] = jnp.zeros_like(loss_out)

    steps = rows // STEP
    gather_rows(g * steps, steps, src, wt, table, zbuf, wbuf)
    z = jnp.concatenate([zbuf[pl.ds(c, rows, stride=8), :] for c in range(blocks)], axis=1).astype(BF16)
    logits = jnp.dot(z, w[...], preferred_element_type=F32)
    col = lax.broadcasted_iota(jnp.int32, logits.shape, 1)
    real = col < classes
    top = jnp.max(jnp.where(real, logits, -jnp.inf), axis=1, keepdims=True)
    shifted = logits - top
    log_sum = jnp.log(jnp.sum(jnp.where(real, jnp.exp(shifted), 0.0), axis=1, keepdims=True))
    log_prob = shifted - log_sum
    tag = label[...]
    hit = col == tag
    loss_out[...] += jnp.sum(jnp.where(hit, log_prob, 0.0), axis=(0, 1), keepdims=True)
    scale = jnp.where(tag >= 0, inv_total[0], 0.0)
    grad = jnp.where(real, (jnp.exp(log_prob) - jnp.where(hit, 1.0, 0.0)) * scale, 0.0).astype(BF16)
    g_out[...] = grad
    gw_out[...] += lax.dot_general(grad, z, (((0,), (0,)), ((), ())), preferred_element_type=F32)


def scatter_kernel(src, wt, grad, s_out, gbuf, wbuf, *parts):
    g = pl.program_id(0)
    rows, deg = grad.shape[0], wt.shape[1]
    steps = rows // STEP

    @pl.when(g == 0)
    def _():
        def clear(i, carry):
            for part in parts:
                for j in range(8):
                    part[pl.ds(pl.multiple_of(i * 64, 64) + j * 8, 8), :] = jnp.zeros((8, LANES), F32)
            return carry

        lax.fori_loop(0, s_out.shape[0] // 64, clear, 0)

    x = grad[...].astype(F32)
    for c in range(2):
        gbuf[pl.ds(c, rows, stride=2), :] = x[:, c * LANES : (c + 1) * LANES]

    def weights_at(i):
        return spread_weights(wt[pl.ds(pl.multiple_of(i * STEP, STEP), STEP), :], deg)

    def step(i, tiles):
        for t, tile in enumerate(tiles):
            wbuf[pl.ds(t * 8, 8), :] = tile
        ahead = weights_at(jnp.minimum(i + 1, steps - 1))
        here = gbuf.at[pl.ds(pl.multiple_of(i * STEP * 2, STEP * 2), STEP * 2)]
        for u in range(STEP):
            row = here[pl.ds(u * 2, 2), :]
            for k in range(deg):
                at = pl.ds(pl.multiple_of(src[u * deg + k, g * steps + i], 2), 2)
                w = wbuf[pl.ds((u // 8 * deg + k) * 8 + u % 8, 2, stride=0), :]
                parts[k][at, :] = parts[k][at, :] + row * w
        return ahead

    lax.fori_loop(0, steps, step, weights_at(0))

    @pl.when(g == pl.num_programs(0) - 1)
    def _():
        def add(i, carry):
            at = pl.ds(pl.multiple_of(i * 64, 64), 64)
            total = parts[0][at, :]
            for part in parts[1:]:
                total = total + part[at, :]
            s_out[at, :] = total
            return carry

        lax.fori_loop(0, s_out.shape[0] // 64, add, 0)


def backward_kernel(lists, own, back, w_t, h, z, gw_out, total):
    g = pl.program_id(0)
    rows = h.shape[0]

    @pl.when(g == 0)
    def _():
        gw_out[...] = jnp.zeros_like(gw_out)

        def copy(i, carry):
            at = pl.ds(pl.multiple_of(i * 64, 64), 64)
            total[at, :] = own[at, :]
            return carry

        lax.fori_loop(0, own.shape[0] // 64, copy, 0)

        def add(i, carry):
            for j in range(4):
                at = pl.ds(pl.multiple_of(lists[i * 4 + j], 2), 2)
                total[at, :] = total[at, :] + back[pl.ds(pl.multiple_of(i * 8, 8) + j * 2, 2), :]
            return carry

        lax.fori_loop(0, back.shape[0] // 8, add, 0)

    s = jnp.concatenate([total[pl.ds(g * rows * 2 + c, rows, stride=2), :] for c in range(2)], axis=1)
    high = s.astype(BF16)
    rest = s - high.astype(F32)
    mid = rest.astype(BF16)
    low = (rest - mid.astype(F32)).astype(BF16)
    wt = w_t[...]
    d = jnp.dot(low, wt, preferred_element_type=F32)
    d = d + jnp.dot(mid, wt, preferred_element_type=F32)
    d = d + jnp.dot(high, wt, preferred_element_type=F32)
    grad = jnp.where(h[...] > 0, d, 0.0).astype(BF16)
    gw_out[...] += lax.dot_general(z[...], grad, (((0,), (0,)), ((), ())), preferred_element_type=F32)


def params():
    return pltpu.CompilerParams(dimension_semantics=("arbitrary",), vmem_limit_bytes=62 * 2**20)


SMEM = pl.BlockSpec(memory_space=pltpu.SMEM)


def solution(mesh):
    dev_count = mesh.shape["graph"]

    def device_step(feats, w_one, w_two, send_idx, send_count, edge_src, edge_wt, labels, label_mask):
        n, f_in = feats.shape
        f_hid, classes = w_two.shape
        halo_rows, deg = send_idx.shape[1], edge_src.shape[1]
        halo = dev_count * halo_rows
        ext = n + halo
        pad = 2 * LANES
        w_one_b = w_one.astype(BF16)
        w_two_b = jnp.pad(w_two.astype(BF16), ((0, 0), (0, pad - classes)))
        list_ids = send_idx.reshape(halo)
        list_ok = jnp.arange(halo_rows)[None, :] < send_count[:, None]
        src_t = edge_src.reshape(n // STEP, STEP * deg).T
        src8, src2 = src_t * 8, src_t * 2
        lists2 = jnp.where(list_ok, send_idx, n).reshape(halo) * 2
        label = jnp.where(label_mask == 1, labels, -1).reshape(n, 1)
        label_total = lax.psum(jnp.sum(label_mask.astype(F32)), "graph")
        inv_total = (1.0 / label_total).reshape(1)
        ok_rows = list_ok.reshape(halo, 1)

        def exchange(h_rows):
            outgoing = jnp.where(ok_rows, h_rows[list_ids], 0)
            return lax.all_to_all(outgoing, "graph", 0, 0, tiled=True)

        def by_rows(width):
            return pl.BlockSpec((BLOCK, width), lambda g: (g, 0))

        gather_scratch = [
            pltpu.VMEM((ext * 8, LANES), F32),
            pltpu.VMEM((BLOCK * 8, LANES), F32),
            pltpu.VMEM((STEP * deg + 8, LANES), F32),
        ]
        z_one, h_one = pl.pallas_call(
            layer_one_kernel,
            grid=(n // BLOCK,),
            in_specs=[SMEM, by_rows(deg), once((n, f_in)), once((halo, f_in)), once((f_in, f_hid))],
            out_specs=[by_rows(f_in), by_rows(f_hid)],
            out_shape=[jax.ShapeDtypeStruct((n, f_in), BF16), jax.ShapeDtypeStruct((n, f_hid), BF16)],
            scratch_shapes=gather_scratch,
            compiler_params=params(),
            name="layer_one",
        )(src8, edge_wt, feats, exchange(feats), w_one_b)
        grad_log, gw_two, loss_sum = pl.pallas_call(
            functools.partial(layer_two_kernel, classes),
            grid=(n // BLOCK,),
            in_specs=[SMEM, SMEM, by_rows(deg), once((n, f_hid)), once((halo, f_hid)), once((f_hid, pad)), by_rows(1)],
            out_specs=[by_rows(pad), once((pad, f_hid)), once((1, 1))],
            out_shape=[
                jax.ShapeDtypeStruct((n, pad), BF16),
                jax.ShapeDtypeStruct((pad, f_hid), F32),
                jax.ShapeDtypeStruct((1, 1), F32),
            ],
            scratch_shapes=gather_scratch,
            compiler_params=params(),
            name="layer_two",
        )(src8, inv_total, edge_wt, h_one, exchange(h_one), w_two_b, label)
        ext_grad = pl.pallas_call(
            scatter_kernel,
            grid=(n // 512,),
            in_specs=[SMEM, pl.BlockSpec((512, deg), lambda g: (g, 0)), pl.BlockSpec((512, pad), lambda g: (g, 0))],
            out_specs=once((ext * 2, LANES)),
            out_shape=jax.ShapeDtypeStruct((ext * 2, LANES), F32),
            scratch_shapes=[pltpu.VMEM((512 * 2, LANES), F32), pltpu.VMEM((STEP * deg + 8, LANES), F32)]
            + [pltpu.VMEM((ext * 2, LANES), F32) for _ in range(deg)],
            compiler_params=params(),
            name="scatter",
        )(src2, edge_wt, grad_log)
        back = lax.all_to_all(ext_grad[n * 2 :], "graph", 0, 0, tiled=True)
        gw_one = pl.pallas_call(
            backward_kernel,
            grid=(n // 512,),
            in_specs=[
                SMEM,
                once((n * 2, LANES)),
                once((halo * 2, LANES)),
                once((pad, f_hid)),
                pl.BlockSpec((512, f_hid), lambda g: (g, 0)),
                pl.BlockSpec((512, f_in), lambda g: (g, 0)),
            ],
            out_specs=once((f_in, f_hid)),
            out_shape=jax.ShapeDtypeStruct((f_in, f_hid), F32),
            scratch_shapes=[pltpu.VMEM((n * 2 + 8, LANES), F32)],
            compiler_params=params(),
            name="backward",
        )(lists2, ext_grad, back, w_two_b.T, h_one, z_one)
        loss_sum, gw_one, gw_two = lax.psum((loss_sum[0, 0], gw_one, gw_two[:classes].T), "graph")
        return -loss_sum / label_total, gw_one, gw_two

    row_spec = P("graph", None)
    vec_spec = P("graph")
    return jax.shard_map(
        device_step,
        mesh=mesh,
        in_specs=(row_spec, P(), P(), row_spec, vec_spec, row_spec, row_spec, vec_spec, vec_spec),
        out_specs=(P(), P(), P()),
        check_vma=False,
    )
```

time: 1120 us -> 516 us (0.46)
  other arithmetic: 417 us -> 7.54 us
  local copies, waits for them, and re-layouts: 367 us -> 41.2 us
  Pallas kernels: 0 us -> 190 us
  waiting for transfers between devices: 189 us -> 105 us
  blocking collectives: 62.5 us -> 133 us
  matrix products: 43.7 us -> 0 us
    gather x6 -> x4, local copies, waits for them, and re-layouts: 329 us -> 13.8 us  [exchange(): outgoing = jnp.where(ok_rows, h_rows[list_ids], 0)]
    scatter-add x2 -> x0, other arithmetic: 303 us -> none  [the longest x1 287 us: device_step(): jax.ops.segment_sum(contrib, flat_src, num_segments=row_count + dev_count...]
    pallas_call x0 -> x4, Pallas kernels: none -> 190 us  [the longest x1 65.7 us: device_step(): pl.pallas_call(functools.partial(layer_two_kernel, classes), grid=(n // B...]
    reduce_sum x5 -> x1, other arithmetic: 90.2 us -> 0.6 us  [device_step(): label_total = lax.psum(jnp.sum(label_mask.astype(F32)), 'graph')]
    psum x1 -> x2, blocking collectives: 62.5 us -> 133 us  [the longest x1 69.6 us: device_step(): label_total = lax.psum(jnp.sum(label_mask.astype(F32)), 'graph')]
    psum x1, waiting for transfers between devices: 149 us -> 86.1 us  [device_step(): lax.psum((loss_sum[0, 0], gw_one, gw_two[:classes].T), 'graph')]
    dot_general x5 -> x0, matrix products: 43.7 us -> none  [the longest x1 14.5 us: device_step(): jnp.einsum('nf,nh->fh', z_one, d_y1, preferred_element_type=jnp.float32)]
    all_to_all x3, waiting for transfers between devices: 40.1 us -> 18.7 us  [the longest x1 10.8 us: device_step(): back = lax.all_to_all(ext_grad[n * 2:], 'graph', 0, 0, tiled=True)]
  transfers between devices with their start and end apart: 4 -> 4, of which waited for: 4 -> 3; matrix products, arithmetic and copies ran while one was open for 2% -> 4% of each run, Pallas kernels for 0% -> 0%
where the time goes in v1:
time: 516 us; the launch traced here: 515 us
  Pallas kernels  190 us (37%)
  blocking collectives  133 us (26%)
  waiting for transfers between devices  105 us (20%)
  local copies, waits for them, and re-layouts  41.2 us (8%)
  starting transfers between devices  22.1 us (4%)
  between operations  17.4 us (3%)
  other arithmetic  7.54 us (1%)
    psum x1, waiting for transfers between devices, device_step(): lax.psum((loss_sum[0, 0], gw_one, gw_two[:classes].T), 'graph')  86.1 us
    psum x1, blocking collectives, device_step(): label_total = lax.psum(jnp.sum(label_mask.astype(F32)), 'graph')  69.6 us
    pallas_call x1, Pallas kernels, device_step(): pl.pallas_call(functools.partial(layer_two_kernel, classes), grid=(n // B...  65.7 us
    psum x1, blocking collectives, device_step(): lax.psum((loss_sum[0, 0], gw_one, gw_two[:classes].T), 'graph')  63 us
    pallas_call x1, Pallas kernels, device_step(): pl.pallas_call(layer_one_kernel, grid=(n // BLOCK,), in_specs=[SMEM, by_r...  57.3 us
    pallas_call x1, Pallas kernels, device_step(): pl.pallas_call(scatter_kernel, grid=(n // 512,), in_specs=[SMEM, pl.Block...  42.1 us
    pallas_call x1, Pallas kernels, device_step(): pl.pallas_call(backward_kernel, grid=(n // 512,), in_specs=[SMEM, once((n...  24.5 us
    all_to_all x2, starting transfers between devices, exchange(): return lax.all_to_all(outgoing, 'graph', 0, 0, tiled=True)  16 us
  transfers between devices with their start and end apart: 4, of which 3 were waited for; matrix products, arithmetic and copies ran while one was open for 4% of the time, Pallas kernels for 0%

profile of v1, /device:TPU:1, one launch (start us, length us, event | category | flops | bytes accessed | tf_op | source)
XLA Modules:
  0.0 515.2 jit_solution(9850326937469167445)
XLA Ops:
  8.1 6.0 %gather_fusion = bf16[512,768]{1,0:T(8,128)(2,1)S(1)} fusion(bf16[4096,768]{1,0:T(8,128)(2,1)} %own.1, s32[1024]{0:T(1024)S(1)} %pad_clamp_fusion), kind=kCustom, calls=%fused_computation | custom fusion | bytes 1574912 | tf_op jit(solution)/shard_map/gather | solution.py:221
  15.8 11.5 %all-to-all-start = ((bf16[128,4,768]{2,1,0:T(4,128)(2,1)}), bf16[128,4,768]{2,1,0:T(4,128)(2,1)S(1)}, u32[]{:S(2)}, u32[]{:S(2)}) async-start(bf16[128,4,768]{2,1,0:T(4,128)(2,1)} %broadcast_select_fusion.1), calls=%async_computation | async-start | bytes 1572864 | tf_op jit(solution)/shard_map/all_to_all | solution.py:222
  30.4 1.9 copy.24.wt
  32.3 3.3 convert_element_type.16.w
  35.6 7.9 %all-to-all-done = bf16[128,4,768]{2,1,0:T(4,128)(2,1)S(1)} async-done(((bf16[128,4,768]{2,1,0:T(4,128)(2,1)}), bf16[128,4,768]{2,1,0:T(4,128)(2,1)S(1)}, u32[]{:S(2)}, u32[]{:S(2)}) %all-to-all-start) | async-done | bytes 786464 | tf_op jit(solution)/shard_map/all_to_all | solution.py:222
  44.6 57.3 %layer_one.1 = (bf16[4096,768]{1,0:T(8,128)(2,1)}, bf16[4096,1024]{1,0:T(8,128)(2,1)}) custom-call(s32[128,256]{1,0:T(8,128)} %bitcast.14, f32[4096,8]{1,0:T(8,128)} %copy.24.wt, bf16[4096,768]{1,0:T(8,128)(2,1)} %own.1, bf16[512,768]{1,0:T(8,128)(2,1)} %all_to_all.18.halo, bf16[768,1024]{1,0:T(8,128)(2,1)} %convert_element_type.16.w), custom_call_target="tpu_custom_call" | custom-call | tf_op jit(solution)/shard_map/layer_one/pallas_call | solution.py:232
  101.9 7.2 %gather_fusion.1 = bf16[512,1024]{1,0:T(8,128)(2,1)S(1)} fusion(bf16[4096,1024]{1,0:T(8,128)(2,1)} %get-tuple-element.8.own.h, s32[1024]{0:T(1024)S(1)} %pad_clamp_fusion), kind=kCustom, calls=%fused_computation.1 | custom fusion | bytes 2099200 | tf_op jit(solution)/shard_map/gather | solution.py:221
  109.6 1.5 broadcast_select_fusion
  111.1 4.5 all-to-all-start.1
  116.2 69.6 %psum.28 = f32[]{:T(128)} all-reduce(f32[]{:T(128)} %convert_reduce_fusion), channel_id=1, replica_groups=mesh['graph'=128] {'graph'}, use_global_device_ids=true, to_apply=%region_1.2 | all-reduce | flops 1 | bytes 8 | tf_op jit(solution)/shard_map/psum | solution.py:216
  186.9 1.9 copy.26.label
  188.8 1.5 copy.28
  190.3 1.6 mul.37
  191.9 1.6 copy.29
  193.6 1.9 pad.4.clone.w
  197.4 65.7 %layer_two.1 = (bf16[4096,256]{1,0:T(8,128)(2,1)}, f32[256,1024]{1,0:T(8,128)}, f32[1,1]{1,0:T(1,128)}) custom-call(s32[128,256]{1,0:T(8,128)} %bitcast.15, f32[1]{0:T(128)} %bitcast.1.inv_total, f32[4096,8]{1,0:T(8,128)} %copy.24.wt, bf16[4096,1024]{1,0:T(8,128)(2,1)} %get-tuple-element.8.own.h, bf16[512,1024]{1,0:T(8,128)(2,1)} %all_to_all.20.halo, ...), custom_call_target="tpu_custom_call" | custom-call | tf_op jit(solution)/shard_map/layer_two/pallas_call | solution.py:242
  263.1 42.1 %scatter.1.own = f32[9216,128]{1,0:T(8,128)} custom-call(s32[128,256]{1,0:T(8,128)} %bitcast.16, f32[4096,8]{1,0:T(8,128)} %copy.24.wt, bf16[4096,256]{1,0:T(8,128)(2,1)} %get-tuple-element.10.grad), custom_call_target="tpu_custom_call" | custom-call | tf_op jit(solution)/shard_map/scatter/pallas_call | solution.py:256
  305.2 2.0 slice_bitcast_fusion.1
  307.1 6.0 %all-to-all-start.2 = ((f32[128,8,128]{2,1,0:T(8,128)}), f32[128,8,128]{2,1,0:T(8,128)S(1)}, u32[]{:S(2)}, u32[]{:S(2)}) async-start(f32[128,8,128]{2,1,0:T(8,128)} %slice_bitcast_fusion.1), calls=%async_computation.2 | async-start | bytes 1048576 | tf_op jit(solution)/shard_map/all_to_all | solution.py:267
  315.8 10.8 %all-to-all-done.2 = f32[128,8,128]{2,1,0:T(8,128)S(1)} async-done(((f32[128,8,128]{2,1,0:T(8,128)}), f32[128,8,128]{2,1,0:T(8,128)S(1)}, u32[]{:S(2)}, u32[]{:S(2)}) %all-to-all-start.2) | async-done | bytes 524320 | tf_op jit(solution)/shard_map/all_to_all | solution.py:267
  327.4 24.5 %backward.1 = f32[768,1024]{1,0:T(8,128)} custom-call(s32[512]{0:T(512)} %mul.34.lists, f32[9216,128]{1,0:T(8,128)} %scatter.1.own, f32[1024,128]{1,0:T(8,128)} %bitcast.13, bf16[256,1024]{1,0:T(8,128)(2,1)} %pad_bitcast_fusion.w_t, bf16[4096,1024]{1,0:T(8,128)(2,1)} %get-tuple-element.8.own.h, bf16[4096,768]{1,0:T(8,128)(2,1)} %get-tuple-element.11.z), custom_call_target="tpu_custom_call" | custom-call | tf_op jit(solution)/shard_map/backward/pallas_call | solution.py:268
  351.9 63.0 %psum.29 = f32[]{:T(128)} all-reduce(f32[]{:T(128)} %bitcast.4), channel_id=1, replica_groups=mesh['graph'=128] {'graph'}, use_global_device_ids=true, to_apply=%region_2.3 | all-reduce | flops 1 | bytes 8 | tf_op jit(solution)/shard_map/psum | solution.py:285
  416.2 86.1 %all-reduce.4.cloned.1.call-done = (f32[768,1024]{1,0:T(8,128)}, f32[1024,153]{0,1:T(8,128)}) async-done(((f32[768,1024]{1,0:T(8,128)}, f32[1024,153]{0,1:T(8,128)}), (f32[768,1024]{1,0:T(8,128)}, f32[1024,153]{0,1:T(8,128)})) %all-reduce.4.cloned.1.call-update) | async-done | bytes 3772432 | tf_op jit(solution)/shard_map/psum | solution.py:285
  502.3 4.0 copy.34
  (48 shorter events, 14.2 us)
Async XLA Ops:
  8.1 6.2 %copy-start.9 = (s32[128]{0:T(128)S(1)}, s32[128]{0:T(128)}, u32[]{:S(2)}) copy-start(s32[128]{0:T(128)} %param.13) | copy-start | bytes 1540
  14.1 13.2 %copy-start.4 = (s32[4096,8]{0,1:T(8,128)S(1)}, s32[4096,8]{0,1:T(8,128)}, u32[]{:S(2)}) copy-start(s32[4096,8]{0,1:T(8,128)} %param.14) | copy-start | bytes 393220
  15.8 14.6 %copy-start.5 = (f32[4096,8]{0,1:T(8,128)S(1)}, f32[4096,8]{0,1:T(8,128)}, u32[]{:S(2)}) copy-start(f32[4096,8]{0,1:T(8,128)} %param.15) | copy-start | bytes 393220
  15.8 27.7 %all-to-all-start = ((bf16[128,4,768]{2,1,0:T(4,128)(2,1)}), bf16[128,4,768]{2,1,0:T(4,128)(2,1)S(1)}, u32[]{:S(2)}, u32[]{:S(2)}) async-start(bf16[128,4,768]{2,1,0:T(4,128)(2,1)} %broadcast_select_fusion.1), calls=%async_computation | async-start | bytes 1572864 | tf_op jit(solution)/shard_map/all_to_all | solution.py:222
  109.1 6.5 %copy-start.6 = (s32[4096]{0:T(1024)S(1)}, s32[4096]{0:T(1024)}, u32[]{:S(2)}) copy-start(s32[4096]{0:T(1024)} %param.17) | copy-start | bytes 49156
  109.5 76.3 %copy-start.2 = (f32[1024,153]{0,1:T(8,128)S(1)}, f32[1024,153]{0,1:T(8,128)}, u32[]{:S(2)}) copy-start(f32[1024,153]{0,1:T(8,128)} %param.11) | copy-start | bytes 1880068
  109.6 77.3 %copy-start.7 = (s32[4096]{0:T(1024)S(1)}, s32[4096]{0:T(1024)}, u32[]{:S(2)}) copy-start(s32[4096]{0:T(1024)} %param.16) | copy-start | bytes 49156
  111.1 85.1 %all-to-all-start.1 = ((bf16[128,4,1024]{2,1,0:T(4,128)(2,1)}), bf16[128,4,1024]{2,1,0:T(4,128)(2,1)S(1)}, u32[]{:S(2)}, u32[]{:S(2)}) async-start(bf16[128,4,1024]{2,1,0:T(4,128)(2,1)} %broadcast_select_fusion), calls=%async_computation.1 | async-start | bytes 2097152 | tf_op jit(solution)/shard_map/all_to_all | solution.py:222
  263.1 50.1 %copy-start.8 = (s32[128,4]{0,1:T(4,128)S(1)}, s32[128,4]{0,1:T(4,128)}, u32[]{:S(2)}) copy-start(s32[128,4]{0,1:T(4,128)} %param.12) | copy-start | bytes 6148
  305.2 9.7 %copy-start.3 = (f32[256,1024]{1,0:T(8,128)S(1)}, f32[256,1024]{1,0:T(8,128)}, u32[]{:S(2)}) copy-start(f32[256,1024]{1,0:T(8,128)} %get-tuple-element.12) | copy-start | bytes 3145732
  307.1 19.4 %all-to-all-start.2 = ((f32[128,8,128]{2,1,0:T(8,128)}), f32[128,8,128]{2,1,0:T(8,128)S(1)}, u32[]{:S(2)}, u32[]{:S(2)}) async-start(f32[128,8,128]{2,1,0:T(8,128)} %slice_bitcast_fusion.1), calls=%async_computation.2 | async-start | bytes 1048576 | tf_op jit(solution)/shard_map/all_to_all | solution.py:267
  313.2 189.2 %all-reduce.4.cloned.1.call-start = ((), (), s32[]{:S(2)}) async-start(), calls=%async_computation.3 | async-start | bytes 7602176 | tf_op jit(solution)/shard_map/psum | solution.py:285
  326.6 0.8 copy-start
  502.3 4.0 copy-start.1
Sparse Core Ops, SparseCore 0:
  352.0 150.3 all-reduce.3

commit v2 on v1

--- a/solution.py
+++ b/solution.py
@@ -72,7 +72,7 @@
     h_out[...] = jnp.maximum(y, 0.0).astype(BF16)
 
 
-def layer_two_kernel(classes, src, inv_total, wt, own, halo, w, label, g_out, gw_out, loss_out, table, zbuf, wbuf):
+def layer_two_kernel(classes, src, inv_total, wt, own, halo, w, label, g_out, gw_out, table, zbuf, wbuf, loss_sum):
     g = pl.program_id(0)
     rows, blocks = g_out.shape[0], own.shape[1] // LANES
 
@@ -81,7 +81,7 @@
         fill_rows(table, own, 0, blocks)
         fill_rows(table, halo, own.shape[0], blocks)
         gw_out[...] = jnp.zeros_like(gw_out)
-        loss_out[...] = jnp.zeros_like(loss_out)
+        loss_sum[...] = jnp.zeros_like(loss_sum)
 
     steps = rows // STEP
     gather_rows(g * steps, steps, src, wt, table, zbuf, wbuf)
@@ -95,11 +95,16 @@
     log_prob = shifted - log_sum
     tag = label[...]
     hit = col == tag
-    loss_out[...] += jnp.sum(jnp.where(hit, log_prob, 0.0), axis=(0, 1), keepdims=True)
+    loss_sum[...] += jnp.sum(jnp.where(hit, log_prob, 0.0), axis=0, keepdims=True)
     scale = jnp.where(tag >= 0, inv_total[0], 0.0)
     grad = jnp.where(real, (jnp.exp(log_prob) - jnp.where(hit, 1.0, 0.0)) * scale, 0.0).astype(BF16)
     g_out[...] = grad
     gw_out[...] += lax.dot_general(grad, z, (((0,), (0,)), ((), ())), preferred_element_type=F32)
+
+    @pl.when(g == pl.num_programs(0) - 1)
+    def _():
+        total = jnp.sum(loss_sum[...], axis=1, keepdims=True)
+        gw_out[pl.ds(gw_out.shape[0] - 1, 1), pl.ds(0, LANES)] = jnp.broadcast_to(total, (1, LANES))
 
 
 def scatter_kernel(src, wt, grad, s_out, gbuf, wbuf, *parts):
@@ -152,13 +157,15 @@
         lax.fori_loop(0, s_out.shape[0] // 64, add, 0)
 
 
-def backward_kernel(lists, own, back, w_t, h, z, gw_out, total):
+def backward_kernel(lists, own, back, w_t, gw_two, h, z, gw_out, total):
     g = pl.program_id(0)
     rows = h.shape[0]
 
     @pl.when(g == 0)
     def _():
-        gw_out[...] = jnp.zeros_like(gw_out)
+        f_in = z.shape[1]
+        gw_out[pl.ds(0, f_in), :] = jnp.zeros((f_in, gw_out.shape[1]), F32)
+        gw_out[pl.ds(f_in, gw_two.shape[0]), :] = gw_two[...]
 
         def copy(i, carry):
             at = pl.ds(pl.multiple_of(i * 64, 64), 64)
@@ -185,7 +192,160 @@
     d = d + jnp.dot(mid, wt, preferred_element_type=F32)
     d = d + jnp.dot(high, wt, preferred_element_type=F32)
     grad = jnp.where(h[...] > 0, d, 0.0).astype(BF16)
-    gw_out[...] += lax.dot_general(z[...], grad, (((0,), (0,)), ((), ())), preferred_element_type=F32)
+    gw_out[pl.ds(0, z.shape[1]), :] += lax.dot_general(z[...], grad, (((0,), (0,)), ((), ())), preferred_element_type=F32)
+
+
+MESH = pl.DeviceIdType.MESH
+SIDE = 4
+COLORS = ((0, 384, (0, 1, 2)), (384, 384, (1, 2, 0)), (768, 256, (2, 0, 1)))
+
+
+def reduce_kernel(x, out, acc, pair_buf, far, mid, near, *sems):
+    pair_send, pair_recv, rs_send, rs_recv, ag_send, ag_recv, back_send, back_recv = sems
+    me = lax.axis_index("graph")
+    core = lax.rem(me, 2)
+    where = [lax.rem(me // (2 * SIDE**d), SIDE) for d in range(3)]
+    partner = me + 1 - 2 * core
+
+    def peer(axis, t):
+        p = lax.rem(where[axis] + t, SIDE)
+        return p, me + (p - where[axis]) * (2 * SIDE**axis)
+
+    barrier = pltpu.get_barrier_semaphore()
+    pl.semaphore_signal(barrier, inc=1, device_id=(partner,), device_id_type=MESH)
+    for axis in range(3):
+        for t in range(1, SIDE):
+            pl.semaphore_signal(barrier, inc=1, device_id=(peer(axis, t)[1],), device_id_type=MESH)
+    pl.semaphore_wait(barrier, 10)
+
+    def remote(src, dst, send, recv, dev):
+        return pltpu.make_async_remote_copy(src_ref=src, dst_ref=dst, send_sem=send, recv_sem=recv, device_id=(dev,), device_id_type=MESH)
+
+    pending = []
+    base = pl.multiple_of(core * 512, 512)
+    other = pl.multiple_of(512 - core * 512, 512)
+    order = (2, 1, 3, 0)
+    pair = {}
+    for t in order:
+        for c, (lane, width, axes) in enumerate(COLORS):
+            p = lax.rem(where[axes[0]] + t, SIDE)
+            rows = pl.ds(pl.multiple_of(p * 128, 128), 128)
+            copy = remote(x.at[pl.ds(pl.multiple_of(other + p * 128, 128), 128), pl.ds(lane, width)], pair_buf.at[rows, pl.ds(lane, width)], pair_send.at[c, t], pair_recv.at[c, t], partner)
+            copy.start()
+            pair[c, t] = copy
+            pending.append(copy)
+    first = {}
+    for t in order:
+        for c, (lane, width, axes) in enumerate(COLORS):
+            p, dev = peer(axes[0], t)
+            rows = pl.ds(pl.multiple_of(p * 128, 128), 128)
+            lanes = pl.ds(lane, width)
+            pair[c, t].wait_recv()
+            acc[rows, lanes] = x[pl.ds(pl.multiple_of(base + p * 128, 128), 128), lanes] + pair_buf[rows, lanes]
+            if t:
+                copy = remote(acc.at[rows, lanes], far.at[t - 1, :, lanes], rs_send.at[0, c, t - 1], rs_recv.at[0, c, t - 1], dev)
+                copy.start()
+                first[c, t] = copy
+                pending.append(copy)
+    start = [0, 0, 0]
+    for stage, (size, buf) in enumerate(((128, far), (32, mid), (8, near))):
+        if stage:
+            first = {}
+            for c, (lane, width, axes) in enumerate(COLORS):
+                for t in (2, 1, 3):
+                    p, dev = peer(axes[stage], t)
+                    rows = pl.ds(pl.multiple_of(start[c] + p * size, 8), size)
+                    copy = remote(acc.at[rows, pl.ds(lane, width)], buf.at[t - 1, :, pl.ds(lane, width)], rs_send.at[stage, c, t - 1], rs_recv.at[stage, c, t - 1], dev)
+                    copy.start()
+                    first[c, t] = copy
+                    pending.append(copy)
+        for c, (lane, width, axes) in enumerate(COLORS):
+            lanes = pl.ds(lane, width)
+            start[c] = start[c] + where[axes[stage]] * size
+            rows = pl.ds(pl.multiple_of(start[c], 8), size)
+            for t in (1, 2, 3):
+                first[c, t].wait_recv()
+            mine = acc[rows, lanes] + buf[0, :, lanes] + buf[1, :, lanes] + buf[2, :, lanes]
+            if stage < 2:
+                acc[rows, lanes] = mine
+            else:
+                out[pl.ds(pl.multiple_of(base + start[c], 8), size), lanes] = mine
+    for stage, size in ((2, 8), (1, 32), (0, 128)):
+        copies = {}
+        for c, (lane, width, axes) in enumerate(COLORS):
+            lanes = pl.ds(lane, width)
+            rows = pl.ds(pl.multiple_of(base + start[c], 8), size)
+            for t in (2, 1, 3):
+                _, dev = peer(axes[stage], t)
+                copy = remote(out.at[rows, lanes], out.at[rows, lanes], ag_send.at[stage, c, t - 1], ag_recv.at[stage, c, t - 1], dev)
+                copy.start()
+                copies[c, t] = copy
+                pending.append(copy)
+            if stage == 0:
+                copy = remote(out.at[rows, lanes], out.at[rows, lanes], back_send.at[c, 0], back_recv.at[c, 0], partner)
+                copy.start()
+                copies[c, 0] = copy
+                pending.append(copy)
+        if stage:
+            for c, (lane, width, axes) in enumerate(COLORS):
+                for t in (1, 2, 3):
+                    copies[c, t].wait_recv()
+                start[c] = start[c] - where[axes[stage]] * size
+        else:
+            for t in (1, 3, 2):
+                for c, (lane, width, axes) in enumerate(COLORS):
+                    lanes = pl.ds(lane, width)
+                    copies[c, t].wait_recv()
+                    p, _ = peer(axes[0], SIDE - t)
+                    rows = pl.ds(pl.multiple_of(base + p * 128, 128), 128)
+                    copy = remote(out.at[rows, lanes], out.at[rows, lanes], back_send.at[c, t], back_recv.at[c, t], partner)
+                    copy.start()
+                    copies[c, t + 4] = copy
+                    pending.append(copy)
+            for c in range(3):
+                copies[c, 0].wait_recv()
+                for t in (1, 2, 3):
+                    copies[c, t + 4].wait_recv()
+    for copy in pending:
+        copy.wait_send()
+
+
+def reduce_all(x):
+    sem = pltpu.SemaphoreType.DMA
+    return pl.pallas_call(reduce_kernel,
+        in_specs=[pl.BlockSpec(memory_space=pltpu.VMEM)], out_specs=pl.BlockSpec(memory_space=pltpu.VMEM),
+        out_shape=jax.ShapeDtypeStruct((1024,1024),F32),
+        scratch_shapes=[pltpu.VMEM((512,1024),F32), pltpu.VMEM((512,1024),F32), pltpu.VMEM((3,128,1024),F32), pltpu.VMEM((3,32,1024),F32), pltpu.VMEM((3,8,1024),F32),
+            sem((3,4)), sem((3,4)), sem((3,3,3)), sem((3,3,3)), sem((3,3,3)), sem((3,3,3)), sem((3,4)), sem((3,4))],
+        compiler_params=pltpu.CompilerParams(collective_id=0, has_side_effects=True, vmem_limit_bytes=40*2**20),
+        name="reduce_all")(x)
+
+
+def exchange_body(n, outs, ins, sems):
+    me = lax.axis_index("graph")
+
+    def send(t, carry):
+        q = lax.rem(me + t, n)
+        for j, (o, i) in enumerate(zip(outs, ins)):
+            src = o.at[q] if o.shape[0] == n else o.at[0]
+            pltpu.make_async_remote_copy(src_ref=src, dst_ref=i.at[me], send_sem=sems[2*j], recv_sem=sems[2*j+1], device_id=(q,), device_id_type=MESH).start()
+        return carry
+    lax.fori_loop(1, n, send, 0)
+    for j, (o, i) in enumerate(zip(outs, ins)):
+        whole = i.at[pl.ds(0, n - 1)]
+        pltpu.make_async_copy(whole, whole, sems[2*j]).wait()
+        pltpu.make_async_copy(whole, whole, sems[2*j+1]).wait()
+
+def exchange(n, *arrays, name="exchange"):
+    k = len(arrays)
+    def kernel(*refs):
+        exchange_body(n, refs[:k], refs[k:2*k], refs[2*k:])
+    return pl.pallas_call(kernel,
+        in_specs=[pl.BlockSpec(memory_space=pltpu.VMEM)]*k, out_specs=[pl.BlockSpec(memory_space=pltpu.VMEM)]*k,
+        out_shape=[jax.ShapeDtypeStruct((n,)+a.shape[1:], a.dtype) for a in arrays],
+        scratch_shapes=[pltpu.SemaphoreType.DMA]*(2*k),
+        compiler_params=pltpu.CompilerParams(has_side_effects=True, vmem_limit_bytes=40*2**20),
+        name=name)(*arrays)
 
 
 def params():
@@ -213,13 +373,13 @@
         src8, src2 = src_t * 8, src_t * 2
         lists2 = jnp.where(list_ok, send_idx, n).reshape(halo) * 2
         label = jnp.where(label_mask == 1, labels, -1).reshape(n, 1)
-        label_total = lax.psum(jnp.sum(label_mask.astype(F32)), "graph")
+        ok_rows = list_ok.reshape(halo, 1)
+        count = jnp.sum(label_mask.astype(F32))
+        first_rows = jnp.where(ok_rows, feats[list_ids], 0).reshape(dev_count, halo_rows, f_in)
+        feats_in, counts = exchange(dev_count, first_rows, jnp.full((1, 1, LANES), count), name="exchange_one")
+        mine = jnp.arange(dev_count) == lax.axis_index("graph")
+        label_total = jnp.sum(jnp.where(mine, count, counts[:, 0, 0]))
         inv_total = (1.0 / label_total).reshape(1)
-        ok_rows = list_ok.reshape(halo, 1)
-
-        def exchange(h_rows):
-            outgoing = jnp.where(ok_rows, h_rows[list_ids], 0)
-            return lax.all_to_all(outgoing, "graph", 0, 0, tiled=True)
 
         def by_rows(width):
             return pl.BlockSpec((BLOCK, width), lambda g: (g, 0))
@@ -238,21 +398,19 @@
             scratch_shapes=gather_scratch,
             compiler_params=params(),
             name="layer_one",
-        )(src8, edge_wt, feats, exchange(feats), w_one_b)
-        grad_log, gw_two, loss_sum = pl.pallas_call(
+        )(src8, edge_wt, feats, feats_in.reshape(halo, f_in), w_one_b)
+        second_rows = jnp.where(ok_rows, h_one[list_ids], 0)
+        h_in = lax.all_to_all(second_rows, "graph", 0, 0, tiled=True)
+        grad_log, gw_two = pl.pallas_call(
             functools.partial(layer_two_kernel, classes),
             grid=(n // BLOCK,),
             in_specs=[SMEM, SMEM, by_rows(deg), once((n, f_hid)), once((halo, f_hid)), once((f_hid, pad)), by_rows(1)],
-            out_specs=[by_rows(pad), once((pad, f_hid)), once((1, 1))],
-            out_shape=[
-                jax.ShapeDtypeStruct((n, pad), BF16),
-                jax.ShapeDtypeStruct((pad, f_hid), F32),
-                jax.ShapeDtypeStruct((1, 1), F32),
-            ],
-            scratch_shapes=gather_scratch,
+            out_specs=[by_rows(pad), once((pad, f_hid))],
+            out_shape=[jax.ShapeDtypeStruct((n, pad), BF16), jax.ShapeDtypeStruct((pad, f_hid), F32)],
+            scratch_shapes=gather_scratch + [pltpu.VMEM((1, pad), F32)],
             compiler_params=params(),
             name="layer_two",
-        )(src8, inv_total, edge_wt, h_one, exchange(h_one), w_two_b, label)
+        )(src8, inv_total, edge_wt, h_one, h_in, w_two_b, label)
         ext_grad = pl.pallas_call(
             scatter_kernel,
             grid=(n // 512,),
@@ -265,7 +423,7 @@
             name="scatter",
         )(src2, edge_wt, grad_log)
         back = lax.all_to_all(ext_grad[n * 2 :], "graph", 0, 0, tiled=True)
-        gw_one = pl.pallas_call(
+        partial = pl.pallas_call(
             backward_kernel,
             grid=(n // 512,),
             in_specs=[
@@ -273,17 +431,18 @@
                 once((n * 2, LANES)),
                 once((halo * 2, LANES)),
                 once((pad, f_hid)),
+                once((pad, f_hid)),
                 pl.BlockSpec((512, f_hid), lambda g: (g, 0)),
                 pl.BlockSpec((512, f_in), lambda g: (g, 0)),
             ],
-            out_specs=once((f_in, f_hid)),
-            out_shape=jax.ShapeDtypeStruct((f_in, f_hid), F32),
+            out_specs=once((f_in + pad, f_hid)),
+            out_shape=jax.ShapeDtypeStruct((f_in + pad, f_hid), F32),
             scratch_shapes=[pltpu.VMEM((n * 2 + 8, LANES), F32)],
             compiler_params=params(),
             name="backward",
-        )(lists2, ext_grad, back, w_two_b.T, h_one, z_one)
-        loss_sum, gw_one, gw_two = lax.psum((loss_sum[0, 0], gw_one, gw_two[:classes].T), "graph")
-        return -loss_sum / label_total, gw_one, gw_two
+        )(lists2, ext_grad, back, w_two_b.T, gw_two, h_one, z_one)
+        total = reduce_all(partial)
+        return -total[f_in + pad - 1, 0] / label_total, total[:f_in], total[f_in : f_in + classes].T
 
     row_spec = P("graph", None)
     vec_spec = P("graph")

time: 516 us -> 352 us (0.68)
  blocking collectives: 133 us -> 0 us
  waiting for transfers between devices: 105 us -> 19.4 us
  Pallas kernels: 190 us -> 262 us
  between operations: 17.4 us -> 3.81 us
  starting transfers between devices: 22.1 us -> 12.4 us
    psum x2 -> x0, blocking collectives: 133 us -> none  [the longest x1 69.6 us: device_step(): label_total = lax.psum(jnp.sum(label_mask.astype(F32)), 'graph')]
    psum x1 -> x0, waiting for transfers between devices: 86.1 us -> none  [device_step(): lax.psum((loss_sum[0, 0], gw_one, gw_two[:classes].T), 'graph')]
    pallas_call x0 -> x2, Pallas kernels: none -> 71.3 us  [the longest x1 43.7 us: reduce_all(): pl.pallas_call(reduce_kernel, in_specs=[pl.BlockSpec(memory_space=pltpu.V...]
    all_to_all x2 -> x1, starting transfers between devices: 16 us -> 7.88 us  [device_step(): h_in = lax.all_to_all(second_rows, 'graph', 0, 0, tiled=True)]
  transfers between devices with their start and end apart: 4 -> 2, of which waited for: 3 -> 2; matrix products, arithmetic and copies ran while one was open for 4% -> 4% of each run, Pallas kernels for 0% -> 0%
where the time goes in v2:
time: 352 us; the launch traced here: 351 us
  Pallas kernels  262 us (74%)
  local copies, waits for them, and re-layouts  44.3 us (13%)
  waiting for transfers between devices  19.4 us (6%)
  starting transfers between devices  12.4 us (4%)
  other arithmetic  9.5 us (3%)
  between operations  3.81 us (1%)
    pallas_call x1, Pallas kernels, device_step(): pl.pallas_call(functools.partial(layer_two_kernel, classes), grid=(n // B...  65.8 us
    pallas_call x1, Pallas kernels, device_step(): pl.pallas_call(layer_one_kernel, grid=(n // BLOCK,), in_specs=[SMEM, by_r...  57.2 us
    pallas_call x1, Pallas kernels, reduce_all(): pl.pallas_call(reduce_kernel, in_specs=[pl.BlockSpec(memory_space=pltpu.V...  43.7 us
    pallas_call x1, Pallas kernels, device_step(): pl.pallas_call(scatter_kernel, grid=(n // 512,), in_specs=[SMEM, pl.Block...  42.1 us
    pallas_call x1, Pallas kernels, exchange(): pl.pallas_call(kernel, in_specs=[pl.BlockSpec(memory_space=pltpu.VMEM)] *...  27.6 us
    pallas_call x1, Pallas kernels, device_step(): pl.pallas_call(backward_kernel, grid=(n // 512,), in_specs=[SMEM, once((n...  25.2 us
    all_to_all x1, waiting for transfers between devices, device_step(): back = lax.all_to_all(ext_grad[n * 2:], 'graph', 0, 0, tiled=True)  11.7 us
    mul x6, local copies, waits for them, and re-layouts, device_step(): src8, src2 = (src_t * 8, src_t * 2)  10.7 us
  transfers between devices with their start and end apart: 2, of which 2 were waited for; matrix products, arithmetic and copies ran while one was open for 4% of the time, Pallas kernels for 0%

profile of v2, /device:TPU:1, one launch (start us, length us, event | category | flops | bytes accessed | tf_op | source)
XLA Modules:
  0.0 351.1 jit_solution(998395762767872539)
XLA Ops:
  0.6 1.3 convert_reduce_fusion
  4.6 6.0 %gather_fusion = bf16[512,768]{1,0:T(8,128)(2,1)S(1)} fusion(bf16[4096,768]{1,0:T(8,128)(2,1)} %own.1, s32[1024]{0:T(1024)S(1)} %pad_clamp_fusion), kind=kCustom, calls=%fused_computation | custom fusion | bytes 1574912 | tf_op jit(solution)/shard_map/gather | solution.py:378
  11.9 27.6 %exchange_one.1 = (bf16[128,4,768]{2,1,0:T(4,128)(2,1)S(1)}, f32[128,1,128]{2,1,0:T(1,128)S(1)}) custom-call(bf16[128,4,768]{2,1,0:T(4,128)(2,1)S(1)} %broadcast_select_fusion.1.refs_0_, f32[1,1,128]{2,1,0:T(1,128)S(1)} %broadcast_in_dim.47.refs_1_), custom_call_target="tpu_custom_call" | custom-call | tf_op jit(solution)/shard_map/exchange_one/pallas_call | solution.py:343
  40.6 3.3 convert_element_type.16.w
  43.9 1.9 copy.21
  45.8 2.6 mul.37
  49.2 1.9 copy.30.wt
  51.2 57.2 %layer_one.1 = (bf16[4096,768]{1,0:T(8,128)(2,1)}, bf16[4096,1024]{1,0:T(8,128)(2,1)}) custom-call(s32[128,256]{1,0:T(8,128)} %bitcast.14, f32[4096,8]{1,0:T(8,128)} %copy.30.wt, bf16[4096,768]{1,0:T(8,128)(2,1)} %own.1, bf16[512,768]{1,0:T(8,128)(2,1)} %reshape.87.halo, bf16[768,1024]{1,0:T(8,128)(2,1)} %convert_element_type.16.w), custom_call_target="tpu_custom_call" | custom-call | tf_op jit(solution)/shard_map/layer_one/pallas_call | solution.py:392
  108.4 7.2 %gather_fusion.1 = bf16[512,1024]{1,0:T(8,128)(2,1)S(1)} fusion(bf16[4096,1024]{1,0:T(8,128)(2,1)} %get-tuple-element.11.own.h, s32[1024]{0:T(1024)S(1)} %pad_clamp_fusion), kind=kCustom, calls=%fused_computation.1 | custom fusion | bytes 2099200 | tf_op jit(solution)/shard_map/gather | solution.py:402
  116.1 1.5 broadcast_select_fusion
  117.6 7.9 %all-to-all-start = ((bf16[128,4,1024]{2,1,0:T(4,128)(2,1)}), bf16[128,4,1024]{2,1,0:T(4,128)(2,1)S(1)}, u32[]{:S(2)}, u32[]{:S(2)}) async-start(bf16[128,4,1024]{2,1,0:T(4,128)(2,1)} %broadcast_select_fusion), calls=%async_computation | async-start | bytes 2097152 | tf_op jit(solution)/shard_map/all_to_all | solution.py:403
  125.8 2.0 copy.29.label
  127.8 1.9 copy.19
  129.7 2.6 mul.33
  136.8 7.7 %all-to-all-done = bf16[128,4,1024]{2,1,0:T(4,128)(2,1)S(1)} async-done(((bf16[128,4,1024]{2,1,0:T(4,128)(2,1)}), bf16[128,4,1024]{2,1,0:T(4,128)(2,1)S(1)}, u32[]{:S(2)}, u32[]{:S(2)}) %all-to-all-start) | async-done | bytes 1048608 | tf_op jit(solution)/shard_map/all_to_all | solution.py:403
  145.6 65.8 %layer_two.1 = (bf16[4096,256]{1,0:T(8,128)(2,1)}, f32[256,1024]{1,0:T(8,128)}) custom-call(s32[128,256]{1,0:T(8,128)} %bitcast.15, f32[1]{0:T(128)} %bitcast.3.inv_total, f32[4096,8]{1,0:T(8,128)} %copy.30.wt, bf16[4096,1024]{1,0:T(8,128)(2,1)} %get-tuple-element.11.own.h, bf16[512,1024]{1,0:T(8,128)(2,1)} %all_to_all.13.halo, ...), custom_call_target="tpu_custom_call" | custom-call | tf_op jit(solution)/shard_map/layer_two/pallas_call | solution.py:404
  211.5 42.1 %scatter.1.own = f32[9216,128]{1,0:T(8,128)} custom-call(s32[128,256]{1,0:T(8,128)} %bitcast.16, f32[4096,8]{1,0:T(8,128)} %copy.30.wt, bf16[4096,256]{1,0:T(8,128)(2,1)} %get-tuple-element.12.grad), custom_call_target="tpu_custom_call" | custom-call | tf_op jit(solution)/shard_map/scatter/pallas_call | solution.py:414
  253.6 1.9 slice_bitcast_fusion.1
  255.4 4.5 %all-to-all-start.1 = ((f32[128,8,128]{2,1,0:T(8,128)}), f32[128,8,128]{2,1,0:T(8,128)S(1)}, u32[]{:S(2)}, u32[]{:S(2)}) async-start(f32[128,8,128]{2,1,0:T(8,128)} %slice_bitcast_fusion.1), calls=%async_computation.1 | async-start | bytes 1048576 | tf_op jit(solution)/shard_map/all_to_all | solution.py:425
  261.6 11.7 %all-to-all-done.1 = f32[128,8,128]{2,1,0:T(8,128)S(1)} async-done(((f32[128,8,128]{2,1,0:T(8,128)}), f32[128,8,128]{2,1,0:T(8,128)S(1)}, u32[]{:S(2)}, u32[]{:S(2)}) %all-to-all-start.1) | async-done | bytes 524320 | tf_op jit(solution)/shard_map/all_to_all | solution.py:425
  274.1 25.2 %backward.1.x = f32[1024,1024]{1,0:T(8,128)} custom-call(s32[512]{0:T(512)} %mul.30.lists, f32[9216,128]{1,0:T(8,128)} %scatter.1.own, f32[1024,128]{1,0:T(8,128)} %bitcast.13, bf16[256,1024]{1,0:T(8,128)(2,1)} %pad_bitcast_fusion.w_t, f32[256,1024]{1,0:T(8,128)} %get-tuple-element.13.gw_two, bf16[4096,1024]{1,0:T(8,128)(2,1)} %get-tuple-element.11.own.h, ...), custom_call_target="tpu_custom_call" | custom-call | tf_op jit(solution)/shard_map/backward/pallas_call | solution.py:426
  299.4 2.2 copy-done
  301.5 43.7 %reduce_all.1 = f32[1024,1024]{1,0:T(8,128)S(1)} custom-call(f32[1024,1024]{1,0:T(8,128)S(1)} %copy-done), custom_call_target="tpu_custom_call" | custom-call | tf_op jit(solution)/shard_map/reduce_all/pallas_call | solution.py:315
  346.7 2.1 slice.18
  (42 shorter events, 15.3 us)
Async XLA Ops:
  40.6 8.7 %copy-start.3 = (f32[4096,8]{0,1:T(8,128)S(1)}, f32[4096,8]{0,1:T(8,128)}, u32[]{:S(2)}) copy-start(f32[4096,8]{0,1:T(8,128)} %param.15) | copy-start | bytes 393220
  115.6 9.9 %copy-start.2 = (f32[1024,153]{0,1:T(8,128)S(1)}, f32[1024,153]{0,1:T(8,128)}, u32[]{:S(2)}) copy-start(f32[1024,153]{0,1:T(8,128)} %param.11) | copy-start | bytes 1880068
  115.6 10.2 %copy-start.4 = (s32[4096]{0:T(1024)S(1)}, s32[4096]{0:T(1024)}, u32[]{:S(2)}) copy-start(s32[4096]{0:T(1024)} %param.17) | copy-start | bytes 49156
  115.6 10.2 %copy-start.5 = (s32[4096]{0:T(1024)S(1)}, s32[4096]{0:T(1024)}, u32[]{:S(2)}) copy-start(s32[4096]{0:T(1024)} %param.16) | copy-start | bytes 49156
  117.6 26.9 %all-to-all-start = ((bf16[128,4,1024]{2,1,0:T(4,128)(2,1)}), bf16[128,4,1024]{2,1,0:T(4,128)(2,1)S(1)}, u32[]{:S(2)}, u32[]{:S(2)}) async-start(bf16[128,4,1024]{2,1,0:T(4,128)(2,1)} %broadcast_select_fusion), calls=%async_computation | async-start | bytes 2097152 | tf_op jit(solution)/shard_map/all_to_all | solution.py:403
  211.5 48.5 %copy-start.6 = (s32[128,4]{0,1:T(4,128)S(1)}, s32[128,4]{0,1:T(4,128)}, u32[]{:S(2)}) copy-start(s32[128,4]{0,1:T(4,128)} %param.12) | copy-start | bytes 6148
  211.5 48.5 %copy-start.7 = (s32[128]{0:T(128)S(1)}, s32[128]{0:T(128)}, u32[]{:S(2)}) copy-start(s32[128]{0:T(128)} %param.13) | copy-start | bytes 1540
  255.4 17.9 %all-to-all-start.1 = ((f32[128,8,128]{2,1,0:T(8,128)}), f32[128,8,128]{2,1,0:T(8,128)S(1)}, u32[]{:S(2)}, u32[]{:S(2)}) async-start(f32[128,8,128]{2,1,0:T(8,128)} %slice_bitcast_fusion.1), calls=%async_computation.1 | async-start | bytes 1048576 | tf_op jit(solution)/shard_map/all_to_all | solution.py:425
  273.3 0.8 copy-start.1
  299.4 2.2 copy-start

commit v3 on v2

--- a/solution.py
+++ b/solution.py
@@ -9,7 +9,7 @@
 
 LANES = 128
 STEP = 16
-BLOCK = 256
+BLOCK = 512
 F32, BF16 = jnp.float32, jnp.bfloat16
 
 
@@ -28,63 +28,145 @@
     lax.fori_loop(0, src.shape[0] // 64, step, 0)
 
 
-def spread_weights(w, deg):
-    return tuple(jnp.broadcast_to(w[h * 8 : h * 8 + 8, k : k + 1], (8, LANES)) for h in range(STEP // 8) for k in range(deg))
-
-
-def gather_rows(first_step, steps, src, wt, table, out, wbuf):
+def put_weights(wbuf, w):
+    deg = w.shape[1]
+    for h in range(STEP // 8):
+        for k in range(deg):
+            tile = jnp.broadcast_to(w[h * 8 : h * 8 + 8, k : k + 1], (8, LANES))
+            wbuf[pl.ds((h * deg + k) * 8, 8), :] = tile
+
+
+def gather_rows(steps, row_of, src, wt, table, out, wbuf):
     deg = wt.shape[1]
 
-    def weights_at(i):
-        return spread_weights(wt[pl.ds(pl.multiple_of(i * STEP, STEP), STEP), :], deg)
-
-    def step(i, tiles):
-        for t, tile in enumerate(tiles):
-            wbuf[pl.ds(t * 8, 8), :] = tile
-        ahead = weights_at(jnp.minimum(i + 1, steps - 1))
+    def put(i):
+        put_weights(wbuf, wt[pl.ds(pl.multiple_of(i * STEP, STEP), STEP), :])
+
+    put(0)
+
+    def step(i, carry):
         dst = out.at[pl.ds(pl.multiple_of(i * STEP * 8, STEP * 8), STEP * 8)]
         for u in range(STEP):
+            n = row_of(i * STEP + u)
             acc = None
             for k in range(deg):
-                row = table[pl.ds(pl.multiple_of(src[u * deg + k, first_step + i], 8), 8), :]
+                row = table[pl.ds(pl.multiple_of(src[k][n], 8), 8), :]
                 term = row * wbuf[pl.ds((u // 8 * deg + k) * 8 + u % 8, 8, stride=0), :]
                 acc = term if acc is None else acc + term
             dst[pl.ds(u * 8, 8), :] = acc
-        return ahead
-
-    lax.fori_loop(0, steps, step, weights_at(0))
-
-
-def layer_one_kernel(src, wt, own, halo, w, z_out, h_out, table, zbuf, wbuf):
+        put(jnp.minimum(i + 1, steps - 1))
+        return carry
+
+    lax.fori_loop(0, steps, step, 0)
+
+
+def load_sources(src_hbm, src, sems):
+    n = src[0].shape[0]
+    copies = [pltpu.make_async_copy(src_hbm.at[pl.ds(k * n, n)], ref, sems.at[k]) for k, ref in enumerate(src)]
+    for copy in copies:
+        copy.start()
+    return copies
+
+
+def fill_tiles(dst, src, offset):
+    def step(i, carry):
+        at = pl.multiple_of(i * 128, 128)
+        dst[pl.ds(pl.multiple_of(offset * 8 + at, 8), 128), :] = src[pl.ds(at, 128), :].astype(F32)
+        return carry
+
+    lax.fori_loop(0, src.shape[0] // 128, step, 0)
+
+
+def layer_one_kernel(lists, list_ok, src_hbm, feats, halo, wt_t, w_f32, z_out, h_out, wt_out, second,
+                     table, zbuf, wbuf, w, chunk, list_wt, src_sem, chunk_sem, *src):
     g = pl.program_id(0)
-    rows, blocks = z_out.shape[0], own.shape[1] // LANES
+    rows, blocks = z_out.shape[0], feats.shape[1] // LANES
+    n, deg = wt_out.shape
+
+    def aggregate():
+        return jnp.concatenate([zbuf[pl.ds(c, rows, stride=8), :] for c in range(blocks)], axis=1).astype(BF16)
+
+    def hidden(z):
+        return jnp.maximum(jnp.dot(z, w[...], preferred_element_type=F32), 0.0)
 
     @pl.when(g == 0)
     def _():
-        fill_rows(table, own, 0, blocks)
-        fill_rows(table, halo, own.shape[0], blocks)
-
-    steps = rows // STEP
-    gather_rows(g * steps, steps, src, wt, table, zbuf, wbuf)
-    z = jnp.concatenate([zbuf[pl.ds(c, rows, stride=8), :] for c in range(blocks)], axis=1).astype(BF16)
-    z_out[...] = z
-    y = jnp.dot(z, w[...], preferred_element_type=F32)
-    h_out[...] = jnp.maximum(y, 0.0).astype(BF16)
-
-
-def layer_two_kernel(classes, src, inv_total, wt, own, halo, w, label, g_out, gw_out, table, zbuf, wbuf, loss_sum):
+        index_copies = load_sources(src_hbm, src, src_sem)
+
+        def fetch(i):
+            slot = lax.rem(i, 2)
+            return pltpu.make_async_copy(feats.at[pl.ds(pl.multiple_of(i * rows, rows), rows), :], chunk.at[slot], chunk_sem.at[slot])
+
+        fetch(0).start()
+
+        def turn(i, carry):
+            at = pl.ds(pl.multiple_of(i * LANES, LANES), LANES)
+            wt_out[at, :] = wt_t[:, at].T
+            return carry
+
+        lax.fori_loop(0, n // LANES, turn, 0)
+        w[...] = w_f32[...].astype(BF16)
+        fill_rows(table, halo, n, blocks)
+
+        def take(i, carry):
+            @pl.when(i + 1 < n // rows)
+            def _():
+                fetch(i + 1).start()
+
+            fetch(i).wait()
+            slot = lax.rem(i, 2)
+
+            def fill(j, carry):
+                r = pl.multiple_of(j * 64, 64)
+                x = chunk[slot, pl.ds(r, 64), :].astype(F32)
+                for c in range(blocks):
+                    table[pl.ds((i * rows + r) * 8 + c, 64, stride=8), :] = x[:, c * LANES : (c + 1) * LANES]
+                return carry
+
+            return lax.fori_loop(0, rows // 64, fill, carry)
+
+        lax.fori_loop(0, n // rows, take, 0)
+
+        def pick(i, carry):
+            for u in range(8):
+                j = i * 8 + u
+                list_wt[pl.ds(j, 1), :] = wt_out[pl.ds(lists[j], 1), :] * list_ok[j]
+            return carry
+
+        lax.fori_loop(0, rows // 8, pick, 0)
+        for copy in index_copies:
+            copy.wait()
+        gather_rows(rows // STEP, lambda j: lists[j], src, list_wt, table, zbuf, wbuf)
+        h = hidden(aggregate())
+        for c in range(h.shape[1] // LANES):
+            zbuf[pl.ds(c, rows, stride=8), :] = h[:, c * LANES : (c + 1) * LANES]
+        second[...] = zbuf[...].astype(BF16)
+
+    @pl.when(g > 0)
+    def _():
+        first_row = pl.multiple_of((g - 1) * rows, rows)
+        gather_rows(rows // STEP, lambda j: first_row + j, src, wt_out.at[pl.ds(first_row, rows)], table, zbuf, wbuf)
+        z = aggregate()
+        z_out[...] = z
+        h_out[...] = hidden(z).astype(BF16)
+
+
+def layer_two_kernel(classes, src_hbm, inv_total, wt, own, halo, w, label, g_out, gw_out, table, zbuf, wbuf, loss_sum, src_sem, *src):
     g = pl.program_id(0)
     rows, blocks = g_out.shape[0], own.shape[1] // LANES
 
     @pl.when(g == 0)
     def _():
+        index_copies = load_sources(src_hbm, src, src_sem)
         fill_rows(table, own, 0, blocks)
-        fill_rows(table, halo, own.shape[0], blocks)
+        fill_tiles(table, halo, own.shape[0])
+        for copy in index_copies:
+            copy.wait()
         gw_out[...] = jnp.zeros_like(gw_out)
         loss_sum[...] = jnp.zeros_like(loss_sum)
 
-    steps = rows // STEP
-    gather_rows(g * steps, steps, src, wt, table, zbuf, wbuf)
+    first_row = g * rows
+    gather_rows(rows // STEP, lambda j: first_row + j, src, wt, table, zbuf, wbuf)
     z = jnp.concatenate([zbuf[pl.ds(c, rows, stride=8), :] for c in range(blocks)], axis=1).astype(BF16)
     logits = jnp.dot(z, w[...], preferred_element_type=F32)
     col = lax.broadcasted_iota(jnp.int32, logits.shape, 1)
@@ -107,13 +189,16 @@
         gw_out[pl.ds(gw_out.shape[0] - 1, 1), pl.ds(0, LANES)] = jnp.broadcast_to(total, (1, LANES))
 
 
-def scatter_kernel(src, wt, grad, s_out, gbuf, wbuf, *parts):
+def scatter_kernel(src_hbm, wt, grad, s_out, gbuf, wbuf, src_sem, *refs):
     g = pl.program_id(0)
     rows, deg = grad.shape[0], wt.shape[1]
+    src, parts = refs[:deg], refs[deg:]
     steps = rows // STEP
 
     @pl.when(g == 0)
     def _():
+        index_copies = load_sources(src_hbm, src, src_sem)
+
         def clear(i, carry):
             for part in parts:
                 for j in range(8):
@@ -121,28 +206,31 @@
             return carry
 
         lax.fori_loop(0, s_out.shape[0] // 64, clear, 0)
+        for copy in index_copies:
+            copy.wait()
 
     x = grad[...].astype(F32)
     for c in range(2):
         gbuf[pl.ds(c, rows, stride=2), :] = x[:, c * LANES : (c + 1) * LANES]
 
-    def weights_at(i):
-        return spread_weights(wt[pl.ds(pl.multiple_of(i * STEP, STEP), STEP), :], deg)
-
-    def step(i, tiles):
-        for t, tile in enumerate(tiles):
-            wbuf[pl.ds(t * 8, 8), :] = tile
-        ahead = weights_at(jnp.minimum(i + 1, steps - 1))
+    def put(i):
+        put_weights(wbuf, wt[pl.ds(pl.multiple_of(i * STEP, STEP), STEP), :])
+
+    put(0)
+
+    def step(i, carry):
         here = gbuf.at[pl.ds(pl.multiple_of(i * STEP * 2, STEP * 2), STEP * 2)]
         for u in range(STEP):
             row = here[pl.ds(u * 2, 2), :]
+            n = g * rows + i * STEP + u
             for k in range(deg):
-                at = pl.ds(pl.multiple_of(src[u * deg + k, g * steps + i], 2), 2)
+                at = pl.ds(pl.multiple_of(src[k][n], 2), 2)
                 w = wbuf[pl.ds((u // 8 * deg + k) * 8 + u % 8, 2, stride=0), :]
                 parts[k][at, :] = parts[k][at, :] + row * w
-        return ahead
-
-    lax.fori_loop(0, steps, step, weights_at(0))
+        put(jnp.minimum(i + 1, steps - 1))
+        return carry
+
+    lax.fori_loop(0, steps, step, 0)
 
     @pl.when(g == pl.num_programs(0) - 1)
     def _():
@@ -321,31 +409,59 @@
         name="reduce_all")(x)
 
 
-def exchange_body(n, outs, ins, sems):
+def count_kernel(x, out, came, send, recv):
     me = lax.axis_index("graph")
-
-    def send(t, carry):
-        q = lax.rem(me + t, n)
-        for j, (o, i) in enumerate(zip(outs, ins)):
-            src = o.at[q] if o.shape[0] == n else o.at[0]
-            pltpu.make_async_remote_copy(src_ref=src, dst_ref=i.at[me], send_sem=sems[2*j], recv_sem=sems[2*j+1], device_id=(q,), device_id_type=MESH).start()
-        return carry
-    lax.fori_loop(1, n, send, 0)
-    for j, (o, i) in enumerate(zip(outs, ins)):
-        whole = i.at[pl.ds(0, n - 1)]
-        pltpu.make_async_copy(whole, whole, sems[2*j]).wait()
-        pltpu.make_async_copy(whole, whole, sems[2*j+1]).wait()
-
-def exchange(n, *arrays, name="exchange"):
-    k = len(arrays)
-    def kernel(*refs):
-        exchange_body(n, refs[:k], refs[k:2*k], refs[2*k:])
-    return pl.pallas_call(kernel,
-        in_specs=[pl.BlockSpec(memory_space=pltpu.VMEM)]*k, out_specs=[pl.BlockSpec(memory_space=pltpu.VMEM)]*k,
-        out_shape=[jax.ShapeDtypeStruct((n,)+a.shape[1:], a.dtype) for a in arrays],
-        scratch_shapes=[pltpu.SemaphoreType.DMA]*(2*k),
-        compiler_params=pltpu.CompilerParams(has_side_effects=True, vmem_limit_bytes=40*2**20),
-        name=name)(*arrays)
+    hops = [(1, 2)] + [(2 * SIDE**axis, SIDE) for axis in range(3)]
+
+    def peer(stride, size, t):
+        here = lax.rem(me // stride, size)
+        return me + (lax.rem(here + t, size) - here) * stride
+
+    barrier = pltpu.get_barrier_semaphore()
+    for stride, size in hops:
+        for t in range(1, size):
+            pl.semaphore_signal(barrier, inc=1, device_id=(peer(stride, size, t),), device_id_type=MESH)
+    pl.semaphore_wait(barrier, came.shape[0])
+    out[0] = x[...]
+    slot = 0
+    copies = []
+    for stage, (stride, size) in enumerate(hops):
+        step = []
+        for t in range(1, size):
+            at = slot + t - 1
+            step.append(
+                pltpu.make_async_remote_copy(
+                    src_ref=out.at[stage],
+                    dst_ref=came.at[at],
+                    send_sem=send.at[at],
+                    recv_sem=recv.at[at],
+                    device_id=(peer(stride, size, t),),
+                    device_id_type=MESH,
+                )
+            )
+            step[-1].start()
+        total = out[stage]
+        for t, copy in enumerate(step):
+            copy.wait_recv()
+            total = total + came[slot + t]
+        out[stage + 1] = total
+        slot += size - 1
+        copies += step
+    for copy in copies:
+        copy.wait_send()
+
+
+def count_all(x):
+    vmem = pl.BlockSpec(memory_space=pltpu.VMEM)
+    return pl.pallas_call(
+        count_kernel,
+        in_specs=[vmem],
+        out_specs=vmem,
+        out_shape=jax.ShapeDtypeStruct((5, 8, LANES), F32),
+        scratch_shapes=[pltpu.VMEM((10, 8, LANES), F32), pltpu.SemaphoreType.DMA((10,)), pltpu.SemaphoreType.DMA((10,))],
+        compiler_params=pltpu.CompilerParams(collective_id=1, has_side_effects=True, vmem_limit_bytes=2**20),
+        name="count_all",
+    )(x)
 
 
 def params():
@@ -365,63 +481,80 @@
         halo = dev_count * halo_rows
         ext = n + halo
         pad = 2 * LANES
-        w_one_b = w_one.astype(BF16)
         w_two_b = jnp.pad(w_two.astype(BF16), ((0, 0), (0, pad - classes)))
+        list_ok = jnp.arange(halo_rows)[None, :] < send_count[:, None]
         list_ids = send_idx.reshape(halo)
-        list_ok = jnp.arange(halo_rows)[None, :] < send_count[:, None]
-        src_t = edge_src.reshape(n // STEP, STEP * deg).T
+        first_rows = jnp.where(list_ok.reshape(halo, 1), feats[list_ids], 0)
+        first_in = lax.all_to_all(first_rows, "graph", 0, 0, tiled=True)
+        lists2 = jnp.where(list_ok, send_idx, n).reshape(halo) * 2
+        src_t = edge_src.T.reshape(deg * n)
         src8, src2 = src_t * 8, src_t * 2
-        lists2 = jnp.where(list_ok, send_idx, n).reshape(halo) * 2
         label = jnp.where(label_mask == 1, labels, -1).reshape(n, 1)
-        ok_rows = list_ok.reshape(halo, 1)
         count = jnp.sum(label_mask.astype(F32))
-        first_rows = jnp.where(ok_rows, feats[list_ids], 0).reshape(dev_count, halo_rows, f_in)
-        feats_in, counts = exchange(dev_count, first_rows, jnp.full((1, 1, LANES), count), name="exchange_one")
-        mine = jnp.arange(dev_count) == lax.axis_index("graph")
-        label_total = jnp.sum(jnp.where(mine, count, counts[:, 0, 0]))
-        inv_total = (1.0 / label_total).reshape(1)
 
         def by_rows(width):
             return pl.BlockSpec((BLOCK, width), lambda g: (g, 0))
+
+        def after_first(width):
+            return pl.BlockSpec((BLOCK, width), lambda g: (jnp.maximum(g - 1, 0), 0))
 
         gather_scratch = [
             pltpu.VMEM((ext * 8, LANES), F32),
             pltpu.VMEM((BLOCK * 8, LANES), F32),
             pltpu.VMEM((STEP * deg + 8, LANES), F32),
         ]
-        z_one, h_one = pl.pallas_call(
+        index_scratch = [pltpu.SMEM((n,), jnp.int32) for _ in range(deg)]
+        whole = pl.BlockSpec(memory_space=pl.ANY)
+        dma = pltpu.SemaphoreType.DMA
+        z_one, h_one, wt, second = pl.pallas_call(
             layer_one_kernel,
-            grid=(n // BLOCK,),
-            in_specs=[SMEM, by_rows(deg), once((n, f_in)), once((halo, f_in)), once((f_in, f_hid))],
-            out_specs=[by_rows(f_in), by_rows(f_hid)],
-            out_shape=[jax.ShapeDtypeStruct((n, f_in), BF16), jax.ShapeDtypeStruct((n, f_hid), BF16)],
-            scratch_shapes=gather_scratch,
+            grid=(1 + n // BLOCK,),
+            in_specs=[SMEM, SMEM, whole, whole, once((halo, f_in)), once((deg, n)), once((f_in, f_hid))],
+            out_specs=[after_first(f_in), after_first(f_hid), once((n, deg)), once((halo * 8, LANES))],
+            out_shape=[
+                jax.ShapeDtypeStruct((n, f_in), BF16),
+                jax.ShapeDtypeStruct((n, f_hid), BF16),
+                jax.ShapeDtypeStruct((n, deg), F32),
+                jax.ShapeDtypeStruct((halo * 8, LANES), BF16),
+            ],
+            scratch_shapes=gather_scratch
+            + [
+                pltpu.VMEM((f_in, f_hid), BF16),
+                pltpu.VMEM((2, BLOCK, f_in), BF16),
+                pltpu.VMEM((halo, deg), F32),
+                dma((deg,)),
+                dma((2,)),
+            ]
+            + index_scratch,
             compiler_params=params(),
             name="layer_one",
-        )(src8, edge_wt, feats, feats_in.reshape(halo, f_in), w_one_b)
-        second_rows = jnp.where(ok_rows, h_one[list_ids], 0)
-        h_in = lax.all_to_all(second_rows, "graph", 0, 0, tiled=True)
+        )(list_ids, list_ok.reshape(halo).astype(F32), src8, feats, first_in, edge_wt.T, w_one)
+        count, second = lax.optimization_barrier((count, second))
+        h_in = lax.all_to_all(second, "graph", 0, 0, tiled=True)
+        label_total = count_all(jnp.full((8, LANES), count))[4, 0, 0]
+        inv_total = (1.0 / label_total).reshape(1)
         grad_log, gw_two = pl.pallas_call(
             functools.partial(layer_two_kernel, classes),
             grid=(n // BLOCK,),
-            in_specs=[SMEM, SMEM, by_rows(deg), once((n, f_hid)), once((halo, f_hid)), once((f_hid, pad)), by_rows(1)],
+            in_specs=[whole, SMEM, by_rows(deg), once((n, f_hid)), once((halo * 8, LANES)), once((f_hid, pad)), by_rows(1)],
             out_specs=[by_rows(pad), once((pad, f_hid))],
             out_shape=[jax.ShapeDtypeStruct((n, pad), BF16), jax.ShapeDtypeStruct((pad, f_hid), F32)],
-            scratch_shapes=gather_scratch + [pltpu.VMEM((1, pad), F32)],
+            scratch_shapes=gather_scratch + [pltpu.VMEM((1, pad), F32), dma((deg,))] + index_scratch,
             compiler_params=params(),
             name="layer_two",
-        )(src8, inv_total, edge_wt, h_one, h_in, w_two_b, label)
+        )(src8, inv_total, wt, h_one, h_in, w_two_b, label)
         ext_grad = pl.pallas_call(
             scatter_kernel,
             grid=(n // 512,),
-            in_specs=[SMEM, pl.BlockSpec((512, deg), lambda g: (g, 0)), pl.BlockSpec((512, pad), lambda g: (g, 0))],
+            in_specs=[whole, by_rows(deg), by_rows(pad)],
             out_specs=once((ext * 2, LANES)),
             out_shape=jax.ShapeDtypeStruct((ext * 2, LANES), F32),
-            scratch_shapes=[pltpu.VMEM((512 * 2, LANES), F32), pltpu.VMEM((STEP * deg + 8, LANES), F32)]
+            scratch_shapes=[pltpu.VMEM((BLOCK * 2, LANES), F32), pltpu.VMEM((STEP * deg + 8, LANES), F32), dma((deg,))]
+            + index_scratch
             + [pltpu.VMEM((ext * 2, LANES), F32) for _ in range(deg)],
             compiler_params=params(),
             name="scatter",
-        )(src2, edge_wt, grad_log)
+        )(src2, wt, grad_log)
         back = lax.all_to_all(ext_grad[n * 2 :], "graph", 0, 0, tiled=True)
         partial = pl.pallas_call(
             backward_kernel,

time: 352 us -> 323 us (0.918)
  Pallas kernels: 262 us -> 242 us
  local copies, waits for them, and re-layouts: 44.3 us -> 26.3 us
  starting transfers between devices: 12.4 us -> 22.3 us
  other arithmetic: 9.5 us -> 2.69 us
  waiting for transfers between devices: 19.4 us -> 25.2 us
    pallas_call x1, Pallas kernels: 65.8 us -> 51.7 us  [device_step(): pl.pallas_call(functools.partial(layer_two_kernel, classes), grid=(n // B...]
    mul x6 -> x0, local copies, waits for them, and re-layouts: 10.7 us -> none  [device_step(): src8, src2 = (src_t * 8, src_t * 2)]
    all_to_all x1 -> x2, starting transfers between devices: 7.88 us -> 16.1 us  [the longest x1 11.5 us: device_step(): first_in = lax.all_to_all(first_rows, 'graph', 0, 0, tiled=True)]
    gather x4 -> x2, local copies, waits for them, and re-layouts: 13.8 us -> 6.17 us  [device_step(): first_rows = jnp.where(list_ok.reshape(halo, 1), feats[list_ids], 0)]
    all_to_all x1 -> x2, waiting for transfers between devices: 7.7 us -> 13.5 us  [the longest x1 13.5 us: device_step(): first_in = lax.all_to_all(first_rows, 'graph', 0, 0, tiled=True)]
    pallas_call x3, Pallas kernels: 127 us -> 121 us  [the longest x1 57.9 us: device_step(): pl.pallas_call(layer_one_kernel, grid=(1 + n // BLOCK,), in_specs=[SMEM,...]
  transfers between devices with their start and end apart: 2 -> 3, of which waited for: 2 -> 2; matrix products, arithmetic and copies ran while one was open for 4% -> 3% of each run, Pallas kernels for 0% -> 6%
where the time goes in v3:
time: 323 us; the launch traced here: 322 us
  Pallas kernels  242 us (75%)
  local copies, waits for them, and re-layouts  26.3 us (8%)
  waiting for transfers between devices  25.2 us (8%)
  starting transfers between devices  22.3 us (7%)
  between operations  3.92 us (1%)
    pallas_call x1, Pallas kernels, device_step(): pl.pallas_call(layer_one_kernel, grid=(1 + n // BLOCK,), in_specs=[SMEM,...  57.9 us
    pallas_call x1, Pallas kernels, device_step(): pl.pallas_call(functools.partial(layer_two_kernel, classes), grid=(n // B...  51.7 us
    pallas_call x1, Pallas kernels, device_step(): pl.pallas_call(scatter_kernel, grid=(n // 512,), in_specs=[whole, by_rows...  45.5 us
    pallas_call x1, Pallas kernels, reduce_all(): pl.pallas_call(reduce_kernel, in_specs=[pl.BlockSpec(memory_space=pltpu.V...  43.7 us
    pallas_call x1, Pallas kernels, device_step(): pl.pallas_call(backward_kernel, grid=(n // 512,), in_specs=[SMEM, once((n...  25.3 us
    pallas_call x1, Pallas kernels, count_all(): pl.pallas_call(count_kernel, in_specs=[vmem], out_specs=vmem, out_shape=j...  17.9 us
    all_to_all x1, waiting for transfers between devices, device_step(): first_in = lax.all_to_all(first_rows, 'graph', 0, 0, tiled=True)  13.5 us
    all_to_all x1, waiting for transfers between devices, device_step(): back = lax.all_to_all(ext_grad[n * 2:], 'graph', 0, 0, tiled=True)  11.7 us
  transfers between devices with their start and end apart: 3, of which 2 were waited for; matrix products, arithmetic and copies ran while one was open for 3% of the time, Pallas kernels for 6%

profile of v3, /device:TPU:1, one launch (start us, length us, event | category | flops | bytes accessed | tf_op | source)
XLA Modules:
  0.0 322.4 jit_solution(2508807085100712692)
XLA Ops:
  1.4 0.8 copy.15
  2.4 6.0 %gather_fusion = bf16[512,768]{1,0:T(8,128)(2,1)S(1)} fusion(bf16[4096,768]{1,0:T(8,128)(2,1)} %feats.1, s32[1024]{0:T(1024)S(1)} %pad_clamp_fusion), kind=kCustom, calls=%fused_computation | custom fusion | bytes 1574912 | tf_op jit(solution)/shard_map/gather | solution.py:487
  8.6 1.3 broadcast_select_fusion
  9.9 11.5 %all-to-all-start = ((bf16[128,4,768]{2,1,0:T(4,128)(2,1)}), bf16[128,4,768]{2,1,0:T(4,128)(2,1)S(1)}, u32[]{:S(2)}, u32[]{:S(2)}) async-start(bf16[128,4,768]{2,1,0:T(4,128)(2,1)} %broadcast_select_fusion), calls=%async_computation | async-start | bytes 1572864 | tf_op jit(solution)/shard_map/all_to_all | solution.py:488
  24.2 13.5 %all-to-all-done = bf16[128,4,768]{2,1,0:T(4,128)(2,1)S(1)} async-done(((bf16[128,4,768]{2,1,0:T(4,128)(2,1)}), bf16[128,4,768]{2,1,0:T(4,128)(2,1)S(1)}, u32[]{:S(2)}, u32[]{:S(2)}) %all-to-all-start) | async-done | bytes 786464 | tf_op jit(solution)/shard_map/all_to_all | solution.py:488
  37.6 1.1 all_to_all.20.halo
  38.7 57.9 %layer_one.1 = (bf16[4096,768]{1,0:T(8,128)(2,1)}, bf16[4096,1024]{1,0:T(8,128)(2,1)}, f32[4096,8]{1,0:T(8,128)}, bf16[4096,128]{1,0:T(8,128)(2,1)}) custom-call(s32[512]{0:T(512)} %reshape.85.lists, f32[512]{0:T(512)} %reshape.89.list_ok, s32[32768]{0:T(1024)} %bitcast.25, bf16[4096,768]{1,0:T(8,128)(2,1)} %feats.1, bf16[512,768]{1,0:T(8,128)(2,1)} %all_to_all.20.halo, ...), custom_call_target="tpu_custom_call" | custom-call | tf_op jit(solution)/shard_map/layer_one/pallas_call | solution.py:509
  96.6 4.6 %all-to-all-start.1 = ((bf16[128,32,128]{2,1,0:T(8,128)(2,1)}), bf16[128,32,128]{2,1,0:T(8,128)(2,1)S(1)}, u32[]{:S(2)}, u32[]{:S(2)}) async-start(bf16[128,32,128]{2,1,0:T(8,128)(2,1)} %bitcast.27), calls=%async_computation.1 | async-start | bytes 2097152 | tf_op jit(solution)/shard_map/all_to_all | solution.py:533
  102.2 2.0 copy.20.label
  104.1 0.9 pad.4.clone.w
  105.7 17.9 %count_all.1 = f32[5,8,128]{2,1,0:T(8,128)S(1)} custom-call(f32[8,128]{1,0:T(8,128)S(1)} %broadcast_in_dim.29.x), custom_call_target="tpu_custom_call" | custom-call | tf_op jit(solution)/shard_map/count_all/pallas_call | solution.py:456
  124.7 1.0 copy-done.1
  125.7 51.7 %layer_two.1 = (bf16[4096,256]{1,0:T(8,128)(2,1)}, f32[256,1024]{1,0:T(8,128)}) custom-call(s32[32768]{0:T(1024)} %bitcast.26, f32[1]{0:T(128)} %bitcast.5.inv_total, f32[4096,8]{1,0:T(8,128)} %get-tuple-element.11.wt, bf16[4096,1024]{1,0:T(8,128)(2,1)} %get-tuple-element.14.own.h, bf16[4096,128]{1,0:T(8,128)(2,1)} %bitcast.23, ...), custom_call_target="tpu_custom_call" | custom-call | tf_op jit(solution)/shard_map/layer_two/pallas_call | solution.py:536
  177.5 45.5 %scatter.1.own = f32[9216,128]{1,0:T(8,128)} custom-call(s32[32768]{0:T(1024)} %bitcast.28, f32[4096,8]{1,0:T(8,128)} %get-tuple-element.11.wt, bf16[4096,256]{1,0:T(8,128)(2,1)} %get-tuple-element.16.grad), custom_call_target="tpu_custom_call" | custom-call | tf_op jit(solution)/shard_map/scatter/pallas_call | solution.py:546
  223.0 1.9 slice_bitcast_fusion.1
  224.9 6.3 %all-to-all-start.2 = ((f32[128,8,128]{2,1,0:T(8,128)}), f32[128,8,128]{2,1,0:T(8,128)S(1)}, u32[]{:S(2)}, u32[]{:S(2)}) async-start(f32[128,8,128]{2,1,0:T(8,128)} %slice_bitcast_fusion.1), calls=%async_computation.2 | async-start | bytes 1048576 | tf_op jit(solution)/shard_map/all_to_all | solution.py:558
  232.0 0.8 pad_bitcast_fusion.w_t
  232.9 11.7 %all-to-all-done.2 = f32[128,8,128]{2,1,0:T(8,128)S(1)} async-done(((f32[128,8,128]{2,1,0:T(8,128)}), f32[128,8,128]{2,1,0:T(8,128)S(1)}, u32[]{:S(2)}, u32[]{:S(2)}) %all-to-all-start.2) | async-done | bytes 524320 | tf_op jit(solution)/shard_map/all_to_all | solution.py:558
  244.6 0.8 copy-done.2
  245.4 25.3 %backward.1.x = f32[1024,1024]{1,0:T(8,128)} custom-call(s32[512]{0:T(512)} %mul.30.lists, f32[9216,128]{1,0:T(8,128)} %scatter.1.own, f32[1024,128]{1,0:T(8,128)} %bitcast.24, bf16[256,1024]{1,0:T(8,128)(2,1)} %pad_bitcast_fusion.w_t, f32[256,1024]{1,0:T(8,128)} %get-tuple-element.17.gw_two, bf16[4096,1024]{1,0:T(8,128)(2,1)} %get-tuple-element.14.own.h, ...), custom_call_target="tpu_custom_call" | custom-call | tf_op jit(solution)/shard_map/backward/pallas_call | solution.py:559
  270.7 2.2 copy-done
  272.9 43.7 %reduce_all.1 = f32[1024,1024]{1,0:T(8,128)S(1)} custom-call(f32[1024,1024]{1,0:T(8,128)S(1)} %copy-done), custom_call_target="tpu_custom_call" | custom-call | tf_op jit(solution)/shard_map/reduce_all/pallas_call | solution.py:403
  317.0 0.9 slice_bitcast_fusion
  317.9 2.1 slice.18
  (40 shorter events, 7.3 us)
Async XLA Ops:
  8.4 14.5 %copy-start.4 = (s32[4096,8]{0,1:T(8,128)S(1)}, s32[4096,8]{0,1:T(8,128)}, u32[]{:S(2)}) copy-start(s32[4096,8]{0,1:T(8,128)} %param.14) | copy-start | bytes 393220
  8.4 15.2 %copy-start.5 = (s32[4096]{0:T(1024)S(1)}, s32[4096]{0:T(1024)}, u32[]{:S(2)}) copy-start(s32[4096]{0:T(1024)} %param.17) | copy-start | bytes 49156
  9.9 27.7 %all-to-all-start = ((bf16[128,4,768]{2,1,0:T(4,128)(2,1)}), bf16[128,4,768]{2,1,0:T(4,128)(2,1)S(1)}, u32[]{:S(2)}, u32[]{:S(2)}) async-start(bf16[128,4,768]{2,1,0:T(4,128)(2,1)} %broadcast_select_fusion), calls=%async_computation | async-start | bytes 1572864 | tf_op jit(solution)/shard_map/all_to_all | solution.py:488
  38.7 63.2 %copy-start.3 = (f32[1024,153]{0,1:T(8,128)S(1)}, f32[1024,153]{0,1:T(8,128)}, u32[]{:S(2)}) copy-start(f32[1024,153]{0,1:T(8,128)} %param.11) | copy-start | bytes 1880068
  96.6 5.5 %copy-start.6 = (s32[4096]{0:T(1024)S(1)}, s32[4096]{0:T(1024)}, u32[]{:S(2)}) copy-start(s32[4096]{0:T(1024)} %param.17) | copy-start | bytes 49156
  96.6 5.5 %copy-start.7 = (s32[4096]{0:T(1024)S(1)}, s32[4096]{0:T(1024)}, u32[]{:S(2)}) copy-start(s32[4096]{0:T(1024)} %param.16) | copy-start | bytes 49156
  96.6 28.1 %all-to-all-start.1 = ((bf16[128,32,128]{2,1,0:T(8,128)(2,1)}), bf16[128,32,128]{2,1,0:T(8,128)(2,1)S(1)}, u32[]{:S(2)}, u32[]{:S(2)}) async-start(bf16[128,32,128]{2,1,0:T(8,128)(2,1)} %bitcast.27), calls=%async_computation.1 | async-start | bytes 2097152 | tf_op jit(solution)/shard_map/all_to_all | solution.py:533
  124.7 1.0 copy-start.1
  177.5 53.7 %copy-start.8 = (s32[128,4]{0,1:T(4,128)S(1)}, s32[128,4]{0,1:T(4,128)}, u32[]{:S(2)}) copy-start(s32[128,4]{0,1:T(4,128)} %param.12) | copy-start | bytes 6148
  177.5 53.7 %copy-start.9 = (s32[128]{0:T(128)S(1)}, s32[128]{0:T(128)}, u32[]{:S(2)}) copy-start(s32[128]{0:T(128)} %param.13) | copy-start | bytes 1540
  224.9 19.7 %all-to-all-start.2 = ((f32[128,8,128]{2,1,0:T(8,128)}), f32[128,8,128]{2,1,0:T(8,128)S(1)}, u32[]{:S(2)}, u32[]{:S(2)}) async-start(f32[128,8,128]{2,1,0:T(8,128)} %slice_bitcast_fusion.1), calls=%async_computation.2 | async-start | bytes 1048576 | tf_op jit(solution)/shard_map/all_to_all | solution.py:558
  244.6 0.8 copy-start.2
  270.7 2.2 copy-start

commit v4 on v3

--- a/solution.py
+++ b/solution.py
@@ -60,14 +60,6 @@
     lax.fori_loop(0, steps, step, 0)
 
 
-def load_sources(src_hbm, src, sems):
-    n = src[0].shape[0]
-    copies = [pltpu.make_async_copy(src_hbm.at[pl.ds(k * n, n)], ref, sems.at[k]) for k, ref in enumerate(src)]
-    for copy in copies:
-        copy.start()
-    return copies
-
-
 def fill_tiles(dst, src, offset):
     def step(i, carry):
         at = pl.multiple_of(i * 128, 128)
@@ -77,11 +69,11 @@
     lax.fori_loop(0, src.shape[0] // 128, step, 0)
 
 
-def layer_one_kernel(lists, list_ok, src_hbm, feats, halo, wt_t, w_f32, z_out, h_out, wt_out, second,
-                     table, zbuf, wbuf, w, chunk, list_wt, src_sem, chunk_sem, *src):
+def layer_one_kernel(deg, lists, *refs):
+    src, (feats, halo, wt_t, w_f32, z_out, h_out, wt_out, second, table, zbuf, wbuf, w, list_wt) = refs[:deg], refs[deg:]
     g = pl.program_id(0)
     rows, blocks = z_out.shape[0], feats.shape[1] // LANES
-    n, deg = wt_out.shape
+    n = wt_out.shape[0]
 
     def aggregate():
         return jnp.concatenate([zbuf[pl.ds(c, rows, stride=8), :] for c in range(blocks)], axis=1).astype(BF16)
@@ -91,14 +83,6 @@
 
     @pl.when(g == 0)
     def _():
-        index_copies = load_sources(src_hbm, src, src_sem)
-
-        def fetch(i):
-            slot = lax.rem(i, 2)
-            return pltpu.make_async_copy(feats.at[pl.ds(pl.multiple_of(i * rows, rows), rows), :], chunk.at[slot], chunk_sem.at[slot])
-
-        fetch(0).start()
-
         def turn(i, carry):
             at = pl.ds(pl.multiple_of(i * LANES, LANES), LANES)
             wt_out[at, :] = wt_t[:, at].T
@@ -108,34 +92,15 @@
         w[...] = w_f32[...].astype(BF16)
         fill_rows(table, halo, n, blocks)
 
-        def take(i, carry):
-            @pl.when(i + 1 < n // rows)
-            def _():
-                fetch(i + 1).start()
-
-            fetch(i).wait()
-            slot = lax.rem(i, 2)
-
-            def fill(j, carry):
-                r = pl.multiple_of(j * 64, 64)
-                x = chunk[slot, pl.ds(r, 64), :].astype(F32)
-                for c in range(blocks):
-                    table[pl.ds((i * rows + r) * 8 + c, 64, stride=8), :] = x[:, c * LANES : (c + 1) * LANES]
-                return carry
-
-            return lax.fori_loop(0, rows // 64, fill, carry)
-
-        lax.fori_loop(0, n // rows, take, 0)
+        fill_rows(table, feats, 0, blocks)
 
         def pick(i, carry):
             for u in range(8):
                 j = i * 8 + u
-                list_wt[pl.ds(j, 1), :] = wt_out[pl.ds(lists[j], 1), :] * list_ok[j]
+                list_wt[pl.ds(j, 1), :] = wt_out[pl.ds(lists[j], 1), :]
             return carry
 
         lax.fori_loop(0, rows // 8, pick, 0)
-        for copy in index_copies:
-            copy.wait()
         gather_rows(rows // STEP, lambda j: lists[j], src, list_wt, table, zbuf, wbuf)
         h = hidden(aggregate())
         for c in range(h.shape[1] // LANES):
@@ -151,17 +116,15 @@
         h_out[...] = hidden(z).astype(BF16)
 
 
-def layer_two_kernel(classes, src_hbm, inv_total, wt, own, halo, w, label, g_out, gw_out, table, zbuf, wbuf, loss_sum, src_sem, *src):
+def layer_two_kernel(classes, deg, inv_total, *refs):
+    src, (wt, own, halo, w, label, g_out, gw_out, table, zbuf, wbuf, loss_sum) = refs[:deg], refs[deg:]
     g = pl.program_id(0)
     rows, blocks = g_out.shape[0], own.shape[1] // LANES
 
     @pl.when(g == 0)
     def _():
-        index_copies = load_sources(src_hbm, src, src_sem)
         fill_rows(table, own, 0, blocks)
         fill_tiles(table, halo, own.shape[0])
-        for copy in index_copies:
-            copy.wait()
         gw_out[...] = jnp.zeros_like(gw_out)
         loss_sum[...] = jnp.zeros_like(loss_sum)
 
@@ -189,16 +152,14 @@
         gw_out[pl.ds(gw_out.shape[0] - 1, 1), pl.ds(0, LANES)] = jnp.broadcast_to(total, (1, LANES))
 
 
-def scatter_kernel(src_hbm, wt, grad, s_out, gbuf, wbuf, src_sem, *refs):
+def scatter_kernel(deg, *refs):
+    src, (wt, grad, s_out, gbuf, wbuf), parts = refs[:deg], refs[deg : deg + 5], refs[deg + 5 :]
     g = pl.program_id(0)
-    rows, deg = grad.shape[0], wt.shape[1]
-    src, parts = refs[:deg], refs[deg:]
+    rows = grad.shape[0]
     steps = rows // STEP
 
     @pl.when(g == 0)
     def _():
-        index_copies = load_sources(src_hbm, src, src_sem)
-
         def clear(i, carry):
             for part in parts:
                 for j in range(8):
@@ -206,8 +167,6 @@
             return carry
 
         lax.fori_loop(0, s_out.shape[0] // 64, clear, 0)
-        for copy in index_copies:
-            copy.wait()
 
     x = grad[...].astype(F32)
     for c in range(2):
@@ -288,12 +247,14 @@
 COLORS = ((0, 384, (0, 1, 2)), (384, 384, (1, 2, 0)), (768, 256, (2, 0, 1)))
 
 
-def reduce_kernel(x, out, acc, pair_buf, far, mid, near, *sems):
-    pair_send, pair_recv, rs_send, rs_recv, ag_send, ag_recv, back_send, back_recv = sems
+def reduce_kernel(x, out, acc, pair_buf, relay, far, mid, near, *sems):
+    pair_send, pair_recv, ring_send, ring_recv, rs_send, rs_recv, ag_send, ag_recv, back_send, back_recv = sems
     me = lax.axis_index("graph")
     core = lax.rem(me, 2)
     where = [lax.rem(me // (2 * SIDE**d), SIDE) for d in range(3)]
     partner = me + 1 - 2 * core
+    half = acc.shape[0]
+    big = half // SIDE
 
     def peer(axis, t):
         p = lax.rem(where[axis] + t, SIDE)
@@ -305,95 +266,112 @@
         for t in range(1, SIDE):
             pl.semaphore_signal(barrier, inc=1, device_id=(peer(axis, t)[1],), device_id_type=MESH)
     pl.semaphore_wait(barrier, 10)
-
-    def remote(src, dst, send, recv, dev):
-        return pltpu.make_async_remote_copy(src_ref=src, dst_ref=dst, send_sem=send, recv_sem=recv, device_id=(dev,), device_id_type=MESH)
-
     pending = []
-    base = pl.multiple_of(core * 512, 512)
-    other = pl.multiple_of(512 - core * 512, 512)
-    order = (2, 1, 3, 0)
+
+    def send(src, dst, send_sem, recv_sem, dev):
+        copy = pltpu.make_async_remote_copy(
+            src_ref=src, dst_ref=dst, send_sem=send_sem, recv_sem=recv_sem, device_id=(dev,), device_id_type=MESH
+        )
+        copy.start()
+        pending.append(copy)
+        return copy
+
+    base, other = pl.multiple_of(core * half, 8), pl.multiple_of(half - core * half, 8)
+    colors = [(pl.ds(lane, width), axes) for lane, width, axes in COLORS]
+
+    def piece(c, t, part, start=0):
+        p, _ = peer(colors[c][1][0], t)
+        return pl.ds(pl.multiple_of(start + p * big + part * (big // 2), 8), big // 2)
+
+    order = ((2, 0), (2, 1), (1, 1), (3, 0), (1, 0), (3, 1), (0, 0), (0, 1))
     pair = {}
-    for t in order:
-        for c, (lane, width, axes) in enumerate(COLORS):
-            p = lax.rem(where[axes[0]] + t, SIDE)
-            rows = pl.ds(pl.multiple_of(p * 128, 128), 128)
-            copy = remote(x.at[pl.ds(pl.multiple_of(other + p * 128, 128), 128), pl.ds(lane, width)], pair_buf.at[rows, pl.ds(lane, width)], pair_send.at[c, t], pair_recv.at[c, t], partner)
-            copy.start()
-            pair[c, t] = copy
-            pending.append(copy)
-    first = {}
-    for t in order:
-        for c, (lane, width, axes) in enumerate(COLORS):
-            p, dev = peer(axes[0], t)
-            rows = pl.ds(pl.multiple_of(p * 128, 128), 128)
-            lanes = pl.ds(lane, width)
-            pair[c, t].wait_recv()
-            acc[rows, lanes] = x[pl.ds(pl.multiple_of(base + p * 128, 128), 128), lanes] + pair_buf[rows, lanes]
-            if t:
-                copy = remote(acc.at[rows, lanes], far.at[t - 1, :, lanes], rs_send.at[0, c, t - 1], rs_recv.at[0, c, t - 1], dev)
-                copy.start()
-                first[c, t] = copy
-                pending.append(copy)
+    for t, part in order:
+        for c, (lanes, _) in enumerate(colors):
+            at = piece(c, t, part)
+            pair[c, t, part] = send(
+                x.at[piece(c, t, part, other), lanes], pair_buf.at[at, lanes], pair_send.at[c, t * 2 + part], pair_recv.at[c, t * 2 + part], partner
+            )
+    ring = {}
+    for t, part in order:
+        for c, (lanes, axes) in enumerate(colors):
+            at = piece(c, t, part)
+            pair[c, t, part].wait_recv()
+            mine = x[piece(c, t, part, base), lanes] + pair_buf[at, lanes]
+            if (t, part) in ((1, 0), (3, 1)):
+                ring[c, 2, part].wait_recv()
+                mine = mine + relay[part, :, lanes]
+            acc[at, lanes] = mine
+            if t == 0:
+                continue
+            forward = part == 0 if t == 2 else t == 1
+            _, dev = peer(axes[0], 1 if forward else 3)
+            if t == 2:
+                dst = relay.at[part, :, lanes]
+            else:
+                dst = far.at[0 if forward else 1, pl.ds(part * (big // 2), big // 2), lanes]
+            slot = order.index((t, part))
+            ring[c, t, part] = send(acc.at[at, lanes], dst, ring_send.at[0, c, slot], ring_recv.at[0, c, slot], dev)
     start = [0, 0, 0]
-    for stage, (size, buf) in enumerate(((128, far), (32, mid), (8, near))):
-        if stage:
-            first = {}
-            for c, (lane, width, axes) in enumerate(COLORS):
-                for t in (2, 1, 3):
-                    p, dev = peer(axes[stage], t)
-                    rows = pl.ds(pl.multiple_of(start[c] + p * size, 8), size)
-                    copy = remote(acc.at[rows, pl.ds(lane, width)], buf.at[t - 1, :, pl.ds(lane, width)], rs_send.at[stage, c, t - 1], rs_recv.at[stage, c, t - 1], dev)
-                    copy.start()
-                    first[c, t] = copy
-                    pending.append(copy)
-        for c, (lane, width, axes) in enumerate(COLORS):
-            lanes = pl.ds(lane, width)
+    for c, (lanes, axes) in enumerate(colors):
+        start[c] = where[axes[0]] * big
+        for key in ((1, 1), (3, 0), (1, 0), (3, 1)):
+            ring[(c, *key)].wait_recv()
+        rows = pl.ds(pl.multiple_of(start[c], 8), big)
+        acc[rows, lanes] = acc[rows, lanes] + far[0, :, lanes] + far[1, :, lanes]
+    for stage, (size, buf) in enumerate(((big // SIDE, mid), (big // SIDE**2, near)), 1):
+        copies = {}
+        for c, (lanes, axes) in enumerate(colors):
+            for t in (2, 1, 3):
+                p, dev = peer(axes[stage], t)
+                rows = pl.ds(pl.multiple_of(start[c] + p * size, 8), size)
+                sem = (stage - 1, c, t - 1)
+                copies[c, t] = send(acc.at[rows, lanes], buf.at[t - 1, :, lanes], rs_send.at[sem], rs_recv.at[sem], dev)
+        for c, (lanes, axes) in enumerate(colors):
             start[c] = start[c] + where[axes[stage]] * size
             rows = pl.ds(pl.multiple_of(start[c], 8), size)
             for t in (1, 2, 3):
-                first[c, t].wait_recv()
+                copies[c, t].wait_recv()
             mine = acc[rows, lanes] + buf[0, :, lanes] + buf[1, :, lanes] + buf[2, :, lanes]
-            if stage < 2:
+            if stage == 1:
                 acc[rows, lanes] = mine
             else:
                 out[pl.ds(pl.multiple_of(base + start[c], 8), size), lanes] = mine
-    for stage, size in ((2, 8), (1, 32), (0, 128)):
+    for stage, size in ((2, big // SIDE**2), (1, big // SIDE)):
         copies = {}
-        for c, (lane, width, axes) in enumerate(COLORS):
-            lanes = pl.ds(lane, width)
-            rows = pl.ds(pl.multiple_of(base + start[c], 8), size)
+        for c, (lanes, axes) in enumerate(colors):
+            here = out.at[pl.ds(pl.multiple_of(base + start[c], 8), size), lanes]
             for t in (2, 1, 3):
                 _, dev = peer(axes[stage], t)
-                copy = remote(out.at[rows, lanes], out.at[rows, lanes], ag_send.at[stage, c, t - 1], ag_recv.at[stage, c, t - 1], dev)
-                copy.start()
-                copies[c, t] = copy
-                pending.append(copy)
-            if stage == 0:
-                copy = remote(out.at[rows, lanes], out.at[rows, lanes], back_send.at[c, 0], back_recv.at[c, 0], partner)
-                copy.start()
-                copies[c, 0] = copy
-                pending.append(copy)
-        if stage:
-            for c, (lane, width, axes) in enumerate(COLORS):
-                for t in (1, 2, 3):
-                    copies[c, t].wait_recv()
-                start[c] = start[c] - where[axes[stage]] * size
-        else:
-            for t in (1, 3, 2):
-                for c, (lane, width, axes) in enumerate(COLORS):
-                    lanes = pl.ds(lane, width)
-                    copies[c, t].wait_recv()
-                    p, _ = peer(axes[0], SIDE - t)
-                    rows = pl.ds(pl.multiple_of(base + p * 128, 128), 128)
-                    copy = remote(out.at[rows, lanes], out.at[rows, lanes], back_send.at[c, t], back_recv.at[c, t], partner)
-                    copy.start()
-                    copies[c, t + 4] = copy
-                    pending.append(copy)
-            for c in range(3):
-                copies[c, 0].wait_recv()
-                for t in (1, 2, 3):
-                    copies[c, t + 4].wait_recv()
+                sem = (stage - 1, c, t - 1)
+                copies[c, t] = send(here, here, ag_send.at[sem], ag_recv.at[sem], dev)
+        for c, (lanes, axes) in enumerate(colors):
+            for t in (1, 2, 3):
+                copies[c, t].wait_recv()
+            start[c] = start[c] - where[axes[stage]] * size
+    got = {}
+
+    def pass_on(c, t, part, slot, directions):
+        here = out.at[piece(c, t, part, base), colors[c][0]]
+        for d, name in directions:
+            _, dev = peer(colors[c][1][0], d)
+            got[c, name] = send(here, here, ring_send.at[1, c, name], ring_recv.at[1, c, name], dev)
+        got[c, slot] = send(here, here, back_send.at[c, slot - 6], back_recv.at[c, slot - 6], partner)
+
+    for c in range(3):
+        pass_on(c, 0, 0, 6, ((1, 0), (3, 3)))
+        pass_on(c, 0, 1, 7, ((3, 2), (1, 1)))
+    for c in range(3):
+        got[c, 0].wait_recv()
+        pass_on(c, 3, 0, 8, ((1, 4),))
+        got[c, 2].wait_recv()
+        pass_on(c, 1, 1, 9, ((3, 5),))
+    for name, (t, part), slot in ((1, (3, 1), 10), (3, (1, 0), 11), (4, (2, 0), 12), (5, (2, 1), 13)):
+        for c in range(3):
+            got[c, name].wait_recv()
+            pass_on(c, t, part, slot, ())
+    for c in range(3):
+        for slot in range(6, 14):
+            got[c, slot].wait_recv()
     for copy in pending:
         copy.wait_send()
 
@@ -403,8 +381,8 @@
     return pl.pallas_call(reduce_kernel,
         in_specs=[pl.BlockSpec(memory_space=pltpu.VMEM)], out_specs=pl.BlockSpec(memory_space=pltpu.VMEM),
         out_shape=jax.ShapeDtypeStruct((1024,1024),F32),
-        scratch_shapes=[pltpu.VMEM((512,1024),F32), pltpu.VMEM((512,1024),F32), pltpu.VMEM((3,128,1024),F32), pltpu.VMEM((3,32,1024),F32), pltpu.VMEM((3,8,1024),F32),
-            sem((3,4)), sem((3,4)), sem((3,3,3)), sem((3,3,3)), sem((3,3,3)), sem((3,3,3)), sem((3,4)), sem((3,4))],
+        scratch_shapes=[pltpu.VMEM((512,1024),F32), pltpu.VMEM((512,1024),F32), pltpu.VMEM((2,64,1024),F32), pltpu.VMEM((2,128,1024),F32), pltpu.VMEM((3,32,1024),F32), pltpu.VMEM((3,8,1024),F32),
+            sem((3,8)), sem((3,8)), sem((2,3,6)), sem((2,3,6)), sem((2,3,3)), sem((2,3,3)), sem((2,3,3)), sem((2,3,3)), sem((3,8)), sem((3,8))],
         compiler_params=pltpu.CompilerParams(collective_id=0, has_side_effects=True, vmem_limit_bytes=40*2**20),
         name="reduce_all")(x)
 
@@ -482,15 +460,17 @@
         ext = n + halo
         pad = 2 * LANES
         w_two_b = jnp.pad(w_two.astype(BF16), ((0, 0), (0, pad - classes)))
-        list_ok = jnp.arange(halo_rows)[None, :] < send_count[:, None]
         list_ids = send_idx.reshape(halo)
-        first_rows = jnp.where(list_ok.reshape(halo, 1), feats[list_ids], 0)
+        lists2 = list_ids * 2
+        src8 = [edge_src[:, k] * 8 for k in range(deg)]
+        src2 = [edge_src[:, k] * 2 for k in range(deg)]
+        count = jnp.sum(label_mask.astype(F32))
+        first_rows, count = lax.optimization_barrier((feats[list_ids], count))
         first_in = lax.all_to_all(first_rows, "graph", 0, 0, tiled=True)
-        lists2 = jnp.where(list_ok, send_idx, n).reshape(halo) * 2
-        src_t = edge_src.T.reshape(deg * n)
-        src8, src2 = src_t * 8, src_t * 2
+        label_total = count_all(jnp.full((8, LANES), count))[4, 0, 0]
+        first_in, label_total = lax.optimization_barrier((first_in, label_total))
+        inv_total = (1.0 / label_total).reshape(1)
         label = jnp.where(label_mask == 1, labels, -1).reshape(n, 1)
-        count = jnp.sum(label_mask.astype(F32))
 
         def by_rows(width):
             return pl.BlockSpec((BLOCK, width), lambda g: (g, 0))
@@ -503,13 +483,10 @@
             pltpu.VMEM((BLOCK * 8, LANES), F32),
             pltpu.VMEM((STEP * deg + 8, LANES), F32),
         ]
-        index_scratch = [pltpu.SMEM((n,), jnp.int32) for _ in range(deg)]
-        whole = pl.BlockSpec(memory_space=pl.ANY)
-        dma = pltpu.SemaphoreType.DMA
         z_one, h_one, wt, second = pl.pallas_call(
-            layer_one_kernel,
+            functools.partial(layer_one_kernel, deg),
             grid=(1 + n // BLOCK,),
-            in_specs=[SMEM, SMEM, whole, whole, once((halo, f_in)), once((deg, n)), once((f_in, f_hid))],
+            in_specs=[SMEM] + [SMEM] * deg + [once((n, f_in)), once((halo, f_in)), once((deg, n)), once((f_in, f_hid))],
             out_specs=[after_first(f_in), after_first(f_hid), once((n, deg)), once((halo * 8, LANES))],
             out_shape=[
                 jax.ShapeDtypeStruct((n, f_in), BF16),
@@ -520,41 +497,33 @@
             scratch_shapes=gather_scratch
             + [
                 pltpu.VMEM((f_in, f_hid), BF16),
-                pltpu.VMEM((2, BLOCK, f_in), BF16),
                 pltpu.VMEM((halo, deg), F32),
-                dma((deg,)),
-                dma((2,)),
-            ]
-            + index_scratch,
+            ],
             compiler_params=params(),
             name="layer_one",
-        )(list_ids, list_ok.reshape(halo).astype(F32), src8, feats, first_in, edge_wt.T, w_one)
-        count, second = lax.optimization_barrier((count, second))
+        )(list_ids, *src8, feats, first_in, edge_wt.T, w_one)
         h_in = lax.all_to_all(second, "graph", 0, 0, tiled=True)
-        label_total = count_all(jnp.full((8, LANES), count))[4, 0, 0]
-        inv_total = (1.0 / label_total).reshape(1)
         grad_log, gw_two = pl.pallas_call(
-            functools.partial(layer_two_kernel, classes),
+            functools.partial(layer_two_kernel, classes, deg),
             grid=(n // BLOCK,),
-            in_specs=[whole, SMEM, by_rows(deg), once((n, f_hid)), once((halo * 8, LANES)), once((f_hid, pad)), by_rows(1)],
+            in_specs=[SMEM] + [SMEM] * deg + [by_rows(deg), once((n, f_hid)), once((halo * 8, LANES)), once((f_hid, pad)), by_rows(1)],
             out_specs=[by_rows(pad), once((pad, f_hid))],
             out_shape=[jax.ShapeDtypeStruct((n, pad), BF16), jax.ShapeDtypeStruct((pad, f_hid), F32)],
-            scratch_shapes=gather_scratch + [pltpu.VMEM((1, pad), F32), dma((deg,))] + index_scratch,
+            scratch_shapes=gather_scratch + [pltpu.VMEM((1, pad), F32)],
             compiler_params=params(),
             name="layer_two",
-        )(src8, inv_total, wt, h_one, h_in, w_two_b, label)
+        )(inv_total, *src8, wt, h_one, h_in, w_two_b, label)
         ext_grad = pl.pallas_call(
-            scatter_kernel,
+            functools.partial(scatter_kernel, deg),
             grid=(n // 512,),
-            in_specs=[whole, by_rows(deg), by_rows(pad)],
+            in_specs=[SMEM] * deg + [by_rows(deg), by_rows(pad)],
             out_specs=once((ext * 2, LANES)),
             out_shape=jax.ShapeDtypeStruct((ext * 2, LANES), F32),
-            scratch_shapes=[pltpu.VMEM((BLOCK * 2, LANES), F32), pltpu.VMEM((STEP * deg + 8, LANES), F32), dma((deg,))]
-            + index_scratch
+            scratch_shapes=[pltpu.VMEM((BLOCK * 2, LANES), F32), pltpu.VMEM((STEP * deg + 8, LANES), F32)]
             + [pltpu.VMEM((ext * 2, LANES), F32) for _ in range(deg)],
             compiler_params=params(),
             name="scatter",
-        )(src2, wt, grad_log)
+        )(*src2, wt, grad_log)
         back = lax.all_to_all(ext_grad[n * 2 :], "graph", 0, 0, tiled=True)
         partial = pl.pallas_call(
             backward_kernel,

time: 323 us -> 344 us (1.065)
  Pallas kernels: 242 us -> 263 us
    pallas_call x3, Pallas kernels: 155 us -> 179 us  [the longest x1 70.2 us: device_step(): pl.pallas_call(functools.partial(layer_one_kernel, deg), grid=(1 + n // B...]
    all_to_all x1, waiting for transfers between devices: 0.01 us -> 14.5 us  [device_step(): h_in = lax.all_to_all(second, 'graph', 0, 0, tiled=True)]
    all_to_all x1, waiting for transfers between devices: 13.5 us -> 0.01 us  [device_step(): first_in = lax.all_to_all(first_rows, 'graph', 0, 0, tiled=True)]
  transfers between devices with their start and end apart: 3 -> 3, of which waited for: 2 -> 2; matrix products, arithmetic and copies ran while one was open for 3% -> 2% of each run, Pallas kernels for 6% -> 5%
where the time goes in v4:
time: 344 us
  Pallas kernels  263 us (76%)
  waiting for transfers between devices  26.6 us (8%)
  local copies, waits for them, and re-layouts  24.1 us (7%)
  starting transfers between devices  22.2 us (6%)
  between operations  3.9 us (1%)
  other arithmetic  3.6 us (1%)
    pallas_call x1, Pallas kernels, device_step(): pl.pallas_call(functools.partial(layer_one_kernel, deg), grid=(1 + n // B...  70.2 us
    pallas_call x1, Pallas kernels, device_step(): pl.pallas_call(functools.partial(layer_two_kernel, classes, deg), grid=(n...  63.3 us
    pallas_call x1, Pallas kernels, device_step(): pl.pallas_call(functools.partial(scatter_kernel, deg), grid=(n // 512,),...  45.1 us
    pallas_call x1, Pallas kernels, reduce_all(): pl.pallas_call(reduce_kernel, in_specs=[pl.BlockSpec(memory_space=pltpu.V...  41.9 us
    pallas_call x1, Pallas kernels, device_step(): pl.pallas_call(backward_kernel, grid=(n // 512,), in_specs=[SMEM, once((n...  24.5 us
    pallas_call x1, Pallas kernels, count_all(): pl.pallas_call(count_kernel, in_specs=[vmem], out_specs=vmem, out_shape=j...  18.2 us
    all_to_all x1, waiting for transfers between devices, device_step(): h_in = lax.all_to_all(second, 'graph', 0, 0, tiled=True)  14.5 us
    all_to_all x1, waiting for transfers between devices, device_step(): back = lax.all_to_all(ext_grad[n * 2:], 'graph', 0, 0, tiled=True)  12.1 us
  transfers between devices with their start and end apart: 3, of which 2 were waited for; matrix products, arithmetic and copies ran while one was open for 2% of the time, Pallas kernels for 5%

profile of v4, /device:TPU:1, one launch (start us, length us, event | category | flops | bytes accessed | tf_op | source)
XLA Modules:
  0.0 343.6 jit_solution(16789756659829452721)
XLA Ops:
  0.6 1.3 convert_reduce_fusion
  2.9 6.0 %gather_fusion = bf16[512,768]{1,0:T(8,128)(2,1)S(1)} fusion(bf16[4096,768]{1,0:T(8,128)(2,1)} %refs_8_.1, s32[1024]{0:T(1024)S(1)} %pad_clamp_fusion), kind=kCustom, calls=%fused_computation | custom fusion | bytes 1574912 | tf_op jit(solution)/shard_map/gather | solution.py:468
  8.9 1.1 all_to_all.22
  10.0 11.5 %all-to-all-start = ((bf16[128,4,768]{2,1,0:T(4,128)(2,1)}), bf16[128,4,768]{2,1,0:T(4,128)(2,1)S(1)}, u32[]{:S(2)}, u32[]{:S(2)}) async-start(bf16[128,4,768]{2,1,0:T(4,128)(2,1)} %all_to_all.22), calls=%async_computation | async-start | bytes 1572864 | tf_op jit(solution)/shard_map/all_to_all | solution.py:469
  22.8 18.2 %count_all.1 = f32[5,8,128]{2,1,0:T(8,128)S(1)} custom-call(f32[8,128]{1,0:T(8,128)S(1)} %broadcast_in_dim.8.x), custom_call_target="tpu_custom_call" | custom-call | tf_op jit(solution)/shard_map/count_all/pallas_call | solution.py:434
  41.5 0.9 slice_multiply_fusion
  42.4 1.1 all_to_all.24.refs_9_
  43.5 70.2 %layer_one.1 = (bf16[4096,768]{1,0:T(8,128)(2,1)}, bf16[4096,1024]{1,0:T(8,128)(2,1)}, f32[4096,8]{1,0:T(8,128)}, bf16[4096,128]{1,0:T(8,128)(2,1)}) custom-call(s32[512]{0:T(512)} %reshape.84.lists, s32[4096]{0:T(1024)} %bitcast.36, s32[4096]{0:T(1024)} %bitcast.38, s32[4096]{0:T(1024)} %bitcast.40, s32[4096]{0:T(1024)} %bitcast.42, s32[4096]{0:T(1024)} %bitcast.44, ...), custom_call_target="tpu_custom_call" | custom-call | tf_op jit(solution)/shard_map/layer_one/pallas_call | solution.py:486
  113.7 6.3 %all-to-all-start.1 = ((bf16[128,32,128]{2,1,0:T(8,128)(2,1)}), bf16[128,32,128]{2,1,0:T(8,128)(2,1)S(1)}, u32[]{:S(2)}, u32[]{:S(2)}) async-start(bf16[128,32,128]{2,1,0:T(8,128)(2,1)} %bitcast.33), calls=%async_computation.1 | async-start | bytes 2097152 | tf_op jit(solution)/shard_map/all_to_all | solution.py:505
  121.0 1.9 copy.15.refs_12_
  123.0 0.9 pad.4.clone.refs_11_
  124.5 14.5 %all-to-all-done.1 = bf16[128,32,128]{2,1,0:T(8,128)(2,1)S(1)} async-done(((bf16[128,32,128]{2,1,0:T(8,128)(2,1)}), bf16[128,32,128]{2,1,0:T(8,128)(2,1)S(1)}, u32[]{:S(2)}, u32[]{:S(2)}) %all-to-all-start.1) | async-done | bytes 1048608 | tf_op jit(solution)/shard_map/all_to_all | solution.py:505
  139.0 1.0 copy-done.1
  140.0 63.3 %layer_two.1 = (bf16[4096,256]{1,0:T(8,128)(2,1)}, f32[256,1024]{1,0:T(8,128)}) custom-call(f32[1]{0:T(128)} %bitcast.19.inv_total, s32[4096]{0:T(1024)} %bitcast.37, s32[4096]{0:T(1024)} %bitcast.39, s32[4096]{0:T(1024)} %bitcast.41, s32[4096]{0:T(1024)} %bitcast.43, s32[4096]{0:T(1024)} %bitcast.45, s32[4096]{0:T(1024)} %bitcast.47, s32[4096]{0:T(1024)} %bitcast.49, ...), custom_call_target="tpu_custom_call" | custom-call | tf_op jit(solution)/shard_map/layer_two/pallas_call | solution.py:506
  203.4 45.1 %scatter.1.own = f32[9216,128]{1,0:T(8,128)} custom-call(s32[4096]{0:T(1024)} %bitcast.56, s32[4096]{0:T(1024)} %bitcast.55, s32[4096]{0:T(1024)} %bitcast.54, s32[4096]{0:T(1024)} %bitcast.53, s32[4096]{0:T(1024)} %bitcast.52, s32[4096]{0:T(1024)} %bitcast.51, s32[4096]{0:T(1024)} %bitcast.58, s32[4096]{0:T(1024)} %bitcast.57, ...), custom_call_target="tpu_custom_call" | custom-call | tf_op jit(solution)/shard_map/scatter/pallas_call | solution.py:516
  248.5 1.9 slice_bitcast_fusion.1
  250.3 4.4 %all-to-all-start.2 = ((f32[128,8,128]{2,1,0:T(8,128)}), f32[128,8,128]{2,1,0:T(8,128)S(1)}, u32[]{:S(2)}, u32[]{:S(2)}) async-start(f32[128,8,128]{2,1,0:T(8,128)} %slice_bitcast_fusion.1), calls=%async_computation.2 | async-start | bytes 1048576 | tf_op jit(solution)/shard_map/all_to_all | solution.py:527
  254.7 0.8 pad_bitcast_fusion.w_t
  256.2 12.1 %all-to-all-done.2 = f32[128,8,128]{2,1,0:T(8,128)S(1)} async-done(((f32[128,8,128]{2,1,0:T(8,128)}), f32[128,8,128]{2,1,0:T(8,128)S(1)}, u32[]{:S(2)}, u32[]{:S(2)}) %all-to-all-start.2) | async-done | bytes 524320 | tf_op jit(solution)/shard_map/all_to_all | solution.py:527
  269.0 24.5 %backward.1.x = f32[1024,1024]{1,0:T(8,128)} custom-call(s32[512]{0:T(512)} %broadcast_multiply_fusion.lists, f32[9216,128]{1,0:T(8,128)} %scatter.1.own, f32[1024,128]{1,0:T(8,128)} %bitcast.32, bf16[256,1024]{1,0:T(8,128)(2,1)} %pad_bitcast_fusion.w_t, f32[256,1024]{1,0:T(8,128)} %get-tuple-element.21.gw_two, ...), custom_call_target="tpu_custom_call" | custom-call | tf_op jit(solution)/shard_map/backward/pallas_call | solution.py:528
  293.6 2.2 copy-done
  295.8 41.9 %reduce_all.1 = f32[1024,1024]{1,0:T(8,128)S(1)} custom-call(f32[1024,1024]{1,0:T(8,128)S(1)} %copy-done), custom_call_target="tpu_custom_call" | custom-call | tf_op jit(solution)/shard_map/reduce_all/pallas_call | solution.py:381
  338.2 0.9 slice_bitcast_fusion
  339.1 2.1 slice.58
  (23 shorter events, 5.7 us)
Async XLA Ops:
  2.9 38.6 %copy-start.4 = (s32[4096,8]{0,1:T(8,128)S(1)}, s32[4096,8]{0,1:T(8,128)}, u32[]{:S(2)}) copy-start(s32[4096,8]{0,1:T(8,128)} %param.13) | copy-start | bytes 393220
  10.0 32.4 %all-to-all-start = ((bf16[128,4,768]{2,1,0:T(4,128)(2,1)}), bf16[128,4,768]{2,1,0:T(4,128)(2,1)S(1)}, u32[]{:S(2)}, u32[]{:S(2)}) async-start(bf16[128,4,768]{2,1,0:T(4,128)(2,1)} %all_to_all.22), calls=%async_computation | async-start | bytes 1572864 | tf_op jit(solution)/shard_map/all_to_all | solution.py:469
  43.5 76.5 %copy-start.3 = (f32[1024,153]{0,1:T(8,128)S(1)}, f32[1024,153]{0,1:T(8,128)}, u32[]{:S(2)}) copy-start(f32[1024,153]{0,1:T(8,128)} %param.11) | copy-start | bytes 1880068
  113.7 25.3 %all-to-all-start.1 = ((bf16[128,32,128]{2,1,0:T(8,128)(2,1)}), bf16[128,32,128]{2,1,0:T(8,128)(2,1)S(1)}, u32[]{:S(2)}, u32[]{:S(2)}) async-start(bf16[128,32,128]{2,1,0:T(8,128)(2,1)} %bitcast.33), calls=%async_computation.1 | async-start | bytes 2097152 | tf_op jit(solution)/shard_map/all_to_all | solution.py:505
  139.0 1.0 copy-start.1
  203.4 52.2 %copy-start.5 = (s32[512]{0:T(512)S(1)}, s32[512]{0:T(512)}, u32[]{:S(2)}) copy-start(s32[512]{0:T(512)} %reshape.84.lists) | copy-start | bytes 6148
  250.3 17.9 %all-to-all-start.2 = ((f32[128,8,128]{2,1,0:T(8,128)}), f32[128,8,128]{2,1,0:T(8,128)S(1)}, u32[]{:S(2)}, u32[]{:S(2)}) async-start(f32[128,8,128]{2,1,0:T(8,128)} %slice_bitcast_fusion.1), calls=%async_computation.2 | async-start | bytes 1048576 | tf_op jit(solution)/shard_map/all_to_all | solution.py:527
  268.2 0.8 copy-start.2
  293.6 2.2 copy-start

commit v5 on v4

--- a/solution.py
+++ b/solution.py
@@ -8,6 +8,7 @@
 from jax.sharding import PartitionSpec as P
 
 LANES = 128
+TAIL = 32
 STEP = 16
 BLOCK = 512
 F32, BF16 = jnp.float32, jnp.bfloat16
@@ -60,6 +61,13 @@
     lax.fori_loop(0, steps, step, 0)
 
 
+def load_sources(src_hbm, src, sems):
+    copies = [pltpu.make_async_copy(hbm, ref, sems.at[k]) for k, (hbm, ref) in enumerate(zip(src_hbm, src))]
+    for copy in copies:
+        copy.start()
+    return copies
+
+
 def fill_tiles(dst, src, offset):
     def step(i, carry):
         at = pl.multiple_of(i * 128, 128)
@@ -69,64 +77,100 @@
     lax.fori_loop(0, src.shape[0] // 128, step, 0)
 
 
-def layer_one_kernel(deg, lists, *refs):
-    src, (feats, halo, wt_t, w_f32, z_out, h_out, wt_out, second, table, zbuf, wbuf, w, list_wt) = refs[:deg], refs[deg:]
+def fill_from(table, hbm, chunk, sems, blocks):
+    rows = chunk.shape[1]
+    steps = hbm.shape[0] // rows
+
+    def fetch(i):
+        slot = lax.rem(i, 2)
+        return pltpu.make_async_copy(hbm.at[pl.ds(pl.multiple_of(i * rows, rows), rows), :], chunk.at[slot], sems.at[slot])
+
+    fetch(0).start()
+
+    def take(i, carry):
+        @pl.when(i + 1 < steps)
+        def _():
+            fetch(i + 1).start()
+
+        fetch(i).wait()
+        slot = lax.rem(i, 2)
+
+        def fill(j, carry):
+            r = pl.multiple_of(j * 64, 64)
+            x = chunk[slot, pl.ds(r, 64), :].astype(F32)
+            for c in range(blocks):
+                table[pl.ds((i * rows + r) * 8 + c, 64, stride=8), :] = x[:, c * LANES : (c + 1) * LANES]
+            return carry
+
+        return lax.fori_loop(0, rows // 64, fill, carry)
+
+    lax.fori_loop(0, steps, take, 0)
+
+
+def first_layer(zbuf, w, rows, blocks):
+    z = jnp.concatenate([zbuf[pl.ds(c, rows, stride=8), :] for c in range(blocks)], axis=1).astype(BF16)
+    return z, jnp.maximum(jnp.dot(z, w[...], preferred_element_type=F32), 0.0)
+
+
+def list_rows_kernel(deg, lists, *refs):
+    src_hbm, refs, src = refs[:deg], refs[deg:-deg], refs[-deg:]
+    feats, halo, wt, w, second, table, zbuf, wbuf, list_wt, chunk, src_sem, chunk_sem = refs
+    rows, blocks = list_wt.shape[0], feats.shape[1] // LANES
+    index_copies = load_sources(src_hbm, src, src_sem)
+    fill_rows(table, halo, feats.shape[0], blocks)
+    fill_from(table, feats, chunk, chunk_sem, blocks)
+
+    def pick(i, carry):
+        for u in range(8):
+            j = i * 8 + u
+            list_wt[pl.ds(j, 1), :] = wt[pl.ds(lists[j], 1), :]
+        return carry
+
+    lax.fori_loop(0, rows // 8, pick, 0)
+    for copy in index_copies:
+        copy.wait()
+    gather_rows(rows // STEP, lambda j: lists[j], src, list_wt, table, zbuf, wbuf)
+    _, h = first_layer(zbuf, w, rows, blocks)
+    for c in range(h.shape[1] // LANES):
+        zbuf[pl.ds(c, rows, stride=8), :] = h[:, c * LANES : (c + 1) * LANES]
+    second[...] = zbuf[...].astype(BF16)
+
+
+def layer_one_kernel(deg, *refs):
+    src_hbm, refs, src = refs[:deg], refs[deg:-deg], refs[-deg:]
+    feats, halo, wt, w, z_out, h_out, table, zbuf, wbuf, chunk, src_sem, chunk_sem = refs
     g = pl.program_id(0)
     rows, blocks = z_out.shape[0], feats.shape[1] // LANES
-    n = wt_out.shape[0]
-
-    def aggregate():
-        return jnp.concatenate([zbuf[pl.ds(c, rows, stride=8), :] for c in range(blocks)], axis=1).astype(BF16)
-
-    def hidden(z):
-        return jnp.maximum(jnp.dot(z, w[...], preferred_element_type=F32), 0.0)
 
     @pl.when(g == 0)
     def _():
-        def turn(i, carry):
-            at = pl.ds(pl.multiple_of(i * LANES, LANES), LANES)
-            wt_out[at, :] = wt_t[:, at].T
-            return carry
-
-        lax.fori_loop(0, n // LANES, turn, 0)
-        w[...] = w_f32[...].astype(BF16)
-        fill_rows(table, halo, n, blocks)
-
-        fill_rows(table, feats, 0, blocks)
-
-        def pick(i, carry):
-            for u in range(8):
-                j = i * 8 + u
-                list_wt[pl.ds(j, 1), :] = wt_out[pl.ds(lists[j], 1), :]
-            return carry
-
-        lax.fori_loop(0, rows // 8, pick, 0)
-        gather_rows(rows // STEP, lambda j: lists[j], src, list_wt, table, zbuf, wbuf)
-        h = hidden(aggregate())
-        for c in range(h.shape[1] // LANES):
-            zbuf[pl.ds(c, rows, stride=8), :] = h[:, c * LANES : (c + 1) * LANES]
-        second[...] = zbuf[...].astype(BF16)
-
-    @pl.when(g > 0)
-    def _():
-        first_row = pl.multiple_of((g - 1) * rows, rows)
-        gather_rows(rows // STEP, lambda j: first_row + j, src, wt_out.at[pl.ds(first_row, rows)], table, zbuf, wbuf)
-        z = aggregate()
-        z_out[...] = z
-        h_out[...] = hidden(z).astype(BF16)
+        index_copies = load_sources(src_hbm, src, src_sem)
+        fill_rows(table, halo, feats.shape[0], blocks)
+        fill_from(table, feats, chunk, chunk_sem, blocks)
+        for copy in index_copies:
+            copy.wait()
+
+    first_row = pl.multiple_of(g * rows, rows)
+    gather_rows(rows // STEP, lambda j: first_row + j, src, wt, table, zbuf, wbuf)
+    z, h = first_layer(zbuf, w, rows, blocks)
+    z_out[...] = z
+    h_out[...] = h.astype(BF16)
 
 
 def layer_two_kernel(classes, deg, inv_total, *refs):
-    src, (wt, own, halo, w, label, g_out, gw_out, table, zbuf, wbuf, loss_sum) = refs[:deg], refs[deg:]
+    src_hbm, refs, src = refs[:deg], refs[deg:-deg], refs[-deg:]
+    wt, own, halo, w, label, g_out, z_out, loss_out, table, zbuf, wbuf, loss_sum, chunk, src_sem, chunk_sem = refs
     g = pl.program_id(0)
     rows, blocks = g_out.shape[0], own.shape[1] // LANES
 
     @pl.when(g == 0)
     def _():
-        fill_rows(table, own, 0, blocks)
+        index_copies = load_sources(src_hbm, src, src_sem)
+        loss_sum[...] = jnp.zeros_like(loss_sum)
         fill_tiles(table, halo, own.shape[0])
-        gw_out[...] = jnp.zeros_like(gw_out)
-        loss_sum[...] = jnp.zeros_like(loss_sum)
+        fill_from(table, own, chunk, chunk_sem, blocks)
+        for copy in index_copies:
+            copy.wait()
 
     first_row = g * rows
     gather_rows(rows // STEP, lambda j: first_row + j, src, wt, table, zbuf, wbuf)
@@ -144,22 +188,38 @@
     scale = jnp.where(tag >= 0, inv_total[0], 0.0)
     grad = jnp.where(real, (jnp.exp(log_prob) - jnp.where(hit, 1.0, 0.0)) * scale, 0.0).astype(BF16)
     g_out[...] = grad
-    gw_out[...] += lax.dot_general(grad, z, (((0,), (0,)), ((), ())), preferred_element_type=F32)
+    z_out[...] = z
 
     @pl.when(g == pl.num_programs(0) - 1)
     def _():
-        total = jnp.sum(loss_sum[...], axis=1, keepdims=True)
-        gw_out[pl.ds(gw_out.shape[0] - 1, 1), pl.ds(0, LANES)] = jnp.broadcast_to(total, (1, LANES))
+        loss_out[...] = jnp.broadcast_to(jnp.sum(loss_sum[...], axis=1, keepdims=True), loss_out.shape)
+
+
+def grad_two_kernel(grad, z, loss, gw_out):
+    g = pl.program_id(0)
+
+    @pl.when(g == 0)
+    def _():
+        gw_out[...] = jnp.zeros_like(gw_out)
+
+    gw_out[...] += lax.dot_general(grad[...], z[...], (((0,), (0,)), ((), ())), preferred_element_type=F32)
+
+    @pl.when(g == pl.num_programs(0) - 1)
+    def _():
+        gw_out[pl.ds(gw_out.shape[0] - 1, 1), pl.ds(0, LANES)] = loss[...]
 
 
 def scatter_kernel(deg, *refs):
-    src, (wt, grad, s_out, gbuf, wbuf), parts = refs[:deg], refs[deg : deg + 5], refs[deg + 5 :]
+    src_hbm, (wt, grad, s_out, gbuf, wbuf, sems), refs = refs[:deg], refs[deg : deg + 6], refs[deg + 6 :]
+    src, parts = refs[:deg], refs[deg:]
     g = pl.program_id(0)
     rows = grad.shape[0]
     steps = rows // STEP
 
     @pl.when(g == 0)
     def _():
+        index_copies = load_sources(src_hbm, src, sems)
+
         def clear(i, carry):
             for part in parts:
                 for j in range(8):
@@ -167,6 +227,8 @@
             return carry
 
         lax.fori_loop(0, s_out.shape[0] // 64, clear, 0)
+        for copy in index_copies:
+            copy.wait()
 
     x = grad[...].astype(F32)
     for c in range(2):
@@ -204,42 +266,55 @@
         lax.fori_loop(0, s_out.shape[0] // 64, add, 0)
 
 
-def backward_kernel(lists, own, back, w_t, gw_two, h, z, gw_out, total):
-    g = pl.program_id(0)
-    rows = h.shape[0]
-
-    @pl.when(g == 0)
-    def _():
-        f_in = z.shape[1]
-        gw_out[pl.ds(0, f_in), :] = jnp.zeros((f_in, gw_out.shape[1]), F32)
-        gw_out[pl.ds(f_in, gw_two.shape[0]), :] = gw_two[...]
-
-        def copy(i, carry):
-            at = pl.ds(pl.multiple_of(i * 64, 64), 64)
-            total[at, :] = own[at, :]
-            return carry
-
-        lax.fori_loop(0, own.shape[0] // 64, copy, 0)
-
-        def add(i, carry):
-            for j in range(4):
-                at = pl.ds(pl.multiple_of(lists[i * 4 + j], 2), 2)
-                total[at, :] = total[at, :] + back[pl.ds(pl.multiple_of(i * 8, 8) + j * 2, 2), :]
-            return carry
-
-        lax.fori_loop(0, back.shape[0] // 8, add, 0)
-
-    s = jnp.concatenate([total[pl.ds(g * rows * 2 + c, rows, stride=2), :] for c in range(2)], axis=1)
-    high = s.astype(BF16)
-    rest = s - high.astype(F32)
-    mid = rest.astype(BF16)
-    low = (rest - mid.astype(F32)).astype(BF16)
-    wt = w_t[...]
-    d = jnp.dot(low, wt, preferred_element_type=F32)
-    d = d + jnp.dot(mid, wt, preferred_element_type=F32)
-    d = d + jnp.dot(high, wt, preferred_element_type=F32)
-    grad = jnp.where(h[...] > 0, d, 0.0).astype(BF16)
-    gw_out[pl.ds(0, z.shape[1]), :] += lax.dot_general(z[...], grad, (((0,), (0,)), ((), ())), preferred_element_type=F32)
+def backward_kernel(lists, own, back, w_t, gw_two, h_hbm, z_hbm, gw_out, total, h, z, own_sem, sems):
+    n, f_in = z.shape
+    rows = BLOCK
+    own_copy = pltpu.make_async_copy(own.at[pl.ds(0, total.shape[0])], total, own_sem)
+    own_copy.start()
+
+    def fetch(i):
+        at = pl.ds(pl.multiple_of(i * rows, rows), rows)
+        return (
+            pltpu.make_async_copy(h_hbm.at[at], h.at[at], sems.at[0, i]),
+            pltpu.make_async_copy(z_hbm.at[at], z.at[at], sems.at[1, i]),
+        )
+
+    def begin(i, carry):
+        for copy in fetch(i):
+            copy.start()
+        return carry
+
+    lax.fori_loop(0, n // rows, begin, 0)
+    gw_out[pl.ds(0, f_in), :] = jnp.zeros((f_in, gw_out.shape[1]), F32)
+    gw_out[pl.ds(f_in, gw_two.shape[0]), :] = gw_two[...]
+
+    own_copy.wait()
+
+    def add(i, carry):
+        for j in range(4):
+            at = pl.ds(pl.multiple_of(lists[i * 4 + j], 2), 2)
+            total[at, :] = total[at, :] + back[pl.ds(pl.multiple_of(i * 8, 8) + j * 2, 2), :]
+        return carry
+
+    lax.fori_loop(0, back.shape[0] // 8, add, 0)
+
+    def block(i, carry):
+        for copy in fetch(i):
+            copy.wait()
+        at = pl.ds(pl.multiple_of(i * rows, rows), rows)
+        parts = []
+        for c in range(2):
+            s = total[pl.ds(i * rows * 2 + c, rows, stride=2), :]
+            high = s.astype(BF16).astype(F32)
+            mid = (s - high).astype(BF16).astype(F32)
+            parts.append((high, mid, s - high - mid))
+        tail = parts[1][0] + pltpu.roll(parts[1][1], TAIL, 1) + pltpu.roll(parts[1][2], 2 * TAIL, 1)
+        d = jnp.dot(jnp.concatenate([*parts[0], tail], axis=1).astype(BF16), w_t[...], preferred_element_type=F32)
+        grad = jnp.where(h[at, :] > 0, d, 0.0).astype(BF16)
+        gw_out[pl.ds(0, f_in), :] += lax.dot_general(z[at, :], grad, (((0,), (0,)), ((), ())), preferred_element_type=F32)
+        return carry
+
+    lax.fori_loop(0, n // rows, block, 0)
 
 
 MESH = pl.DeviceIdType.MESH
@@ -383,63 +458,47 @@
         out_shape=jax.ShapeDtypeStruct((1024,1024),F32),
         scratch_shapes=[pltpu.VMEM((512,1024),F32), pltpu.VMEM((512,1024),F32), pltpu.VMEM((2,64,1024),F32), pltpu.VMEM((2,128,1024),F32), pltpu.VMEM((3,32,1024),F32), pltpu.VMEM((3,8,1024),F32),
             sem((3,8)), sem((3,8)), sem((2,3,6)), sem((2,3,6)), sem((2,3,3)), sem((2,3,3)), sem((2,3,3)), sem((2,3,3)), sem((3,8)), sem((3,8))],
-        compiler_params=pltpu.CompilerParams(collective_id=0, has_side_effects=True, vmem_limit_bytes=40*2**20),
+        compiler_params=pltpu.CompilerParams(collective_id=0, has_side_effects=True, vmem_limit_bytes=12*2**20),
         name="reduce_all")(x)
 
 
-def count_kernel(x, out, came, send, recv):
+def exchange_kernel(n_dev, *refs):
+    k = (len(refs) - 1) // 2
+    sems = refs[-1]
     me = lax.axis_index("graph")
-    hops = [(1, 2)] + [(2 * SIDE**axis, SIDE) for axis in range(3)]
-
-    def peer(stride, size, t):
-        here = lax.rem(me // stride, size)
-        return me + (lax.rem(here + t, size) - here) * stride
-
-    barrier = pltpu.get_barrier_semaphore()
-    for stride, size in hops:
-        for t in range(1, size):
-            pl.semaphore_signal(barrier, inc=1, device_id=(peer(stride, size, t),), device_id_type=MESH)
-    pl.semaphore_wait(barrier, came.shape[0])
-    out[0] = x[...]
-    slot = 0
-    copies = []
-    for stage, (stride, size) in enumerate(hops):
-        step = []
-        for t in range(1, size):
-            at = slot + t - 1
-            step.append(
-                pltpu.make_async_remote_copy(
-                    src_ref=out.at[stage],
-                    dst_ref=came.at[at],
-                    send_sem=send.at[at],
-                    recv_sem=recv.at[at],
-                    device_id=(peer(stride, size, t),),
-                    device_id_type=MESH,
-                )
-            )
-            step[-1].start()
-        total = out[stage]
-        for t, copy in enumerate(step):
-            copy.wait_recv()
-            total = total + came[slot + t]
-        out[stage + 1] = total
-        slot += size - 1
-        copies += step
-    for copy in copies:
-        copy.wait_send()
-
-
-def count_all(x):
+
+    def send(t, carry):
+        q = lax.rem(me + t, n_dev)
+        for j in range(k):
+            src, dst = refs[j], refs[k + j]
+            pltpu.make_async_remote_copy(
+                src_ref=src.at[q if src.shape[0] == n_dev else 0],
+                dst_ref=dst.at[me],
+                send_sem=sems.at[2 * j],
+                recv_sem=sems.at[2 * j + 1],
+                device_id=(q,),
+                device_id_type=MESH,
+            ).start()
+        return carry
+
+    lax.fori_loop(1, n_dev, send, 0)
+    for j in range(k):
+        others = refs[k + j].at[pl.ds(0, n_dev - 1)]
+        for side in range(2):
+            pltpu.make_async_copy(others, others, sems.at[2 * j + side]).wait()
+
+
+def exchange(n_dev, *arrays):
     vmem = pl.BlockSpec(memory_space=pltpu.VMEM)
     return pl.pallas_call(
-        count_kernel,
-        in_specs=[vmem],
-        out_specs=vmem,
-        out_shape=jax.ShapeDtypeStruct((5, 8, LANES), F32),
-        scratch_shapes=[pltpu.VMEM((10, 8, LANES), F32), pltpu.SemaphoreType.DMA((10,)), pltpu.SemaphoreType.DMA((10,))],
-        compiler_params=pltpu.CompilerParams(collective_id=1, has_side_effects=True, vmem_limit_bytes=2**20),
-        name="count_all",
-    )(x)
+        functools.partial(exchange_kernel, n_dev),
+        in_specs=[vmem] * len(arrays),
+        out_specs=[vmem] * len(arrays),
+        out_shape=[jax.ShapeDtypeStruct((n_dev,) + a.shape[1:], a.dtype) for a in arrays],
+        scratch_shapes=[pltpu.SemaphoreType.DMA((2 * len(arrays),))],
+        compiler_params=pltpu.CompilerParams(has_side_effects=True, vmem_limit_bytes=8 * 2**20),
+        name="exchange_one",
+    )(*arrays)
 
 
 def params():
@@ -465,84 +524,109 @@
         src8 = [edge_src[:, k] * 8 for k in range(deg)]
         src2 = [edge_src[:, k] * 2 for k in range(deg)]
         count = jnp.sum(label_mask.astype(F32))
-        first_rows, count = lax.optimization_barrier((feats[list_ids], count))
-        first_in = lax.all_to_all(first_rows, "graph", 0, 0, tiled=True)
-        label_total = count_all(jnp.full((8, LANES), count))[4, 0, 0]
-        first_in, label_total = lax.optimization_barrier((first_in, label_total))
+        label = jnp.where(label_mask == 1, labels, -1).reshape(n, 1)
+        first_in, counts = exchange(dev_count, feats[list_ids].reshape(dev_count, halo_rows, f_in), jnp.full((1, 1, LANES), count))
+        first_in = first_in.reshape(halo, f_in)
+        mine = jnp.arange(dev_count) == lax.axis_index("graph")
+        label_total = jnp.sum(jnp.where(mine, count, counts[:, 0, 0]))
         inv_total = (1.0 / label_total).reshape(1)
-        label = jnp.where(label_mask == 1, labels, -1).reshape(n, 1)
+        wt, w_one_b = edge_wt, w_one.astype(BF16)
 
         def by_rows(width):
             return pl.BlockSpec((BLOCK, width), lambda g: (g, 0))
-
-        def after_first(width):
-            return pl.BlockSpec((BLOCK, width), lambda g: (jnp.maximum(g - 1, 0), 0))
 
         gather_scratch = [
             pltpu.VMEM((ext * 8, LANES), F32),
             pltpu.VMEM((BLOCK * 8, LANES), F32),
             pltpu.VMEM((STEP * deg + 8, LANES), F32),
         ]
-        z_one, h_one, wt, second = pl.pallas_call(
+        whole = pl.BlockSpec(memory_space=pl.ANY)
+        dma = pltpu.SemaphoreType.DMA
+        index_scratch = [pltpu.SMEM((n,), jnp.int32) for _ in range(deg)]
+
+        def chunk_scratch(width):
+            return [pltpu.VMEM((2, BLOCK, width), BF16), dma((deg,)), dma((2,))]
+
+        second = pl.pallas_call(
+            functools.partial(list_rows_kernel, deg),
+            grid=(1,),
+            in_specs=[SMEM] + [whole] * (deg + 1) + [once((halo, f_in)), once((n, deg)), once((f_in, f_hid))],
+            out_specs=once((halo * 8, LANES)),
+            out_shape=jax.ShapeDtypeStruct((halo * 8, LANES), BF16),
+            scratch_shapes=gather_scratch + [pltpu.VMEM((halo, deg), F32)] + chunk_scratch(f_in) + index_scratch,
+            compiler_params=params(),
+            cost_estimate=pl.CostEstimate(flops=4 * halo * f_in * f_hid, bytes_accessed=2 * n * f_in, transcendentals=0),
+            name="list_rows",
+        )(list_ids, *src8, feats, first_in, wt, w_one_b)
+        h_in = lax.all_to_all(second, "graph", 0, 0, tiled=True)
+        z_one, h_one = pl.pallas_call(
             functools.partial(layer_one_kernel, deg),
-            grid=(1 + n // BLOCK,),
-            in_specs=[SMEM] + [SMEM] * deg + [once((n, f_in)), once((halo, f_in)), once((deg, n)), once((f_in, f_hid))],
-            out_specs=[after_first(f_in), after_first(f_hid), once((n, deg)), once((halo * 8, LANES))],
-            out_shape=[
-                jax.ShapeDtypeStruct((n, f_in), BF16),
-                jax.ShapeDtypeStruct((n, f_hid), BF16),
-                jax.ShapeDtypeStruct((n, deg), F32),
-                jax.ShapeDtypeStruct((halo * 8, LANES), BF16),
-            ],
-            scratch_shapes=gather_scratch
-            + [
-                pltpu.VMEM((f_in, f_hid), BF16),
-                pltpu.VMEM((halo, deg), F32),
-            ],
+            grid=(n // BLOCK,),
+            in_specs=[whole] * (deg + 1) + [once((halo, f_in)), by_rows(deg), once((f_in, f_hid))],
+            out_specs=[by_rows(f_in), by_rows(f_hid)],
+            out_shape=[jax.ShapeDtypeStruct((n, f_in), BF16), jax.ShapeDtypeStruct((n, f_hid), BF16)],
+            scratch_shapes=gather_scratch + chunk_scratch(f_in) + index_scratch,
             compiler_params=params(),
+            cost_estimate=pl.CostEstimate(flops=8 * n * f_in * f_hid, bytes_accessed=8 * n * f_in, transcendentals=0),
             name="layer_one",
-        )(list_ids, *src8, feats, first_in, edge_wt.T, w_one)
-        h_in = lax.all_to_all(second, "graph", 0, 0, tiled=True)
-        grad_log, gw_two = pl.pallas_call(
+        )(*src8, feats, first_in, wt, w_one_b)
+        grad_log, z_two, loss_part = pl.pallas_call(
             functools.partial(layer_two_kernel, classes, deg),
             grid=(n // BLOCK,),
-            in_specs=[SMEM] + [SMEM] * deg + [by_rows(deg), once((n, f_hid)), once((halo * 8, LANES)), once((f_hid, pad)), by_rows(1)],
-            out_specs=[by_rows(pad), once((pad, f_hid))],
-            out_shape=[jax.ShapeDtypeStruct((n, pad), BF16), jax.ShapeDtypeStruct((pad, f_hid), F32)],
-            scratch_shapes=gather_scratch + [pltpu.VMEM((1, pad), F32)],
+            in_specs=[SMEM] + [whole] * deg + [by_rows(deg), whole, once((halo * 8, LANES)), once((f_hid, pad)), by_rows(1)],
+            out_specs=[by_rows(pad), by_rows(f_hid), once((1, LANES))],
+            out_shape=[
+                jax.ShapeDtypeStruct((n, pad), BF16),
+                jax.ShapeDtypeStruct((n, f_hid), BF16),
+                jax.ShapeDtypeStruct((1, LANES), F32),
+            ],
+            scratch_shapes=gather_scratch + [pltpu.VMEM((1, pad), F32)] + chunk_scratch(f_hid) + index_scratch,
             compiler_params=params(),
             name="layer_two",
         )(inv_total, *src8, wt, h_one, h_in, w_two_b, label)
         ext_grad = pl.pallas_call(
             functools.partial(scatter_kernel, deg),
             grid=(n // 512,),
-            in_specs=[SMEM] * deg + [by_rows(deg), by_rows(pad)],
+            in_specs=[whole] * deg + [by_rows(deg), by_rows(pad)],
             out_specs=once((ext * 2, LANES)),
             out_shape=jax.ShapeDtypeStruct((ext * 2, LANES), F32),
-            scratch_shapes=[pltpu.VMEM((BLOCK * 2, LANES), F32), pltpu.VMEM((STEP * deg + 8, LANES), F32)]
+            scratch_shapes=[pltpu.VMEM((BLOCK * 2, LANES), F32), pltpu.VMEM((STEP * deg + 8, LANES), F32), dma((deg,))]
+            + index_scratch
             + [pltpu.VMEM((ext * 2, LANES), F32) for _ in range(deg)],
             compiler_params=params(),
             name="scatter",
         )(*src2, wt, grad_log)
-        back = lax.all_to_all(ext_grad[n * 2 :], "graph", 0, 0, tiled=True)
+        returned, grad_log = lax.optimization_barrier((ext_grad[n * 2 :], grad_log))
+        back = lax.all_to_all(returned, "graph", 0, 0, tiled=True)
+        gw_two = pl.pallas_call(
+            grad_two_kernel,
+            grid=(n // BLOCK,),
+            in_specs=[by_rows(pad), by_rows(f_hid), once((1, LANES))],
+            out_specs=once((pad, f_hid)),
+            out_shape=jax.ShapeDtypeStruct((pad, f_hid), F32),
+            compiler_params=pltpu.CompilerParams(dimension_semantics=("arbitrary",), vmem_limit_bytes=20 * 2**20),
+            cost_estimate=pl.CostEstimate(flops=2 * n * pad * f_hid, bytes_accessed=2 * n * f_hid, transcendentals=0),
+            name="grad_two",
+        )(grad_log, z_two, loss_part)
+        w_t = w_two.astype(BF16).T
+        w_tail = jnp.pad(w_t[LANES:], ((0, TAIL - (classes - LANES)), (0, 0)))
+        w_parts = jnp.concatenate([w_t[:LANES]] * 3 + [w_tail] * 3 + [jnp.zeros((LANES - 3 * TAIL, f_hid), BF16)])
+        vmem = pl.BlockSpec(memory_space=pltpu.VMEM)
         partial = pl.pallas_call(
             backward_kernel,
-            grid=(n // 512,),
-            in_specs=[
-                SMEM,
-                once((n * 2, LANES)),
-                once((halo * 2, LANES)),
-                once((pad, f_hid)),
-                once((pad, f_hid)),
-                pl.BlockSpec((512, f_hid), lambda g: (g, 0)),
-                pl.BlockSpec((512, f_in), lambda g: (g, 0)),
+            in_specs=[SMEM, whole, vmem, vmem, vmem, whole, whole],
+            out_specs=vmem,
+            out_shape=jax.ShapeDtypeStruct((f_in + pad, f_hid), F32),
+            scratch_shapes=[
+                pltpu.VMEM((n * 2, LANES), F32),
+                pltpu.VMEM((n, f_hid), BF16),
+                pltpu.VMEM((n, f_in), BF16),
+                dma,
+                dma((2, n // BLOCK)),
             ],
-            out_specs=once((f_in + pad, f_hid)),
-            out_shape=jax.ShapeDtypeStruct((f_in + pad, f_hid), F32),
-            scratch_shapes=[pltpu.VMEM((n * 2 + 8, LANES), F32)],
-            compiler_params=params(),
+            compiler_params=pltpu.CompilerParams(vmem_limit_bytes=44 * 2**20),
             name="backward",
-        )(lists2, ext_grad, back, w_two_b.T, gw_two, h_one, z_one)
+        )(lists2, ext_grad, back, w_parts, gw_two, h_one, z_one)
         total = reduce_all(partial)
         return -total[f_in + pad - 1, 0] / label_total, total[:f_in], total[f_in : f_in + classes].T
 

time: 344 us -> 309 us (0.90)
  waiting for transfers between devices: 26.6 us -> 4.57 us
  Pallas kernels: 263 us -> 247 us
  other arithmetic: 3.6 us -> 7.78 us
  starting transfers between devices: 22.2 us -> 18.3 us
    pallas_call x1, Pallas kernels: 63.3 us -> 46.7 us  [device_step(): pl.pallas_call(functools.partial(layer_two_kernel, classes, deg), grid=(n...]
    all_to_all x1, waiting for transfers between devices: 14.5 us -> 0.01 us  [device_step(): h_in = lax.all_to_all(second, 'graph', 0, 0, tiled=True)]
    all_to_all x2 -> x1, waiting for transfers between devices: 12.1 us -> 4.56 us  [device_step(): back = lax.all_to_all(returned, 'graph', 0, 0, tiled=True)]
    all_to_all x2 -> x1, starting transfers between devices: 15.9 us -> 9.9 us  [device_step(): back = lax.all_to_all(returned, 'graph', 0, 0, tiled=True)]
    all_to_all x3 -> x0, local copies, waits for them, and re-layouts: 4 us -> none  [the longest x2 2.14 us: device_step(): first_in = lax.all_to_all(first_rows, 'graph', 0, 0, tiled=True)]
    unnamed x14 -> x25, local copies, waits for them, and re-layouts: 4.98 us -> 8 us
    pallas_call x3 -> x5, Pallas kernels: 113 us -> 114 us  [the longest x1 47.5 us: device_step(): pl.pallas_call(functools.partial(layer_one_kernel, deg), grid=(n // BLOCK...]
  transfers between devices with their start and end apart: 3 -> 2, of which waited for: 2 -> 1; matrix products, arithmetic and copies ran while one was open for 2% -> 2% of each run, Pallas kernels for 5% -> 17%
where the time goes in v5:
time: 309 us; the launch traced here: 308 us
  Pallas kernels  247 us (80%)
  local copies, waits for them, and re-layouts  25.8 us (8%)
  starting transfers between devices  18.3 us (6%)
  other arithmetic  7.78 us (3%)
  waiting for transfers between devices  4.57 us (1%)
  between operations  4.14 us (1%)
    pallas_call x1, Pallas kernels, device_step(): pl.pallas_call(functools.partial(layer_one_kernel, deg), grid=(n // BLOCK...  47.5 us
    pallas_call x1, Pallas kernels, device_step(): pl.pallas_call(functools.partial(layer_two_kernel, classes, deg), grid=(n...  46.7 us
    pallas_call x1, Pallas kernels, device_step(): pl.pallas_call(functools.partial(scatter_kernel, deg), grid=(n // 512,),...  45.2 us
    pallas_call x1, Pallas kernels, reduce_all(): pl.pallas_call(reduce_kernel, in_specs=[pl.BlockSpec(memory_space=pltpu.V...  42 us
    pallas_call x1, Pallas kernels, exchange(): pl.pallas_call(functools.partial(exchange_kernel, n_dev), in_specs=[vmem]...  27.6 us
    pallas_call x1, Pallas kernels, device_step(): pl.pallas_call(backward_kernel, in_specs=[SMEM, whole, vmem, vmem, vmem,...  19 us
    pallas_call x1, Pallas kernels, device_step(): pl.pallas_call(functools.partial(list_rows_kernel, deg), grid=(1,), in_sp...  15.7 us
    all_to_all x1, starting transfers between devices, device_step(): back = lax.all_to_all(returned, 'graph', 0, 0, tiled=True)  9.9 us
  transfers between devices with their start and end apart: 2, of which 1 were waited for; matrix products, arithmetic and copies ran while one was open for 2% of the time, Pallas kernels for 17%

profile of v5, /device:TPU:1, one launch (start us, length us, event | category | flops | bytes accessed | tf_op | source)
XLA Modules:
  0.0 308.1 jit_solution(17886930941894836665)
XLA Ops:
  2.2 2.4 slice_multiply_fusion
  4.7 6.0 %gather_fusion = bf16[512,768]{1,0:T(8,128)(2,1)S(1)} fusion(bf16[4096,768]{1,0:T(8,128)(2,1)} %refs_8_.5, s32[1024]{0:T(1024)S(1)} %pad_clamp_fusion), kind=kCustom, calls=%fused_computation | custom fusion | bytes 1574912 | tf_op jit(solution)/shard_map/gather | solution.py:528
  12.2 27.6 %exchange_one.1 = (bf16[128,4,768]{2,1,0:T(4,128)(2,1)S(1)}, f32[128,1,128]{2,1,0:T(1,128)S(1)}) custom-call(bf16[128,4,768]{2,1,0:T(4,128)(2,1)S(1)} %reshape.90.refs_0_, f32[1,1,128]{2,1,0:T(1,128)S(1)} %broadcast_in_dim.16.refs_1_), custom_call_target="tpu_custom_call" | custom-call | tf_op jit(solution)/shard_map/exchange_one/pallas_call | solution.py:493
  39.8 1.1 reshape.92.refs_9_
  40.9 1.9 copy.23.refs_10_.refs_8_
  42.8 3.3 %convert_element_type.15.refs_11_ = bf16[768,1024]{1,0:T(8,128)(2,1)} convert(f32[768,1024]{1,0:T(8,128)} %param.10) | non-fusion elementwise | flops 786432 | bytes 4718592 | tf_op jit(solution)/shard_map/convert_element_type | solution.py:533
  46.1 15.7 %list_rows.1 = bf16[4096,128]{1,0:T(8,128)(2,1)} custom-call(s32[512]{0:T(512)} %reshape.88.lists, s32[4096]{0:T(1024)} %bitcast.33, s32[4096]{0:T(1024)} %bitcast.36, s32[4096]{0:T(1024)} %bitcast.39, s32[4096]{0:T(1024)} %bitcast.42, s32[4096]{0:T(1024)} %bitcast.45, s32[4096]{0:T(1024)} %bitcast.48, s32[4096]{0:T(1024)} %bitcast.51, s32[4096]{0:T(1024)} %bitcast.30, ...), custom_call_target="tpu_custom_call" | custom-call | flops 1610612736 | bytes 6291456 | tf_op jit(solution)/shard_map/list_rows/pallas_call | solution.py:550
  61.9 8.4 %all-to-all-start = ((bf16[128,32,128]{2,1,0:T(8,128)(2,1)}), bf16[128,32,128]{2,1,0:T(8,128)(2,1)}, u32[]{:S(2)}, u32[]{:S(2)}) async-start(bf16[128,32,128]{2,1,0:T(8,128)(2,1)} %bitcast.29), calls=%async_computation | async-start | bytes 2097152 | tf_op jit(solution)/shard_map/all_to_all | solution.py:561
  70.3 47.5 %layer_one.1 = (bf16[4096,768]{1,0:T(8,128)(2,1)}, bf16[4096,1024]{1,0:T(8,128)(2,1)}) custom-call(s32[4096]{0:T(1024)} %bitcast.34, s32[4096]{0:T(1024)} %bitcast.37, s32[4096]{0:T(1024)} %bitcast.40, s32[4096]{0:T(1024)} %bitcast.43, s32[4096]{0:T(1024)} %bitcast.46, s32[4096]{0:T(1024)} %bitcast.49, s32[4096]{0:T(1024)} %bitcast.52, s32[4096]{0:T(1024)} %bitcast.31, ...), custom_call_target="tpu_custom_call" | custom-call | flops 25769803776 | bytes 25165824 | tf_op jit(solution)/shard_map/layer_one/pallas_call | solution.py:562
  117.9 1.0 slice_reduce_fusion
  118.9 2.0 copy.22.refs_12_
  121.2 1.3 fusion
  123.2 0.9 pad.8.clone.refs_11_
  124.2 46.7 %layer_two.1 = (bf16[4096,256]{1,0:T(8,128)(2,1)}, bf16[4096,1024]{1,0:T(8,128)(2,1)}, f32[1,128]{1,0:T(1,128)}) custom-call(f32[1]{0:T(128)} %bitcast.9.inv_total, s32[4096]{0:T(1024)} %bitcast.35, s32[4096]{0:T(1024)} %bitcast.38, s32[4096]{0:T(1024)} %bitcast.41, s32[4096]{0:T(1024)} %bitcast.44, s32[4096]{0:T(1024)} %bitcast.47, s32[4096]{0:T(1024)} %bitcast.50, ...), custom_call_target="tpu_custom_call" | custom-call | tf_op jit(solution)/shard_map/layer_two/pallas_call | solution.py:573
  170.9 45.2 %scatter.1.own = f32[9216,128]{1,0:T(8,128)} custom-call(s32[4096]{0:T(1024)} %bitcast.59, s32[4096]{0:T(1024)} %bitcast.58, s32[4096]{0:T(1024)} %bitcast.57, s32[4096]{0:T(1024)} %bitcast.56, s32[4096]{0:T(1024)} %bitcast.55, s32[4096]{0:T(1024)} %bitcast.54, s32[4096]{0:T(1024)} %bitcast.61, s32[4096]{0:T(1024)} %bitcast.60, ...), custom_call_target="tpu_custom_call" | custom-call | tf_op jit(solution)/shard_map/scatter/pallas_call | solution.py:587
  216.1 1.9 slice.70
  218.0 9.9 %all-to-all-start.1 = ((f32[128,8,128]{2,1,0:T(8,128)}), f32[128,8,128]{2,1,0:T(8,128)S(1)}, u32[]{:S(2)}, u32[]{:S(2)}) async-start(f32[128,8,128]{2,1,0:T(8,128)} %bitcast.21), calls=%async_computation.1 | async-start | bytes 1048576 | tf_op jit(solution)/shard_map/all_to_all | solution.py:600
  228.0 3.4 %copy-done = bf16[4096,1024]{1,0:T(8,128)(2,1)S(1)} copy-done((bf16[4096,1024]{1,0:T(8,128)(2,1)S(1)}, bf16[4096,1024]{1,0:T(8,128)(2,1)}, u32[]{:S(2)}) %copy-start) | copy-done | bytes 8388632
  231.3 1.6 copy-done.1
  232.9 3.8 %grad_two.1.gw_two = f32[256,1024]{1,0:T(8,128)S(1)} custom-call(bf16[4096,256]{1,0:T(8,128)(2,1)S(1)} %copy-done.1, bf16[4096,1024]{1,0:T(8,128)(2,1)S(1)} %copy-done, f32[1,128]{1,0:T(1,128)S(1)} %copy-done.2), custom_call_target="tpu_custom_call" | custom-call | flops 2147483648 | bytes 8388608 | tf_op jit(solution)/shard_map/grad_two/pallas_call | solution.py:601
  236.8 4.6 %all-to-all-done.1 = f32[128,8,128]{2,1,0:T(8,128)S(1)} async-done(((f32[128,8,128]{2,1,0:T(8,128)}), f32[128,8,128]{2,1,0:T(8,128)S(1)}, u32[]{:S(2)}, u32[]{:S(2)}) %all-to-all-start.1) | async-done | bytes 524320 | tf_op jit(solution)/shard_map/all_to_all | solution.py:600
  241.3 19.0 %backward.1.x = f32[1024,1024]{1,0:T(8,128)S(1)} custom-call(s32[512]{0:T(512)S(1)} %broadcast_multiply_fusion.lists, f32[9216,128]{1,0:T(8,128)} %scatter.1.own, f32[1024,128]{1,0:T(8,128)S(1)} %bitcast.28, bf16[512,1024]{1,0:T(8,128)(2,1)S(1)} %broadcast_dynamic-update-slice_fusion.w_t, f32[256,1024]{1,0:T(8,128)S(1)} %grad_two.1.gw_two, ...), custom_call_target="tpu_custom_call" | custom-call | tf_op jit(solution)/shard_map/backward/pallas_call | solution.py:615
  260.3 42.0 %reduce_all.1 = f32[1024,1024]{1,0:T(8,128)S(1)} custom-call(f32[1024,1024]{1,0:T(8,128)S(1)} %backward.1.x), custom_call_target="tpu_custom_call" | custom-call | tf_op jit(solution)/shard_map/reduce_all/pallas_call | solution.py:456
  302.3 1.9 slice.66
  (38 shorter events, 4.9 us)
Async XLA Ops:
  4.7 6.2 %copy-start.5 = (s32[4096]{0:T(1024)S(1)}, s32[4096]{0:T(1024)}, u32[]{:S(2)}) copy-start(s32[4096]{0:T(1024)} %param.16) | copy-start | bytes 49156
  4.7 36.2 %copy-start.4 = (f32[4096,8]{0,1:T(8,128)S(1)}, f32[4096,8]{0,1:T(8,128)}, u32[]{:S(2)}) copy-start(f32[4096,8]{0,1:T(8,128)} %param.14) | copy-start | bytes 393220
  61.9 62.3 %all-to-all-start = ((bf16[128,32,128]{2,1,0:T(8,128)(2,1)}), bf16[128,32,128]{2,1,0:T(8,128)(2,1)}, u32[]{:S(2)}, u32[]{:S(2)}) async-start(bf16[128,32,128]{2,1,0:T(8,128)(2,1)} %bitcast.29), calls=%async_computation | async-start | bytes 2097152 | tf_op jit(solution)/shard_map/all_to_all | solution.py:561
  70.3 47.5 %copy-start.3 = (f32[1024,153]{0,1:T(8,128)S(1)}, f32[1024,153]{0,1:T(8,128)}, u32[]{:S(2)}) copy-start(f32[1024,153]{0,1:T(8,128)} %param.11) | copy-start | bytes 1880068
  70.3 48.7 %copy-start.7 = (s32[4096]{0:T(1024)S(1)}, s32[4096]{0:T(1024)}, u32[]{:S(2)}) copy-start(s32[4096]{0:T(1024)} %param.15) | copy-start | bytes 49156
  170.9 57.0 %copy-start.6 = (s32[512]{0:T(512)S(1)}, s32[512]{0:T(512)}, u32[]{:S(2)}) copy-start(s32[512]{0:T(512)} %reshape.88.lists) | copy-start | bytes 6148
  170.9 57.0 %copy-start.2 = (f32[1,128]{1,0:T(1,128)S(1)}, f32[1,128]{1,0:T(1,128)}, u32[]{:S(2)}) copy-start(f32[1,128]{1,0:T(1,128)} %get-tuple-element.19.loss) | copy-start | bytes 1540
  218.0 23.3 %all-to-all-start.1 = ((f32[128,8,128]{2,1,0:T(8,128)}), f32[128,8,128]{2,1,0:T(8,128)S(1)}, u32[]{:S(2)}, u32[]{:S(2)}) async-start(f32[128,8,128]{2,1,0:T(8,128)} %bitcast.21), calls=%async_computation.1 | async-start | bytes 1048576 | tf_op jit(solution)/shard_map/all_to_all | solution.py:600
  228.0 3.4 %copy-start = (bf16[4096,1024]{1,0:T(8,128)(2,1)S(1)}, bf16[4096,1024]{1,0:T(8,128)(2,1)}, u32[]{:S(2)}) copy-start(bf16[4096,1024]{1,0:T(8,128)(2,1)} %get-tuple-element.18.z) | copy-start | bytes 25165828
  231.3 1.6 copy-start.1

commit v6 on v5

--- a/solution.py
+++ b/solution.py
@@ -11,6 +11,7 @@
 TAIL = 32
 STEP = 16
 BLOCK = 512
+CHUNK = 512
 F32, BF16 = jnp.float32, jnp.bfloat16
 
 
@@ -157,7 +158,7 @@
     h_out[...] = h.astype(BF16)
 
 
-def layer_two_kernel(classes, deg, inv_total, *refs):
+def layer_two_kernel(classes, deg, label_total, *refs):
     src_hbm, refs, src = refs[:deg], refs[deg:-deg], refs[-deg:]
     wt, own, halo, w, label, g_out, z_out, loss_out, table, zbuf, wbuf, loss_sum, chunk, src_sem, chunk_sem = refs
     g = pl.program_id(0)
@@ -185,7 +186,7 @@
     tag = label[...]
     hit = col == tag
     loss_sum[...] += jnp.sum(jnp.where(hit, log_prob, 0.0), axis=0, keepdims=True)
-    scale = jnp.where(tag >= 0, inv_total[0], 0.0)
+    scale = jnp.where(tag >= 0, (1.0 / label_total[...])[:, :1], 0.0)
     grad = jnp.where(real, (jnp.exp(log_prob) - jnp.where(hit, 1.0, 0.0)) * scale, 0.0).astype(BF16)
     g_out[...] = grad
     z_out[...] = z
@@ -210,7 +211,7 @@
 
 
 def scatter_kernel(deg, *refs):
-    src_hbm, (wt, grad, s_out, gbuf, wbuf, sems), refs = refs[:deg], refs[deg : deg + 6], refs[deg + 6 :]
+    src_hbm, (wt, grad, own_out, back_out, gbuf, wbuf, sems), refs = refs[:deg], refs[deg : deg + 7], refs[deg + 7 :]
     src, parts = refs[:deg], refs[deg:]
     g = pl.program_id(0)
     rows = grad.shape[0]
@@ -226,7 +227,7 @@
                     part[pl.ds(pl.multiple_of(i * 64, 64) + j * 8, 8), :] = jnp.zeros((8, LANES), F32)
             return carry
 
-        lax.fori_loop(0, s_out.shape[0] // 64, clear, 0)
+        lax.fori_loop(0, parts[0].shape[0] // 64, clear, 0)
         for copy in index_copies:
             copy.wait()
 
@@ -255,21 +256,26 @@
 
     @pl.when(g == pl.num_programs(0) - 1)
     def _():
-        def add(i, carry):
-            at = pl.ds(pl.multiple_of(i * 64, 64), 64)
-            total = parts[0][at, :]
-            for part in parts[1:]:
-                total = total + part[at, :]
-            s_out[at, :] = total
-            return carry
-
-        lax.fori_loop(0, s_out.shape[0] // 64, add, 0)
+        def add_into(dst, offset):
+            def add(i, carry):
+                at = pl.multiple_of(i * 64, 64)
+                rows_at = pl.ds(pl.multiple_of(at + offset, 64), 64)
+                total = parts[0][rows_at, :]
+                for part in parts[1:]:
+                    total = total + part[rows_at, :]
+                dst[pl.ds(at, 64), :] = total
+                return carry
+
+            lax.fori_loop(0, dst.shape[0] // 64, add, 0)
+
+        add_into(own_out, 0)
+        add_into(back_out, own_out.shape[0])
 
 
 def backward_kernel(lists, own, back, w_t, gw_two, h_hbm, z_hbm, gw_out, total, h, z, own_sem, sems):
     n, f_in = z.shape
-    rows = BLOCK
-    own_copy = pltpu.make_async_copy(own.at[pl.ds(0, total.shape[0])], total, own_sem)
+    rows = CHUNK
+    own_copy = pltpu.make_async_copy(own, total, own_sem)
     own_copy.start()
 
     def fetch(i):
@@ -319,7 +325,15 @@
 
 MESH = pl.DeviceIdType.MESH
 SIDE = 4
-COLORS = ((0, 384, (0, 1, 2)), (384, 384, (1, 2, 0)), (768, 256, (2, 0, 1)))
+COLORS = (
+    (0, 256, (0, 1, 2)),
+    (256, 128, (1, 2, 0)),
+    (384, 128, (2, 0, 1)),
+    (512, 128, (0, 1, 2)),
+    (640, 256, (1, 2, 0)),
+    (896, 128, (2, 0, 1)),
+)
+SETS = ((0, 1, 2), (3, 4, 5))
 
 
 def reduce_kernel(x, out, acc, pair_buf, relay, far, mid, near, *sems):
@@ -359,71 +373,84 @@
         return pl.ds(pl.multiple_of(start + p * big + part * (big // 2), 8), big // 2)
 
     order = ((2, 0), (2, 1), (1, 1), (3, 0), (1, 0), (3, 1), (0, 0), (0, 1))
-    pair = {}
-    for t, part in order:
-        for c, (lanes, _) in enumerate(colors):
-            at = piece(c, t, part)
-            pair[c, t, part] = send(
-                x.at[piece(c, t, part, other), lanes], pair_buf.at[at, lanes], pair_send.at[c, t * 2 + part], pair_recv.at[c, t * 2 + part], partner
-            )
-    ring = {}
-    for t, part in order:
-        for c, (lanes, axes) in enumerate(colors):
-            at = piece(c, t, part)
-            pair[c, t, part].wait_recv()
-            mine = x[piece(c, t, part, base), lanes] + pair_buf[at, lanes]
-            if (t, part) in ((1, 0), (3, 1)):
-                ring[c, 2, part].wait_recv()
-                mine = mine + relay[part, :, lanes]
-            acc[at, lanes] = mine
-            if t == 0:
-                continue
-            forward = part == 0 if t == 2 else t == 1
-            _, dev = peer(axes[0], 1 if forward else 3)
-            if t == 2:
-                dst = relay.at[part, :, lanes]
-            else:
-                dst = far.at[0 if forward else 1, pl.ds(part * (big // 2), big // 2), lanes]
-            slot = order.index((t, part))
-            ring[c, t, part] = send(acc.at[at, lanes], dst, ring_send.at[0, c, slot], ring_recv.at[0, c, slot], dev)
-    start = [0, 0, 0]
-    for c, (lanes, axes) in enumerate(colors):
-        start[c] = where[axes[0]] * big
-        for key in ((1, 1), (3, 0), (1, 0), (3, 1)):
-            ring[(c, *key)].wait_recv()
-        rows = pl.ds(pl.multiple_of(start[c], 8), big)
-        acc[rows, lanes] = acc[rows, lanes] + far[0, :, lanes] + far[1, :, lanes]
-    for stage, (size, buf) in enumerate(((big // SIDE, mid), (big // SIDE**2, near)), 1):
-        copies = {}
-        for c, (lanes, axes) in enumerate(colors):
-            for t in (2, 1, 3):
-                p, dev = peer(axes[stage], t)
-                rows = pl.ds(pl.multiple_of(start[c] + p * size, 8), size)
-                sem = (stage - 1, c, t - 1)
-                copies[c, t] = send(acc.at[rows, lanes], buf.at[t - 1, :, lanes], rs_send.at[sem], rs_recv.at[sem], dev)
-        for c, (lanes, axes) in enumerate(colors):
-            start[c] = start[c] + where[axes[stage]] * size
-            rows = pl.ds(pl.multiple_of(start[c], 8), size)
+    pair, ring, later, got = {}, {}, {}, {}
+    for phase in (order[:4], order[4:]):
+        for group in SETS:
+            for t, part in phase:
+                for c in group:
+                    lanes = colors[c][0]
+                    at = piece(c, t, part)
+                    slot = (c, t * 2 + part)
+                    src = x.at[piece(c, t, part, other), lanes]
+                    pair[c, t, part] = send(src, pair_buf.at[at, lanes], pair_send.at[slot], pair_recv.at[slot], partner)
+
+    def first_axis(c, t, part):
+        lanes, axes = colors[c]
+        at = piece(c, t, part)
+        pair[c, t, part].wait_recv()
+        mine = x[piece(c, t, part, base), lanes] + pair_buf[at, lanes]
+        if (t, part) in ((1, 0), (3, 1)):
+            ring[c, 2, part].wait_recv()
+            mine = mine + relay[part, :, lanes]
+        acc[at, lanes] = mine
+        if t == 0:
+            return
+        forward = part == 0 if t == 2 else t == 1
+        _, dev = peer(axes[0], 1 if forward else 3)
+        if t == 2:
+            dst = relay.at[part, :, lanes]
+        else:
+            dst = far.at[0 if forward else 1, pl.ds(part * (big // 2), big // 2), lanes]
+        slot = order.index((t, part))
+        ring[c, t, part] = send(acc.at[at, lanes], dst, ring_send.at[0, c, slot], ring_recv.at[0, c, slot], dev)
+
+    for phase in (order[:4], order[4:]):
+        for group in SETS:
+            for t, part in phase:
+                for c in group:
+                    first_axis(c, t, part)
+    start = [where[axes[0]] * big for _, axes in colors]
+    sizes = (big, big // SIDE, big // SIDE**2)
+    bufs = (far, mid, near)
+
+    def collect(stage, c):
+        lanes, axes = colors[c]
+        if stage:
+            start[c] = start[c] + where[axes[stage]] * sizes[stage]
             for t in (1, 2, 3):
-                copies[c, t].wait_recv()
-            mine = acc[rows, lanes] + buf[0, :, lanes] + buf[1, :, lanes] + buf[2, :, lanes]
-            if stage == 1:
-                acc[rows, lanes] = mine
-            else:
-                out[pl.ds(pl.multiple_of(base + start[c], 8), size), lanes] = mine
-    for stage, size in ((2, big // SIDE**2), (1, big // SIDE)):
-        copies = {}
-        for c, (lanes, axes) in enumerate(colors):
-            here = out.at[pl.ds(pl.multiple_of(base + start[c], 8), size), lanes]
-            for t in (2, 1, 3):
-                _, dev = peer(axes[stage], t)
-                sem = (stage - 1, c, t - 1)
-                copies[c, t] = send(here, here, ag_send.at[sem], ag_recv.at[sem], dev)
-        for c, (lanes, axes) in enumerate(colors):
-            for t in (1, 2, 3):
-                copies[c, t].wait_recv()
-            start[c] = start[c] - where[axes[stage]] * size
-    got = {}
+                later[c, t].wait_recv()
+        else:
+            for key in ((1, 1), (3, 0), (1, 0), (3, 1)):
+                ring[(c, *key)].wait_recv()
+        rows = pl.ds(pl.multiple_of(start[c], 8), sizes[stage])
+        mine = acc[rows, lanes]
+        for j in range(bufs[stage].shape[0]):
+            mine = mine + bufs[stage][j, :, lanes]
+        if stage < 2:
+            acc[rows, lanes] = mine
+        else:
+            out[pl.ds(pl.multiple_of(base + start[c], 8), sizes[2]), lanes] = mine
+
+    def scatter_on(stage, c):
+        lanes, axes = colors[c]
+        for t in (2, 1, 3):
+            p, dev = peer(axes[stage], t)
+            rows = pl.ds(pl.multiple_of(start[c] + p * sizes[stage], 8), sizes[stage])
+            slot = (stage - 1, c, t - 1)
+            later[c, t] = send(acc.at[rows, lanes], bufs[stage].at[t - 1, :, lanes], rs_send.at[slot], rs_recv.at[slot], dev)
+
+    def spread(stage, c):
+        lanes, axes = colors[c]
+        here = out.at[pl.ds(pl.multiple_of(base + start[c], 8), sizes[stage]), lanes]
+        for t in (2, 1, 3):
+            _, dev = peer(axes[stage], t)
+            slot = (stage - 1, c, t - 1)
+            later[c, t] = send(here, here, ag_send.at[slot], ag_recv.at[slot], dev)
+
+    def spread_done(stage, c):
+        for t in (1, 2, 3):
+            later[c, t].wait_recv()
+        start[c] = start[c] - where[colors[c][1][stage]] * sizes[stage]
 
     def pass_on(c, t, part, slot, directions):
         here = out.at[piece(c, t, part, base), colors[c][0]]
@@ -432,19 +459,39 @@
             got[c, name] = send(here, here, ring_send.at[1, c, name], ring_recv.at[1, c, name], dev)
         got[c, slot] = send(here, here, back_send.at[c, slot - 6], back_recv.at[c, slot - 6], partner)
 
-    for c in range(3):
-        pass_on(c, 0, 0, 6, ((1, 0), (3, 3)))
-        pass_on(c, 0, 1, 7, ((3, 2), (1, 1)))
-    for c in range(3):
-        got[c, 0].wait_recv()
-        pass_on(c, 3, 0, 8, ((1, 4),))
-        got[c, 2].wait_recv()
-        pass_on(c, 1, 1, 9, ((3, 5),))
-    for name, (t, part), slot in ((1, (3, 1), 10), (3, (1, 0), 11), (4, (2, 0), 12), (5, (2, 1), 13)):
-        for c in range(3):
-            got[c, name].wait_recv()
-            pass_on(c, t, part, slot, ())
-    for c in range(3):
+    for group in SETS:
+        for c in group:
+            collect(0, c)
+            scatter_on(1, c)
+    for group in SETS:
+        for c in group:
+            collect(1, c)
+            scatter_on(2, c)
+    for group in SETS:
+        for c in group:
+            collect(2, c)
+            spread(2, c)
+    for group in SETS:
+        for c in group:
+            spread_done(2, c)
+            spread(1, c)
+    for group in SETS:
+        for c in group:
+            spread_done(1, c)
+            pass_on(c, 0, 0, 6, ((1, 0), (3, 3)))
+            pass_on(c, 0, 1, 7, ((3, 2), (1, 1)))
+    for group in SETS:
+        for c in group:
+            got[c, 0].wait_recv()
+            pass_on(c, 3, 0, 8, ((1, 4),))
+            got[c, 2].wait_recv()
+            pass_on(c, 1, 1, 9, ((3, 5),))
+    for group in SETS:
+        for name, (t, part), slot in ((1, (3, 1), 10), (3, (1, 0), 11), (4, (2, 0), 12), (5, (2, 1), 13)):
+            for c in group:
+                got[c, name].wait_recv()
+                pass_on(c, t, part, slot, ())
+    for c in range(len(colors)):
         for slot in range(6, 14):
             got[c, slot].wait_recv()
     for copy in pending:
@@ -457,22 +504,22 @@
         in_specs=[pl.BlockSpec(memory_space=pltpu.VMEM)], out_specs=pl.BlockSpec(memory_space=pltpu.VMEM),
         out_shape=jax.ShapeDtypeStruct((1024,1024),F32),
         scratch_shapes=[pltpu.VMEM((512,1024),F32), pltpu.VMEM((512,1024),F32), pltpu.VMEM((2,64,1024),F32), pltpu.VMEM((2,128,1024),F32), pltpu.VMEM((3,32,1024),F32), pltpu.VMEM((3,8,1024),F32),
-            sem((3,8)), sem((3,8)), sem((2,3,6)), sem((2,3,6)), sem((2,3,3)), sem((2,3,3)), sem((2,3,3)), sem((2,3,3)), sem((3,8)), sem((3,8))],
+            sem((6,8)), sem((6,8)), sem((2,6,6)), sem((2,6,6)), sem((2,6,3)), sem((2,6,3)), sem((2,6,3)), sem((2,6,3)), sem((6,8)), sem((6,8))],
         compiler_params=pltpu.CompilerParams(collective_id=0, has_side_effects=True, vmem_limit_bytes=12*2**20),
         name="reduce_all")(x)
 
 
-def exchange_kernel(n_dev, *refs):
-    k = (len(refs) - 1) // 2
-    sems = refs[-1]
+def exchange_kernel(n_dev, rows, count, w_hbm, wt_t, labels, mask, rows_in, total, w_out, wt_out, tag_out, came, w_f32, w, wt, tag, sems, local):
     me = lax.axis_index("graph")
+    pairs = ((rows, rows_in), (count, came))
+    load = pltpu.make_async_copy(w_hbm, w_f32, local.at[0])
+    load.start()
 
     def send(t, carry):
         q = lax.rem(me + t, n_dev)
-        for j in range(k):
-            src, dst = refs[j], refs[k + j]
+        for j, (src, dst) in enumerate(pairs):
             pltpu.make_async_remote_copy(
-                src_ref=src.at[q if src.shape[0] == n_dev else 0],
+                src_ref=src.at[q if j == 0 else 0],
                 dst_ref=dst.at[me],
                 send_sem=sems.at[2 * j],
                 recv_sem=sems.at[2 * j + 1],
@@ -482,23 +529,58 @@
         return carry
 
     lax.fori_loop(1, n_dev, send, 0)
-    for j in range(k):
-        others = refs[k + j].at[pl.ds(0, n_dev - 1)]
+    load.wait()
+    w[...] = w_f32[...].astype(BF16)
+    stores = [pltpu.make_async_copy(src, dst, local.at[j]) for j, (src, dst) in enumerate(((w, w_out), (wt, wt_out), (tag, tag_out)), 1)]
+    stores[0].start()
+
+    def turn(i, carry):
+        at = pl.ds(pl.multiple_of(i * LANES, LANES), LANES)
+        wt[at, :] = wt_t[:, at].T
+        return carry
+
+    lax.fori_loop(0, wt.shape[0] // LANES, turn, 0)
+    stores[1].start()
+    tags = jnp.where(mask[...] == 1, labels[...], -1).astype(F32).T.astype(jnp.int32)
+    for j in range(tags.shape[1]):
+        tag[pl.ds(j * LANES, LANES), :] = tags[:, j : j + 1]
+    stores[2].start()
+    came[me] = count[0]
+    for j, (_, dst) in enumerate(pairs):
+        others = dst.at[pl.ds(0, n_dev - 1)]
         for side in range(2):
             pltpu.make_async_copy(others, others, sems.at[2 * j + side]).wait()
-
-
-def exchange(n_dev, *arrays):
-    vmem = pl.BlockSpec(memory_space=pltpu.VMEM)
+    total[...] = jnp.sum(came[...], axis=0)
+    for copy in stores:
+        copy.wait()
+
+
+def exchange(rows, count, w, wt_t, labels, mask):
+    n_dev, (deg, n) = rows.shape[0], wt_t.shape
+    vmem, hbm = pl.BlockSpec(memory_space=pltpu.VMEM), pl.BlockSpec(memory_space=pltpu.HBM)
     return pl.pallas_call(
         functools.partial(exchange_kernel, n_dev),
-        in_specs=[vmem] * len(arrays),
-        out_specs=[vmem] * len(arrays),
-        out_shape=[jax.ShapeDtypeStruct((n_dev,) + a.shape[1:], a.dtype) for a in arrays],
-        scratch_shapes=[pltpu.SemaphoreType.DMA((2 * len(arrays),))],
-        compiler_params=pltpu.CompilerParams(has_side_effects=True, vmem_limit_bytes=8 * 2**20),
+        in_specs=[vmem, vmem, hbm, vmem, vmem, vmem],
+        out_specs=[vmem, vmem, hbm, hbm, hbm],
+        out_shape=[
+            jax.ShapeDtypeStruct(rows.shape, rows.dtype),
+            jax.ShapeDtypeStruct((1, LANES), F32),
+            jax.ShapeDtypeStruct(w.shape, BF16),
+            jax.ShapeDtypeStruct((n, deg), F32),
+            jax.ShapeDtypeStruct((n, 1), jnp.int32),
+        ],
+        scratch_shapes=[
+            pltpu.VMEM((n_dev, 1, LANES), F32),
+            pltpu.VMEM(w.shape, F32),
+            pltpu.VMEM(w.shape, BF16),
+            pltpu.VMEM((n, deg), F32),
+            pltpu.VMEM((n, 1), jnp.int32),
+            pltpu.SemaphoreType.DMA((4,)),
+            pltpu.SemaphoreType.DMA((4,)),
+        ],
+        compiler_params=pltpu.CompilerParams(has_side_effects=True, vmem_limit_bytes=62 * 2**20),
         name="exchange_one",
-    )(*arrays)
+    )(rows, count, w, wt_t, labels.reshape(-1, LANES), mask.reshape(-1, LANES))
 
 
 def params():
@@ -524,28 +606,24 @@
         src8 = [edge_src[:, k] * 8 for k in range(deg)]
         src2 = [edge_src[:, k] * 2 for k in range(deg)]
         count = jnp.sum(label_mask.astype(F32))
-        label = jnp.where(label_mask == 1, labels, -1).reshape(n, 1)
-        first_in, counts = exchange(dev_count, feats[list_ids].reshape(dev_count, halo_rows, f_in), jnp.full((1, 1, LANES), count))
+        first_rows = feats[list_ids].reshape(dev_count, halo_rows, f_in)
+        first_in, label_total, w_one_b, wt, label = exchange(
+            first_rows, jnp.full((1, 1, LANES), count), w_one, edge_wt.T, labels, label_mask
+        )
         first_in = first_in.reshape(halo, f_in)
-        mine = jnp.arange(dev_count) == lax.axis_index("graph")
-        label_total = jnp.sum(jnp.where(mine, count, counts[:, 0, 0]))
-        inv_total = (1.0 / label_total).reshape(1)
-        wt, w_one_b = edge_wt, w_one.astype(BF16)
 
         def by_rows(width):
             return pl.BlockSpec((BLOCK, width), lambda g: (g, 0))
 
-        gather_scratch = [
-            pltpu.VMEM((ext * 8, LANES), F32),
-            pltpu.VMEM((BLOCK * 8, LANES), F32),
-            pltpu.VMEM((STEP * deg + 8, LANES), F32),
-        ]
+        def gather_scratch(rows):
+            return [pltpu.VMEM((ext * 8, LANES), F32), pltpu.VMEM((rows * 8, LANES), F32), pltpu.VMEM((STEP * deg + 8, LANES), F32)]
+
         whole = pl.BlockSpec(memory_space=pl.ANY)
         dma = pltpu.SemaphoreType.DMA
         index_scratch = [pltpu.SMEM((n,), jnp.int32) for _ in range(deg)]
 
         def chunk_scratch(width):
-            return [pltpu.VMEM((2, BLOCK, width), BF16), dma((deg,)), dma((2,))]
+            return [pltpu.VMEM((2, CHUNK, width), BF16), dma((deg,)), dma((2,))]
 
         second = pl.pallas_call(
             functools.partial(list_rows_kernel, deg),
@@ -553,7 +631,7 @@
             in_specs=[SMEM] + [whole] * (deg + 1) + [once((halo, f_in)), once((n, deg)), once((f_in, f_hid))],
             out_specs=once((halo * 8, LANES)),
             out_shape=jax.ShapeDtypeStruct((halo * 8, LANES), BF16),
-            scratch_shapes=gather_scratch + [pltpu.VMEM((halo, deg), F32)] + chunk_scratch(f_in) + index_scratch,
+            scratch_shapes=gather_scratch(halo) + [pltpu.VMEM((halo, deg), F32)] + chunk_scratch(f_in) + index_scratch,
             compiler_params=params(),
             cost_estimate=pl.CostEstimate(flops=4 * halo * f_in * f_hid, bytes_accessed=2 * n * f_in, transcendentals=0),
             name="list_rows",
@@ -565,7 +643,7 @@
             in_specs=[whole] * (deg + 1) + [once((halo, f_in)), by_rows(deg), once((f_in, f_hid))],
             out_specs=[by_rows(f_in), by_rows(f_hid)],
             out_shape=[jax.ShapeDtypeStruct((n, f_in), BF16), jax.ShapeDtypeStruct((n, f_hid), BF16)],
-            scratch_shapes=gather_scratch + chunk_scratch(f_in) + index_scratch,
+            scratch_shapes=gather_scratch(BLOCK) + chunk_scratch(f_in) + index_scratch,
             compiler_params=params(),
             cost_estimate=pl.CostEstimate(flops=8 * n * f_in * f_hid, bytes_accessed=8 * n * f_in, transcendentals=0),
             name="layer_one",
@@ -573,30 +651,30 @@
         grad_log, z_two, loss_part = pl.pallas_call(
             functools.partial(layer_two_kernel, classes, deg),
             grid=(n // BLOCK,),
-            in_specs=[SMEM] + [whole] * deg + [by_rows(deg), whole, once((halo * 8, LANES)), once((f_hid, pad)), by_rows(1)],
+            in_specs=[once((1, LANES))] + [whole] * deg + [by_rows(deg), whole, once((halo * 8, LANES)), once((f_hid, pad)), by_rows(1)],
             out_specs=[by_rows(pad), by_rows(f_hid), once((1, LANES))],
             out_shape=[
                 jax.ShapeDtypeStruct((n, pad), BF16),
                 jax.ShapeDtypeStruct((n, f_hid), BF16),
                 jax.ShapeDtypeStruct((1, LANES), F32),
             ],
-            scratch_shapes=gather_scratch + [pltpu.VMEM((1, pad), F32)] + chunk_scratch(f_hid) + index_scratch,
+            scratch_shapes=gather_scratch(BLOCK) + [pltpu.VMEM((1, pad), F32)] + chunk_scratch(f_hid) + index_scratch,
             compiler_params=params(),
             name="layer_two",
-        )(inv_total, *src8, wt, h_one, h_in, w_two_b, label)
-        ext_grad = pl.pallas_call(
+        )(label_total, *src8, wt, h_one, h_in, w_two_b, label)
+        own_grad, returned = pl.pallas_call(
             functools.partial(scatter_kernel, deg),
             grid=(n // 512,),
             in_specs=[whole] * deg + [by_rows(deg), by_rows(pad)],
-            out_specs=once((ext * 2, LANES)),
-            out_shape=jax.ShapeDtypeStruct((ext * 2, LANES), F32),
+            out_specs=[once((n * 2, LANES)), once((halo * 2, LANES))],
+            out_shape=[jax.ShapeDtypeStruct((n * 2, LANES), F32), jax.ShapeDtypeStruct((halo * 2, LANES), F32)],
             scratch_shapes=[pltpu.VMEM((BLOCK * 2, LANES), F32), pltpu.VMEM((STEP * deg + 8, LANES), F32), dma((deg,))]
             + index_scratch
             + [pltpu.VMEM((ext * 2, LANES), F32) for _ in range(deg)],
             compiler_params=params(),
             name="scatter",
         )(*src2, wt, grad_log)
-        returned, grad_log = lax.optimization_barrier((ext_grad[n * 2 :], grad_log))
+        returned, grad_log = lax.optimization_barrier((returned, grad_log))
         back = lax.all_to_all(returned, "graph", 0, 0, tiled=True)
         gw_two = pl.pallas_call(
             grad_two_kernel,
@@ -622,13 +700,13 @@
                 pltpu.VMEM((n, f_hid), BF16),
                 pltpu.VMEM((n, f_in), BF16),
                 dma,
-                dma((2, n // BLOCK)),
+                dma((2, n // CHUNK)),
             ],
             compiler_params=pltpu.CompilerParams(vmem_limit_bytes=44 * 2**20),
             name="backward",
-        )(lists2, ext_grad, back, w_parts, gw_two, h_one, z_one)
+        )(lists2, own_grad, back, w_parts, gw_two, h_one, z_one)
         total = reduce_all(partial)
-        return -total[f_in + pad - 1, 0] / label_total, total[:f_in], total[f_in : f_in + classes].T
+        return -total[f_in + pad - 1, 0] / label_total[0, 0], total[:f_in], total[f_in : f_in + classes].T
 
     row_spec = P("graph", None)
     vec_spec = P("graph")

time: 309 us -> 301 us (0.974)
  other arithmetic: 7.78 us -> 3.12 us
  local copies, waits for them, and re-layouts: 25.8 us -> 21.5 us
  Pallas kernels: 247 us -> 251 us
    pallas_call x1, Pallas kernels: 27.6 us -> 31 us  [exchange(): pl.pallas_call(functools.partial(exchange_kernel, n_dev), in_specs=[vmem,...]
    convert_element_type x1 -> x0, other arithmetic: 3.35 us -> none  [device_step(): wt, w_one_b = (edge_wt, w_one.astype(BF16))]
    unnamed x25 -> x22, local copies, waits for them, and re-layouts: 8 us -> 6.07 us
  transfers between devices with their start and end apart: 2 -> 2, of which waited for: 1 -> 1; matrix products, arithmetic and copies ran while one was open for 2% -> 0% of each run, Pallas kernels for 17% -> 17%
where the time goes in v6:
time: 301 us; the launch traced here: 300 us
  Pallas kernels  251 us (83%)
  local copies, waits for them, and re-layouts  21.5 us (7%)
  starting transfers between devices  17.7 us (6%)
  waiting for transfers between devices  4.57 us (2%)
  other arithmetic  3.12 us (1%)
    pallas_call x1, Pallas kernels, device_step(): pl.pallas_call(functools.partial(layer_one_kernel, deg), grid=(n // BLOCK...  47.5 us
    pallas_call x1, Pallas kernels, device_step(): pl.pallas_call(functools.partial(layer_two_kernel, classes, deg), grid=(n...  46.9 us
    pallas_call x1, Pallas kernels, device_step(): pl.pallas_call(functools.partial(scatter_kernel, deg), grid=(n // 512,),...  45.2 us
    pallas_call x1, Pallas kernels, reduce_all(): pl.pallas_call(reduce_kernel, in_specs=[pl.BlockSpec(memory_space=pltpu.V...  41.6 us
    pallas_call x1, Pallas kernels, exchange(): pl.pallas_call(functools.partial(exchange_kernel, n_dev), in_specs=[vmem,...  31 us
    pallas_call x1, Pallas kernels, device_step(): pl.pallas_call(backward_kernel, in_specs=[SMEM, whole, vmem, vmem, vmem,...  19 us
    pallas_call x1, Pallas kernels, device_step(): pl.pallas_call(functools.partial(list_rows_kernel, deg), grid=(1,), in_sp...  15.7 us
    all_to_all x1, starting transfers between devices, device_step(): back = lax.all_to_all(returned, 'graph', 0, 0, tiled=True)  9.75 us
  transfers between devices with their start and end apart: 2, of which 1 were waited for; matrix products, arithmetic and copies ran while one was open for 0% of the time, Pallas kernels for 17%

profile of v6, /device:TPU:1, one launch (start us, length us, event | category | flops | bytes accessed | tf_op | source)
XLA Modules:
  0.0 300.3 jit_solution(460648036024524335)
XLA Ops:
  0.6 0.8 copy.12
  1.5 0.7 reshape.89.lists
  2.2 2.4 slice_multiply_fusion
  4.7 6.0 %gather_fusion = bf16[512,768]{1,0:T(8,128)(2,1)S(1)} fusion(bf16[4096,768]{1,0:T(8,128)(2,1)} %refs_8_.3, s32[1024]{0:T(1024)S(1)} %pad_clamp_fusion), kind=kCustom, calls=%fused_computation | custom fusion | bytes 1574912 | tf_op jit(solution)/shard_map/gather | solution.py:609
  10.7 1.1 reshape.91.rows
  11.7 0.6 convert_reduce_fusion
  12.3 1.2 broadcast_in_dim.7.count
  13.5 31.0 %exchange_one.1 = (bf16[128,4,768]{2,1,0:T(4,128)(2,1)}, f32[1,128]{1,0:T(1,128)}, bf16[768,1024]{1,0:T(8,128)(2,1)}, f32[4096,8]{1,0:T(8,128)}, s32[4096,1]{1,0:T(8,128)}) custom-call(bf16[128,4,768]{2,1,0:T(4,128)(2,1)} %reshape.91.rows, f32[1,1,128]{2,1,0:T(1,128)} %broadcast_in_dim.7.count, f32[768,1024]{1,0:T(8,128)} %w_hbm.1, f32[8,4096]{1,0:T(8,128)} %bitcast.57, ...), custom_call_target="tpu_custom_call" | custom-call | tf_op jit(solution)/shard_map/exchange_one/pallas_call | solution.py:561
  44.4 2.3 reshape.94.refs_9_
  46.7 15.7 %list_rows.1 = bf16[4096,128]{1,0:T(8,128)(2,1)} custom-call(s32[512]{0:T(512)} %reshape.89.lists, s32[4096]{0:T(1024)} %bitcast.36, s32[4096]{0:T(1024)} %bitcast.39, s32[4096]{0:T(1024)} %bitcast.42, s32[4096]{0:T(1024)} %bitcast.45, s32[4096]{0:T(1024)} %bitcast.48, s32[4096]{0:T(1024)} %bitcast.51, s32[4096]{0:T(1024)} %bitcast.54, s32[4096]{0:T(1024)} %bitcast.33, ...), custom_call_target="tpu_custom_call" | custom-call | flops 1610612736 | bytes 6291456 | tf_op jit(solution)/shard_map/list_rows/pallas_call | solution.py:628
  62.4 7.9 %all-to-all-start = ((bf16[128,32,128]{2,1,0:T(8,128)(2,1)}), bf16[128,32,128]{2,1,0:T(8,128)(2,1)}, u32[]{:S(2)}, u32[]{:S(2)}) async-start(bf16[128,32,128]{2,1,0:T(8,128)(2,1)} %bitcast.31), calls=%async_computation | async-start | bytes 2097152 | tf_op jit(solution)/shard_map/all_to_all | solution.py:639
  70.4 47.5 %layer_one.1 = (bf16[4096,768]{1,0:T(8,128)(2,1)}, bf16[4096,1024]{1,0:T(8,128)(2,1)}) custom-call(s32[4096]{0:T(1024)} %bitcast.37, s32[4096]{0:T(1024)} %bitcast.40, s32[4096]{0:T(1024)} %bitcast.43, s32[4096]{0:T(1024)} %bitcast.46, s32[4096]{0:T(1024)} %bitcast.49, s32[4096]{0:T(1024)} %bitcast.52, s32[4096]{0:T(1024)} %bitcast.55, s32[4096]{0:T(1024)} %bitcast.34, ...), custom_call_target="tpu_custom_call" | custom-call | flops 25769803776 | bytes 25165824 | tf_op jit(solution)/shard_map/layer_one/pallas_call | solution.py:640
  118.2 0.9 pad.8.clone.refs_11_
  119.3 46.9 %layer_two.1 = (bf16[4096,256]{1,0:T(8,128)(2,1)}, bf16[4096,1024]{1,0:T(8,128)(2,1)}, f32[1,128]{1,0:T(1,128)}) custom-call(f32[1,128]{1,0:T(1,128)} %get-tuple-element.18.label_total, s32[4096]{0:T(1024)} %bitcast.38, s32[4096]{0:T(1024)} %bitcast.41, s32[4096]{0:T(1024)} %bitcast.44, s32[4096]{0:T(1024)} %bitcast.47, s32[4096]{0:T(1024)} %bitcast.50, ...), custom_call_target="tpu_custom_call" | custom-call | tf_op jit(solution)/shard_map/layer_two/pallas_call | solution.py:651
  166.1 45.2 %scatter.1 = (f32[8192,128]{1,0:T(8,128)}, f32[1024,128]{1,0:T(8,128)}) custom-call(s32[4096]{0:T(1024)} %bitcast.63, s32[4096]{0:T(1024)} %bitcast.62, s32[4096]{0:T(1024)} %bitcast.61, s32[4096]{0:T(1024)} %bitcast.60, s32[4096]{0:T(1024)} %bitcast.59, s32[4096]{0:T(1024)} %bitcast.58, s32[4096]{0:T(1024)} %bitcast.65, s32[4096]{0:T(1024)} %bitcast.64, ...), custom_call_target="tpu_custom_call" | custom-call | tf_op jit(solution)/shard_map/scatter/pallas_call | solution.py:665
  211.4 9.7 %all-to-all-start.1 = ((f32[128,8,128]{2,1,0:T(8,128)}), f32[128,8,128]{2,1,0:T(8,128)S(1)}, u32[]{:S(2)}, u32[]{:S(2)}) async-start(f32[128,8,128]{2,1,0:T(8,128)} %bitcast.32), calls=%async_computation.1 | async-start | bytes 1048576 | tf_op jit(solution)/shard_map/all_to_all | solution.py:678
  221.2 3.4 %copy-done = bf16[4096,1024]{1,0:T(8,128)(2,1)S(1)} copy-done((bf16[4096,1024]{1,0:T(8,128)(2,1)S(1)}, bf16[4096,1024]{1,0:T(8,128)(2,1)}, u32[]{:S(2)}) %copy-start) | copy-done | bytes 8388632
  224.6 1.6 copy-done.1
  226.1 3.8 %grad_two.1.gw_two = f32[256,1024]{1,0:T(8,128)S(1)} custom-call(bf16[4096,256]{1,0:T(8,128)(2,1)S(1)} %copy-done.1, bf16[4096,1024]{1,0:T(8,128)(2,1)S(1)} %copy-done, f32[1,128]{1,0:T(1,128)S(1)} %copy-done.2), custom_call_target="tpu_custom_call" | custom-call | flops 2147483648 | bytes 8388608 | tf_op jit(solution)/shard_map/grad_two/pallas_call | solution.py:679
  230.0 4.6 %all-to-all-done.1 = f32[128,8,128]{2,1,0:T(8,128)S(1)} async-done(((f32[128,8,128]{2,1,0:T(8,128)}), f32[128,8,128]{2,1,0:T(8,128)S(1)}, u32[]{:S(2)}, u32[]{:S(2)}) %all-to-all-start.1) | async-done | bytes 524320 | tf_op jit(solution)/shard_map/all_to_all | solution.py:678
  234.5 19.0 %backward.1.x = f32[1024,1024]{1,0:T(8,128)S(1)} custom-call(s32[512]{0:T(512)S(1)} %broadcast_multiply_fusion.lists, f32[8192,128]{1,0:T(8,128)} %get-tuple-element.24.own, f32[1024,128]{1,0:T(8,128)S(1)} %bitcast.30, bf16[512,1024]{1,0:T(8,128)(2,1)S(1)} %broadcast_dynamic-update-slice_fusion.w_t, f32[256,1024]{1,0:T(8,128)S(1)} %grad_two.1.gw_two, ...), custom_call_target="tpu_custom_call" | custom-call | tf_op jit(solution)/shard_map/backward/pallas_call | solution.py:693
  253.5 41.6 %reduce_all.1 = f32[1024,1024]{1,0:T(8,128)S(1)} custom-call(f32[1024,1024]{1,0:T(8,128)S(1)} %backward.1.x), custom_call_target="tpu_custom_call" | custom-call | tf_op jit(solution)/shard_map/reduce_all/pallas_call | solution.py:503
  295.1 1.9 slice.62
  297.0 0.9 slice_bitcast_fusion
  (29 shorter events, 1.0 us)
Async XLA Ops:
  4.6 7.1 %copy-start.4 = (s32[4096]{0:T(1024)S(1)}, s32[4096]{0:T(1024)}, u32[]{:S(2)}) copy-start(s32[4096]{0:T(1024)} %param.16) | copy-start | bytes 49156
  62.4 56.8 %all-to-all-start = ((bf16[128,32,128]{2,1,0:T(8,128)(2,1)}), bf16[128,32,128]{2,1,0:T(8,128)(2,1)}, u32[]{:S(2)}, u32[]{:S(2)}) async-start(bf16[128,32,128]{2,1,0:T(8,128)(2,1)} %bitcast.31), calls=%async_computation | async-start | bytes 2097152 | tf_op jit(solution)/shard_map/all_to_all | solution.py:639
  70.4 47.5 %copy-start.3 = (f32[1024,153]{0,1:T(8,128)S(1)}, f32[1024,153]{0,1:T(8,128)}, u32[]{:S(2)}) copy-start(f32[1024,153]{0,1:T(8,128)} %param.11) | copy-start | bytes 1880068
  166.1 55.0 %copy-start.5 = (s32[512]{0:T(512)S(1)}, s32[512]{0:T(512)}, u32[]{:S(2)}) copy-start(s32[512]{0:T(512)} %reshape.89.lists) | copy-start | bytes 6148
  166.1 55.0 %copy-start.2 = (f32[1,128]{1,0:T(1,128)S(1)}, f32[1,128]{1,0:T(1,128)}, u32[]{:S(2)}) copy-start(f32[1,128]{1,0:T(1,128)} %get-tuple-element.29.loss) | copy-start | bytes 1540
  211.4 23.2 %all-to-all-start.1 = ((f32[128,8,128]{2,1,0:T(8,128)}), f32[128,8,128]{2,1,0:T(8,128)S(1)}, u32[]{:S(2)}, u32[]{:S(2)}) async-start(f32[128,8,128]{2,1,0:T(8,128)} %bitcast.32), calls=%async_computation.1 | async-start | bytes 1048576 | tf_op jit(solution)/shard_map/all_to_all | solution.py:678
  221.2 3.4 %copy-start = (bf16[4096,1024]{1,0:T(8,128)(2,1)S(1)}, bf16[4096,1024]{1,0:T(8,128)(2,1)}, u32[]{:S(2)}) copy-start(bf16[4096,1024]{1,0:T(8,128)(2,1)} %get-tuple-element.28.z) | copy-start | bytes 25165828
  224.6 1.6 copy-start.1
  295.1 3.9 %copy-start.6 = (f32[1,128]{1,0:T(1,128)S(1)}, f32[1,128]{1,0:T(1,128)}, u32[]{:S(2)}) copy-start(f32[1,128]{1,0:T(1,128)} %get-tuple-element.18.label_total) | copy-start | bytes 1540
